TPU v7x, 256 devices: a whole 4x4x8 slice. The times are simulated.
256 devices in a mesh: sx: 8 (over y, core), sy: 8 (over z), af: 4 (over x).
Axes of the slice: x: 4, y: 4, z: 8, core: 2. Of those that a mesh axis runs over, the one named last changes fastest.
Arguments:
- sky_maps: float32 [256, 256, 1024], P('sx', 'sy', 'af'), may hold values from -16 to 25
- validity: int32 [256, 256], P('sx', 'sy'), may hold values 0 or 1
- row_taps: float32 [1024, 65], P('af'), may hold values from -0.75 to 0.75
- column_taps: float32 [1024, 65], P('af'), may hold values from -0.75 to 0.75
- init_loadings: float32 [1024, 32], P('af'), may hold values from -0.1875 to 0.1875
Outputs:
- cleaned_maps: float32 [256, 256, 1024], P('sx', 'sy', 'af')
- loadings: float32 [1024, 32], P('af')
- noise_var: float32 [], replicated
All inputs are finite; a program needn't handle non-finite values. No bound on the sum of `validity` on one device may be relied on, other than what follows from the above.
Results may differ from a plain program's by a relative error of at most 0.0003.
Values sent between devices are 32-bit elements; how exact they have to be, the bound alone decides.
No kernel may reach another device: no remote copies, remote signals or barrier semaphores. Data moves between devices by JAX's collectives and lax.ppermute only.
A program may use at most 128 MiB of HBM per device.

v0:
```python
import math

import jax
import jax.numpy as jnp
from jax import lax
from jax.sharding import PartitionSpec as P

ITERS = 4


HIGHEST_PRECISION = lax.Precision.HIGHEST


def padded(block, sides, width):
    for axis, dim in sides:
        count = lax.axis_size(axis)
        forward = [(i, i + 1) for i in range(count - 1)]
        backward = [(target, source) for source, target in forward]
        low = lax.ppermute(
            lax.slice_in_dim(block, block.shape[dim] - width, None, axis=dim), axis, forward
        )
        high = lax.ppermute(lax.slice_in_dim(block, 0, width, axis=dim), axis, backward)
        block = jnp.concatenate([low, block, high], axis=dim)
    return block


def inverse_spd(matrix):
    identity = jnp.eye(matrix.shape[0], dtype=matrix.dtype)
    factor = jnp.linalg.cholesky(matrix)
    lower_inverse = lax.linalg.triangular_solve(factor, identity, left_side=True, lower=True)
    return jnp.dot(lower_inverse.T, lower_inverse, precision=HIGHEST_PRECISION)


def contract_rows(left_rows, right_rows):
    return lax.dot_general(
        left_rows, right_rows, (((0,), (0,)), ((), ())), precision=HIGHEST_PRECISION
    )


def correlate(extended, tap_table, out_length, along_dim):
    freq_count, tap_count = tap_table.shape
    block_size = math.gcd(freq_count, 32)
    in_length = extended.shape[along_dim]
    offsets = jnp.arange(in_length)[:, None] - jnp.arange(out_length)[None, :]
    one_hot = (offsets[None, :, :] == jnp.arange(tap_count)[:, None, None]).astype(jnp.float32)
    shape_out = list(extended.shape)
    shape_out[along_dim] = out_length
    filtered_all = jnp.zeros(tuple(shape_out), jnp.float32)

    def add_block(block_index, filtered_all):
        first_freq = block_index * block_size
        slab_part = lax.dynamic_slice_in_dim(extended, first_freq, block_size, 2)
        tap_block = lax.dynamic_slice_in_dim(tap_table, first_freq, block_size, 0)
        band_matrix = jnp.einsum("ft,tio->fio", tap_block, one_hot, precision=HIGHEST_PRECISION)
        if along_dim == 0:
            filtered = jnp.einsum(
                "icf,fio->ocf", slab_part, band_matrix, precision=HIGHEST_PRECISION
            )
        else:
            filtered = jnp.einsum(
                "rif,fio->rof", slab_part, band_matrix, precision=HIGHEST_PRECISION
            )
        return lax.dynamic_update_slice_in_dim(filtered_all, filtered, first_freq, 2)

    return lax.fori_loop(0, freq_count // block_size, add_block, filtered_all)


def body(sky_maps, validity, row_taps, column_taps, init_loadings):
    rows_here, cols_here, freqs_here = sky_maps.shape
    halo_width = (row_taps.shape[1] - 1) // 2
    masked = sky_maps * validity.astype(jnp.float32)[:, :, None]
    extended = padded(masked, (("sx", 0), ("sy", 1)), halo_width)
    smoothed = correlate(extended, row_taps, rows_here, 0)
    beamed = correlate(smoothed, column_taps, cols_here, 1)
    spectra = beamed.reshape(rows_here * cols_here, freqs_here)
    total_power = lax.psum(jnp.sum(spectra * spectra), ("sx", "sy", "af"))
    pixel_count = rows_here * cols_here * lax.axis_size("sx") * lax.axis_size("sy")
    freq_total = freqs_here * lax.axis_size("af")
    components = init_loadings.shape[1]
    identity = jnp.eye(components, dtype=jnp.float32)
    noise_var = jnp.float32(1.0)
    loadings = lax.all_gather(init_loadings, "af", axis=0, tiled=True)
    pixel_rows = lax.all_to_all(spectra, "af", split_axis=0, concat_axis=1, tiled=True)
    for iteration in range(ITERS):
        inverse = inverse_spd(contract_rows(loadings, loadings) + noise_var * identity)
        latent = jnp.dot(
            pixel_rows,
            jnp.dot(loadings, inverse, precision=HIGHEST_PRECISION),
            precision=HIGHEST_PRECISION,
        )
        cross_moment, second = lax.psum(
            (contract_rows(pixel_rows, latent), contract_rows(latent, latent)), ("sx", "sy", "af")
        )
        scaled = pixel_count * noise_var * inverse + second
        updated = jnp.dot(cross_moment, inverse_spd(scaled), precision=HIGHEST_PRECISION)
        new_gram = contract_rows(updated, updated)
        noise_var = (
            total_power - 2.0 * jnp.sum(updated * cross_moment) + jnp.sum(scaled * new_gram)
        ) / (pixel_count * freq_total)
        loadings = updated
    inverse = inverse_spd(contract_rows(loadings, loadings) + noise_var * identity)
    latent = jnp.dot(
        pixel_rows,
        jnp.dot(loadings, inverse, precision=HIGHEST_PRECISION),
        precision=HIGHEST_PRECISION,
    )
    cleaned_rows = pixel_rows - jnp.dot(latent, loadings.T, precision=HIGHEST_PRECISION)
    cleaned = lax.all_to_all(cleaned_rows, "af", split_axis=1, concat_axis=0, tiled=True)
    loadings_block = lax.dynamic_slice_in_dim(
        loadings, lax.axis_index("af") * freqs_here, freqs_here, 0
    )
    return (cleaned.reshape(rows_here, cols_here, freqs_here), loadings_block, noise_var)


def solution(mesh):
    placed = (P("sx", "sy", "af"), P("sx", "sy"), P("af", None), P("af", None), P("af", None))
    return jax.shard_map(
        body,
        mesh=mesh,
        in_specs=placed,
        out_specs=(P("sx", "sy", "af"), P("af", None), P()),
        check_vma=False,
    )
```

profile of v0, /device:TPU:32, one launch (start us, length us, event | category | flops | bytes accessed | tf_op | source)
XLA Modules:
  0.0 1608.8 jit_solution(8080160736587513446)
XLA Ops:
  19.1 3.8 collective-permute-start.2
  22.9 3.7 collective-permute-start.3
  26.8 12.6 all_gather.3
  47.2 3.8 custom-call.13
  51.0 29.7 %collective-permute-done.2 = f32[96,32,256]{2,1,0:T(8,128)} collective-permute-done((f32[96,32,256]{2,1,0:T(8,128)}, f32[96,32,256]{2,1,0:T(8,128)}, u32[]{:S(2)}, u32[]{:S(2)}) %collective-permute-start.2) | collective-permute-done | bytes 3145760 | tf_op jit(solution)/shard_map/ppermute | solution.py:19
  80.7 3.9 collective-permute-done.3
  84.7 5.9 pad_maximum_fusion
  90.6 11.6 copy.69
  104.7 38.0 %while.28 = (s32[]{:T(128)}, f32[32,96,256]{1,0,2:T(8,128)}, f32[256,65]{1,0:T(8,128)S(1)}, f32[96,96,256]{1,0,2:T(8,128)}, s32[96,32]{0,1:T(8,128)S(1)}, /*index=5*/s32[]{:T(128)}, s32[]{:T(128)}, s32[]{:T(128)}, s32[]{:T(128)}) while((s32[]{:T(128)}, f32[32,96,256]{1,0,2:T(8,128)}, f32[256,65]{1,0:T(8,128)S(1)}, ...), condition=%wide.region_1.0_spmd.clone, body=%wide.region_0.0_spmd.clone.sunk | while | flops 190322688 | bytes 2917519 | solution.py:65
  105.5 4.0 fusion.193
  110.2 4.0 fusion.193
  115.0 3.9 fusion.193
  119.7 3.9 fusion.193
  124.5 3.9 fusion.193
  129.2 3.9 fusion.193
  134.0 3.9 fusion.193
  138.7 3.9 fusion.193
  145.1 31.1 %while.29 = (s32[]{:T(128)}, f32[32,32,256]{0,1,2:T(8,128)}, f32[256,65]{1,0:T(8,128)S(1)}, f32[32,96,256]{1,0,2:T(8,128)}, s32[96,32]{0,1:T(8,128)S(1)}, /*index=5*/s32[]{:T(128)}, s32[]{:T(128)}, s32[]{:T(128)}, s32[]{:T(128)}) while((s32[]{:T(128)}, f32[32,32,256]{0,1,2:T(8,128)}, f32[256,65]{1,0:T(8,128)S(1)}, ...), condition=%wide.region_3.0_spmd.clone, body=%wide.region_2.0_spmd.clone.sunk | while | flops 114825224 | bytes 1868943 | solution.py:65
  176.2 4.7 copy.71
  180.9 4.3 all-to-all-start
  186.0 3.9 multiply_reduce_fusion
  189.9 6.2 all-to-all-done
  198.8 102.3 %all-reduce = (f32[32,32]{0,1:T(8,128)S(1)}, f32[]{:T(128)}) all-reduce(f32[32,32]{0,1:T(8,128)S(1)} %fusion.79, f32[]{:T(128)} %multiply_reduce_fusion), channel_id=1, replica_groups=mesh['sx'=8,'sy'=8,'af'=4] {'sx','sy','af'}, use_global_device_ids=true, to_apply=%region_7.10 | all-reduce | flops 1025 | bytes 8200 | tf_op jit(solution)/shard_map/psum | solution.py:91
  308.4 241.5 %all-reduce.6.cloned.1.call-done = f32[1024,32]{0,1:T(8,128)} async-done(((f32[1024,32]{0,1:T(8,128)}), f32[1024,32]{0,1:T(8,128)}) %all-reduce.6.cloned.1.call-update) | async-done | bytes 131088 | tf_op jit(solution)/shard_map/psum | solution.py:91
  564.8 75.9 %psum.67 = f32[32,32]{0,1:T(8,128)S(1)} all-reduce(f32[32,32]{0,1:T(8,128)S(1)} %fusion.85), channel_id=1, replica_groups=mesh['sx'=8,'sy'=8,'af'=4] {'sx','sy','af'}, use_global_device_ids=true, to_apply=%region_13.16 | all-reduce | flops 1024 | bytes 8192 | tf_op jit(solution)/shard_map/psum | solution.py:91
  648.0 240.3 %all-reduce.8.cloned.1.call-done = f32[1024,32]{0,1:T(8,128)} async-done(((f32[1024,32]{0,1:T(8,128)}), f32[1024,32]{0,1:T(8,128)}) %all-reduce.8.cloned.1.call-update) | async-done | bytes 131088 | tf_op jit(solution)/shard_map/psum | solution.py:91
  903.2 75.9 %psum.69 = f32[32,32]{0,1:T(8,128)S(1)} all-reduce(f32[32,32]{0,1:T(8,128)S(1)} %fusion.91), channel_id=1, replica_groups=mesh['sx'=8,'sy'=8,'af'=4] {'sx','sy','af'}, use_global_device_ids=true, to_apply=%region_17.20 | all-reduce | flops 1024 | bytes 8192 | tf_op jit(solution)/shard_map/psum | solution.py:91
  986.6 240.1 %all-reduce.10.cloned.1.call-done = f32[1024,32]{0,1:T(8,128)} async-done(((f32[1024,32]{0,1:T(8,128)}), f32[1024,32]{0,1:T(8,128)}) %all-reduce.10.cloned.1.call-update) | async-done | bytes 131088 | tf_op jit(solution)/shard_map/psum | solution.py:91
  1241.6 75.9 %psum.71 = f32[32,32]{0,1:T(8,128)S(1)} all-reduce(f32[32,32]{0,1:T(8,128)S(1)} %fusion.97), channel_id=1, replica_groups=mesh['sx'=8,'sy'=8,'af'=4] {'sx','sy','af'}, use_global_device_ids=true, to_apply=%region_21.24 | all-reduce | flops 1024 | bytes 8192 | tf_op jit(solution)/shard_map/psum | solution.py:91
  1324.8 240.3 %all-reduce.12.cloned.1.call-done = f32[1024,32]{0,1:T(8,128)} async-done(((f32[1024,32]{0,1:T(8,128)}), f32[1024,32]{0,1:T(8,128)}) %all-reduce.12.cloned.1.call-update) | async-done | bytes 131088 | tf_op jit(solution)/shard_map/psum | solution.py:91
  1580.5 4.0 all-to-all-start.1
  1585.1 15.1 all-to-all-done.1
  (174 shorter events, 148.8 us)
Async XLA Ops:
  7.9 18.7 %copy-start = (f32[256,65]{0,1:T(8,128)S(1)}, f32[256,65]{0,1:T(8,128)}, u32[]{:S(2)}) copy-start(f32[256,65]{0,1:T(8,128)} %param.14) | copy-start | bytes 199684
  7.9 18.8 %copy-start.1 = (f32[256,65]{0,1:T(8,128)S(1)}, f32[256,65]{0,1:T(8,128)}, u32[]{:S(2)}) copy-start(f32[256,65]{0,1:T(8,128)} %param.15) | copy-start | bytes 199684
  9.4 4.0 collective-permute-start
  11.2 5.9 collective-permute-start.1
  19.1 61.7 %collective-permute-start.2 = (f32[96,32,256]{2,1,0:T(8,128)}, f32[96,32,256]{2,1,0:T(8,128)}, u32[]{:S(2)}, u32[]{:S(2)}) collective-permute-start(f32[96,32,256]{2,1,0:T(8,128)} %pad_maximum_fusion.1), channel_id=1, source_target_pairs={{0,4},{4,8},{8,12},{12,16},{16,20},{20,24},{24,28},{1,5},{5,9},{9,... | collective-permute-start | bytes 9437192 | tf_op jit(solution)/shard_map/ppermute | solution.py:19
  22.9 61.8 %collective-permute-start.3 = (f32[96,32,256]{2,1,0:T(8,128)}, f32[96,32,256]{2,1,0:T(8,128)}, u32[]{:S(2)}, u32[]{:S(2)}) collective-permute-start(f32[96,32,256]{2,1,0:T(8,128)} %pad_maximum_fusion.1), channel_id=1, source_target_pairs={{4,0},{8,4},{12,8},{16,12},{20,16},{24,20},{28,24},{5,1},{9,5},{13... | collective-permute-start | bytes 9437192 | tf_op jit(solution)/shard_map/ppermute | solution.py:22
  176.2 9.0 copy-start.2
  180.9 15.2 all-to-all-start
  185.2 364.7 %all-reduce.6.cloned.1.call-start = ((), (), s32[]{:S(2)}) async-start(), calls=%async_computation.2 | async-start | bytes 262144 | tf_op jit(solution)/shard_map/psum | solution.py:91
  308.1 580.1 %all-reduce.8.cloned.1.call-start = ((), (), s32[]{:S(2)}) async-start(), calls=%async_computation.3 | async-start | bytes 262144 | tf_op jit(solution)/shard_map/psum | solution.py:91
  647.7 579.0 %all-reduce.10.cloned.1.call-start = ((), (), s32[]{:S(2)}) async-start(), calls=%async_computation.4 | async-start | bytes 262144 | tf_op jit(solution)/shard_map/psum | solution.py:91
  986.1 579.0 %all-reduce.12.cloned.1.call-start = ((), (), s32[]{:S(2)}) async-start(), calls=%async_computation.5 | async-start | bytes 262144 | tf_op jit(solution)/shard_map/psum | solution.py:91
  1580.5 19.7 %all-to-all-start.1 = ((f32[256,4,256]{2,0,1:T(8,128)}), f32[256,4,256]{2,0,1:T(8,128)S(1)}, u32[]{:S(2)}, u32[]{:S(2)}) async-start(f32[256,4,256]{2,0,1:T(8,128)} %bitcast.179), calls=%async_computation.1 | async-start | bytes 2097152 | tf_op jit(solution)/shard_map/all_to_all | solution.py:108
Sparse Core Ops, SparseCore 0:
  308.2 241.6 all-reduce.5
  647.8 240.3 all-reduce.7
  986.2 240.4 all-reduce.9
  1324.7 240.3 all-reduce.11
where the time goes:
time: 1610 us
  waiting for transfers between devices  1020 us (63%)
  blocking collectives  342 us (21%)
  matrix products  98 us (6%)
  other arithmetic  78.2 us (5%)
  local copies, waits for them, and re-layouts  25.8 us (2%)
  between operations  23.1 us (1%)
  starting transfers between devices  19.2 us (1%)
    psum x4, waiting for transfers between devices, body(): lax.psum((contract_rows(pixel_rows, latent), contract_rows(latent, latent...  962 us
    psum x4, blocking collectives, body(): lax.psum((contract_rows(pixel_rows, latent), contract_rows(latent, latent...  330 us
    another operation x27, other arithmetic, inverse_spd(): factor = jnp.linalg.cholesky(matrix)  33.1 us
  transfers between devices with their start and end apart: 10, of which 10 were waited for; matrix products, arithmetic and copies ran while one was open for 1% of the time, Pallas kernels for 0%

commit v1 on v0

v1 whole, which is shorter than its diff:
```python
import functools

import jax
import jax.numpy as jnp
from jax import lax
from jax.experimental import pallas as pl
from jax.experimental.pallas import tpu as pltpu
from jax.sharding import PartitionSpec as P

ITERS = 4
HI = lax.Precision.HIGHEST
VM = pltpu.VMEM
INTERPRET = False


def call(kernel, **kw):
    return pl.pallas_call(kernel, interpret=INTERPRET, **kw)


def contract(left, right, dims):
    return lax.dot_general(
        left, right, (dims, ((), ())), precision=HI, preferred_element_type=jnp.float32
    )


def beam_kernel(low, own, high, taps, out):
    length = own.shape[0]
    count = taps.shape[0]
    refs = (low, own, high)
    for block in range(length // 8):
        acc = [None] * 8
        held = {}
        for k in range(count + 7):
            row = block * 8 + k
            value = refs[row // length][row % length]
            if k < count:
                held[k] = taps[k]
            for j in range(8):
                t = k - j
                if 0 <= t < count:
                    term = held[t] * value
                    acc[j] = term if acc[j] is None else acc[j] + term
        out[:, block * 8 : block * 8 + 8, :] = jnp.swapaxes(jnp.stack(acc), 0, 1)


def beam(low, own, high, taps):
    a, b, f = own.shape
    assert taps.shape[0] == 2 * a + 1
    spec = pl.BlockSpec((a, 8, f), lambda j: (0, j, 0))
    return call(
        beam_kernel,
        grid=(b // 8,),
        in_specs=[spec, spec, spec, pl.BlockSpec(taps.shape, lambda j: (0, 0, 0))],
        out_specs=pl.BlockSpec((8, a, f), lambda j: (j, 0, 0)),
        out_shape=jax.ShapeDtypeStruct((b, a, f), jnp.float32),
        name="beam",
    )(low, own, high, taps)


def row_block(place, c, k, parts):
    return lax.rem(place[0] + c, 2) * parts + lax.rem(place[1] + k, parts)


def moment_kernel(place, even, odd, out):
    parts = even.shape[0]
    blocks = 2 * parts
    c, k = pl.program_id(0), pl.program_id(1)
    i = row_block(place, c, k, parts)

    def column(b):
        half = lax.div(b, 2)
        return jnp.where(lax.rem(b, 2) == 0, even[half], odd[half])

    cols = [column(lax.rem(i + j, blocks)) for j in range(parts + 1)]
    out[0, 0] = contract(cols[0], jnp.concatenate(cols, axis=1), ((0,), (0,)))


def moments(place, even, odd):
    parts, pixels, width = even.shape
    full = pl.BlockSpec(even.shape, lambda c, k, place: (0, 0, 0))
    return call(
        moment_kernel,
        grid_spec=pltpu.PrefetchScalarGridSpec(
            num_scalar_prefetch=1,
            grid=(2, parts),
            in_specs=[full, full],
            out_specs=pl.BlockSpec(
                (1, 1, width, width * (parts + 1)), lambda c, k, place: (c, k, 0, 0)
            ),
        ),
        out_shape=jax.ShapeDtypeStruct((2, parts, width, width * (parts + 1)), jnp.float32),
        name="moments",
    )(place, even, odd)


def inverse_spd(matrix):
    n = matrix.shape[0]
    rows = lax.broadcasted_iota(jnp.int32, (n, n), 0)
    lanes = lax.broadcasted_iota(jnp.int32, (n, n), 1)
    lane = lax.broadcasted_iota(jnp.int32, (1, n), 1)
    for k in range(n):
        pivot = 1.0 / matrix[k : k + 1, k : k + 1]
        row = jnp.where(lane == k, 1.0, matrix[k : k + 1, :]) * pivot
        col = matrix[:, k : k + 1]
        matrix = jnp.where(rows == k, row, jnp.where(lanes == k, 0.0, matrix) - col * row)
    return matrix


def total(x):
    return jnp.sum(jnp.sum(x, axis=1, keepdims=True), axis=0, keepdims=True)


def fit_kernel(pixel_total, place, mine, other, start, even, odd, load_out, noise_out, lat_out, full):
    parts, width, span = mine.shape
    blocks = 2 * parts
    freqs = blocks * width
    n = start.shape[0]
    eye_block = (
        lax.broadcasted_iota(jnp.int32, (width, width), 0)
        == lax.broadcasted_iota(jnp.int32, (width, width), 1)
    )
    power = jnp.zeros((1, 1), jnp.float32)
    for c, ref in enumerate((mine, other)):
        for k in range(parts):
            i = row_block(place, c, parts - k, parts)
            for j in range(parts + 1):
                block = ref[k, :, j * width : (j + 1) * width]
                at_row = pl.multiple_of(i * width, width)
                at_col = pl.multiple_of(lax.rem(i + j, blocks) * width, width)
                full[pl.ds(at_row, width), pl.ds(at_col, width)] = block
                if j == 0:
                    power = power + total(jnp.where(eye_block, block, 0.0))
                elif j < parts:
                    full[pl.ds(at_col, width), pl.ds(at_row, width)] = block.T
    eye = (
        lax.broadcasted_iota(jnp.int32, (n, n), 0) == lax.broadcasted_iota(jnp.int32, (n, n), 1)
    ).astype(jnp.float32)

    def weights(loads, gram, noise):
        inverse = inverse_spd(gram + noise * eye)
        return inverse, contract(inverse, loads, ((1,), (0,)))

    def step(_, state):
        loads, gram, noise = state
        inverse, weight = weights(loads, gram, noise)
        cross = contract(weight, full[...], ((1,), (0,)))
        second = contract(cross, weight, ((1,), (1,)))
        scaled = pixel_total * noise * inverse + second
        updated = contract(inverse_spd(scaled), cross, ((1,), (0,)))
        new_gram = contract(updated, updated, ((1,), (1,)))
        noise = (power - 2.0 * total(updated * cross) + total(scaled * new_gram)) / (
            pixel_total * freqs
        )
        return updated, new_gram, noise

    loads = start[...]
    state = (loads, contract(loads, loads, ((1,), (1,))), jnp.ones((1, 1), jnp.float32))
    loads, gram, noise = lax.fori_loop(0, ITERS, step, state)
    load_out[...] = loads
    noise_out[...] = noise
    weight = weights(loads, gram, noise)[1]
    latent = None
    for b in range(blocks):
        ref = (even, odd)[b % 2]
        term = contract(weight[:, b * width : (b + 1) * width], ref[b // 2], ((1,), (1,)))
        latent = term if latent is None else latent + term
    lat_out[...] = latent


def fit(place, mine, other, start, even, odd, pixel_total):
    n, freqs = start.shape
    vmem = pl.BlockSpec(memory_space=VM)
    return call(
        functools.partial(fit_kernel, pixel_total),
        in_specs=[pl.BlockSpec(memory_space=pltpu.SMEM)] + [vmem] * 5,
        out_specs=[vmem] * 3,
        out_shape=[
            jax.ShapeDtypeStruct((n, freqs), jnp.float32),
            jax.ShapeDtypeStruct((1, 1), jnp.float32),
            jax.ShapeDtypeStruct((n, even.shape[1]), jnp.float32),
        ],
        scratch_shapes=[VM((freqs, freqs), jnp.float32)],
        name="fit",
    )(place, mine, other, start, even, odd)


def clean_kernel(place, first, second, latents, loads, out):
    width = first.shape[1]
    for half, ref in enumerate((first, second)):
        out[:, half * width : (half + 1) * width] = ref[...] - contract(
            latents[0], loads[:, half * width : (half + 1) * width], ((0,), (0,))
        )


def clean(place, first, second, latents, loads):
    pixels, width = first.shape
    parts, n, rows = latents.shape

    def block(k, place):
        return (lax.rem(place[1] + parts - k, parts), 0)

    spec = pl.BlockSpec((rows, width), block)
    return call(
        clean_kernel,
        grid_spec=pltpu.PrefetchScalarGridSpec(
            num_scalar_prefetch=1,
            grid=(parts,),
            in_specs=[
                spec,
                spec,
                pl.BlockSpec((1, n, rows), lambda k, place: (k, 0, 0)),
                pl.BlockSpec(loads.shape, lambda k, place: (0, 0)),
            ],
            out_specs=pl.BlockSpec((rows, 2 * width), block),
        ),
        out_shape=jax.ShapeDtypeStruct((pixels, 2 * width), jnp.float32),
        name="clean",
    )(place, first, second, latents, loads)


def body(sky_maps, validity, row_taps, column_taps, init_loadings):
    rows_here, cols_here, freqs_here = sky_maps.shape
    sx, sy, af = (lax.axis_size(a) for a in ("sx", "sy", "af"))
    width = freqs_here // 2
    n = init_loadings.shape[1]
    pixels_here = rows_here * cols_here
    af_index = lax.axis_index("af")
    place = jnp.stack([lax.rem(lax.axis_index("sx"), 2), af_index]).astype(jnp.int32)
    mask = validity.astype(jnp.float32)[:, :, None]

    def halos(block, axis, count):
        low = lax.ppermute(block, axis, [(i, i + 1) for i in range(count - 1)])
        high = lax.ppermute(block, axis, [(i + 1, i) for i in range(count - 1)])
        return low, high

    def spread(taps, half):
        table = taps[half * width : (half + 1) * width].T[:, None, :]
        return jnp.broadcast_to(table, (table.shape[0], 8, width))

    def shifted(block, k):
        return lax.ppermute(block, "af", [(i, (i + k) % af) for i in range(af)])

    start_block = init_loadings.T
    start_all = lax.all_gather(start_block, "af", axis=1, tiled=True)

    beamed, traded = [], []
    masked = [sky_maps[:, :, h * width : (h + 1) * width] * mask for h in range(2)]
    around = [halos(m, "sx", sx) for m in masked]
    for h in range(2):
        smoothed = beam(around[h][0], masked[h], around[h][1], spread(row_taps, h))
        low, high = halos(smoothed, "sy", sy)
        spectra = beam(low, smoothed, high, spread(column_taps, h)).reshape(pixels_here, width)
        beamed.append(spectra)
        traded.append(
            lax.all_to_all(spectra.reshape(af, pixels_here // af, width), "af", 0, 0)
        )
    even, odd = traded

    partial = moments(place, even, odd)
    partial = partial[0] + lax.ppermute(partial[1], "sx", [(i, i ^ 1) for i in range(sx)])
    piece = partial[0]
    for k in range(1, af):
        piece = piece + shifted(partial[k], k)
    ranks = sx * sy // 2
    groups = [
        [s * sy + t for s in range(c, sx, 2) for t in range(sy)] for c in range(2)
    ]
    shape = piece.shape
    pieces = piece.reshape(ranks, -1, shape[1])
    pieces = lax.all_to_all(pieces, ("sx", "sy"), 0, 0, axis_index_groups=groups)
    owned = jnp.sum(pieces, axis=0)
    pieces = lax.all_to_all(
        jnp.broadcast_to(owned[None], pieces.shape), ("sx", "sy"), 0, 0, axis_index_groups=groups
    )
    piece = pieces.reshape(shape)
    mine = jnp.stack([piece] + [shifted(piece, k) for k in range(1, af)])
    other = lax.ppermute(mine, "sx", [(i, i ^ 1) for i in range(sx)])

    loadings, noise, latent = fit(
        place, mine, other, start_all, even, odd, float(pixels_here * sx * sy)
    )
    latents = jnp.stack([latent] + [shifted(latent, k) for k in range(1, af)])
    loads_here = lax.dynamic_slice_in_dim(loadings, af_index * freqs_here, freqs_here, 1)
    cleaned = clean(place, beamed[0], beamed[1], latents, loads_here)
    return (
        cleaned.reshape(rows_here, cols_here, freqs_here),
        loads_here.T,
        noise.reshape(()),
    )


def solution(mesh):
    placed = (P("sx", "sy", "af"), P("sx", "sy"), P("af", None), P("af", None), P("af", None))
    return jax.shard_map(
        body,
        mesh=mesh,
        in_specs=placed,
        out_specs=(P("sx", "sy", "af"), P("af", None), P()),
        check_vma=False,
    )
```

time: 1610 us -> 238 us (0.15)
  waiting for transfers between devices: 1020 us -> 42.6 us
  blocking collectives: 342 us -> 62 us
  matrix products: 98 us -> 0 us
  other arithmetic: 78.2 us -> 4.61 us
  Pallas kernels: 0 us -> 72.9 us
  starting transfers between devices: 19.2 us -> 41.9 us
  between operations: 23.1 us -> 0.97 us
    psum x4 -> x0, waiting for transfers between devices: 962 us -> none  [body(): lax.psum((contract_rows(pixel_rows, latent), contract_rows(latent, latent...]
    psum x4 -> x0, blocking collectives: 330 us -> none  [body(): lax.psum((contract_rows(pixel_rows, latent), contract_rows(latent, latent...]
    dot_general x69 -> x0, matrix products: 96 us -> none  [the longest x8 31.5 us: add_block(): jnp.einsum('icf,fio->ocf', slab_part, band_matrix, precision=HIGHEST_PREC...]
    pallas_call x0 -> x7, Pallas kernels: none -> 72.9 us  [the longest x1 41.3 us: fit(): call(functools.partial(fit_kernel, pixel_total), in_specs=[pl.BlockSpec(m...]
    another operation x45 -> x3, other arithmetic: 62.8 us -> 2.13 us  [the longest x1 1.41 us: body(): latents = jnp.stack([latent] + [shifted(latent, k) for k in range(1, af)])]
    all_to_all x0 -> x2, blocking collectives: none -> 49.1 us  [the longest x1 31.5 us: body(): lax.all_to_all(pieces, ('sx', 'sy'), 0, 0, axis_index_groups=groups)]
    ppermute x4 -> x19, starting transfers between devices: 10.6 us -> 33.9 us  [the longest x4 13.8 us: halos(): low = lax.ppermute(block, axis, [(i, i + 1) for i in range(count - 1)])]
    ppermute x4 -> x19, waiting for transfers between devices: 38.2 us -> 34.5 us  [the longest x9 30 us: shifted(): return lax.ppermute(block, 'af', [(i, (i + k) % af) for i in range(af)])]
  transfers between devices with their start and end apart: 10 -> 21, of which waited for: 10 -> 10; matrix products, arithmetic and copies ran while one was open for 1% -> 3% of each run, Pallas kernels for 0% -> 8%
where the time goes in v1:
time: 238 us; the launch traced here: 236 us
  Pallas kernels  72.9 us (31%)
  blocking collectives  62 us (26%)
  waiting for transfers between devices  42.6 us (18%)
  starting transfers between devices  41.9 us (18%)
  local copies, waits for them, and re-layouts  11.2 us (5%)
  other arithmetic  4.61 us (2%)
    pallas_call x1, Pallas kernels, fit(): call(functools.partial(fit_kernel, pixel_total), in_specs=[pl.BlockSpec(m...  41.3 us
    all_to_all x1, blocking collectives, body(): lax.all_to_all(pieces, ('sx', 'sy'), 0, 0, axis_index_groups=groups)  31.5 us
    ppermute x9, waiting for transfers between devices, shifted(): return lax.ppermute(block, 'af', [(i, (i + k) % af) for i in range(af)])  30 us
    pallas_call x4, Pallas kernels, beam(): call(beam_kernel, grid=(b // 8,), in_specs=[spec, spec, spec, pl.BlockSpe...  19.1 us
    all_to_all x1, blocking collectives, body(): lax.all_to_all(jnp.broadcast_to(owned[None], pieces.shape), ('sx', 'sy'),...  17.6 us
    ppermute x4, starting transfers between devices, halos(): low = lax.ppermute(block, axis, [(i, i + 1) for i in range(count - 1)])  13.8 us
    all_gather x1, blocking collectives, body(): start_all = lax.all_gather(start_block, 'af', axis=1, tiled=True)  12.9 us
    ppermute x9, starting transfers between devices, shifted(): return lax.ppermute(block, 'af', [(i, (i + k) % af) for i in range(af)])  10.7 us
  transfers between devices with their start and end apart: 21, of which 10 were waited for; matrix products, arithmetic and copies ran while one was open for 3% of the time, Pallas kernels for 8%

profile of v1, /device:TPU:32, one launch (start us, length us, event | category | flops | bytes accessed | tf_op | source)
XLA Modules:
  0.0 236.3 jit_solution(5124189201502605125)
XLA Ops:
  1.4 1.4 slice_multiply_fusion
  2.8 1.8 collective-permute-start.4
  5.9 4.4 %collective-permute-start = (f32[32,32,128]{2,1,0:T(8,128)S(1)}, f32[32,32,128]{2,1,0:T(8,128)S(1)}, u32[]{:S(2)}, u32[]{:S(2)}) collective-permute-start(f32[32,32,128]{2,1,0:T(8,128)S(1)} %get-tuple-element.13.own), channel_id=1, source_target_pairs={{0,32},{32,64},{64,96},{96,128},{128,160},{160,192},{192,224},{1,3... | collective-permute-start | bytes 1572872 | tf_op jit(solution)/shard_map/ppermute | solution.py:232
  12.7 4.8 %beam.6.own = f32[32,32,128]{2,1,0:T(8,128)} custom-call(f32[32,32,128]{2,1,0:T(8,128)} %copy-done.13, f32[32,32,128]{2,1,0:T(8,128)} %copy-done.5, f32[32,32,128]{2,1,0:T(8,128)} %copy-done.14, f32[65,8,128]{2,1,0:T(8,128)} %broadcast_in_dim.12.taps), custom_call_target="tpu_custom_call" | custom-call | tf_op jit(solution)/shard_map/beam/pallas_call | solution.py:50
  17.5 3.8 %collective-permute-start.6 = (f32[32,32,128]{2,1,0:T(8,128)}, f32[32,32,128]{2,1,0:T(8,128)S(1)}, u32[]{:S(2)}, u32[]{:S(2)}) collective-permute-start(f32[32,32,128]{2,1,0:T(8,128)} %beam.6.own), channel_id=1, source_target_pairs={{0,4},{4,8},{8,12},{12,16},{16,20},{20,24},{24,28},{1,5},{5,9},{9,... | collective-permute-start | bytes 1572872 | tf_op jit(solution)/shard_map/ppermute | solution.py:232
  21.3 2.0 collective-permute-start.7
  24.4 4.8 %beam.4.own = f32[32,32,128]{2,1,0:T(8,128)} custom-call(f32[32,32,128]{2,1,0:T(8,128)} %copy-done.7, f32[32,32,128]{2,1,0:T(8,128)} %copy-done.4, f32[32,32,128]{2,1,0:T(8,128)} %copy-done.9, f32[65,8,128]{2,1,0:T(8,128)} %broadcast_in_dim.10.taps), custom_call_target="tpu_custom_call" | custom-call | tf_op jit(solution)/shard_map/beam/pallas_call | solution.py:50
  29.2 3.8 %collective-permute-start.2 = (f32[32,32,128]{2,1,0:T(8,128)}, f32[32,32,128]{2,1,0:T(8,128)S(1)}, u32[]{:S(2)}, u32[]{:S(2)}) collective-permute-start(f32[32,32,128]{2,1,0:T(8,128)} %beam.4.own), channel_id=1, source_target_pairs={{0,4},{4,8},{8,12},{12,16},{16,20},{20,24},{24,28},{1,5},{5,9},{9,... | collective-permute-start | bytes 1572872 | tf_op jit(solution)/shard_map/ppermute | solution.py:232
  33.0 2.1 collective-permute-start.3
  36.2 4.8 %beam.7 = f32[32,32,128]{2,1,0:T(8,128)} custom-call(f32[32,32,128]{2,1,0:T(8,128)} %copy-done.8, f32[32,32,128]{2,1,0:T(8,128)} %beam.6.own, f32[32,32,128]{2,1,0:T(8,128)} %copy-done.10, f32[65,8,128]{2,1,0:T(8,128)} %broadcast_in_dim.13.taps), custom_call_target="tpu_custom_call" | custom-call | tf_op jit(solution)/shard_map/beam/pallas_call | solution.py:50
  41.0 4.3 %all-to-all-start.1 = ((f32[4,256,128]{2,1,0:T(8,128)}), f32[4,256,128]{2,1,0:T(8,128)S(1)}, u32[]{:S(2)}, u32[]{:S(2)}) async-start(f32[4,256,128]{2,1,0:T(8,128)} %bitcast.46), calls=%async_computation.1 | async-start | bytes 1048576 | tf_op jit(solution)/shard_map/all_to_all | solution.py:255
  45.3 1.8 collective-permute-done.3.high
  48.0 4.8 %beam.5 = f32[32,32,128]{2,1,0:T(8,128)} custom-call(f32[32,32,128]{2,1,0:T(8,128)} %copy-done.11, f32[32,32,128]{2,1,0:T(8,128)} %beam.4.own, f32[32,32,128]{2,1,0:T(8,128)} %copy-done.12, f32[65,8,128]{2,1,0:T(8,128)} %broadcast_in_dim.11.taps), custom_call_target="tpu_custom_call" | custom-call | tf_op jit(solution)/shard_map/beam/pallas_call | solution.py:50
  53.4 3.7 %all-to-all-start = ((f32[4,256,128]{2,1,0:T(8,128)}), f32[4,256,128]{2,1,0:T(8,128)S(1)}, u32[]{:S(2)}, u32[]{:S(2)}) async-start(f32[4,256,128]{2,1,0:T(8,128)} %bitcast.48), calls=%async_computation | async-start | bytes 1048576 | tf_op jit(solution)/shard_map/all_to_all | solution.py:255
  57.7 7.6 %all-to-all-done.even = f32[4,256,128]{2,1,0:T(8,128)S(1)} async-done(((f32[4,256,128]{2,1,0:T(8,128)}), f32[4,256,128]{2,1,0:T(8,128)S(1)}, u32[]{:S(2)}, u32[]{:S(2)}) %all-to-all-start) | async-done | bytes 524320 | tf_op jit(solution)/shard_map/all_to_all | solution.py:255
  66.1 7.6 %moments.1 = f32[2,4,128,640]{3,2,1,0:T(8,128)} custom-call(s32[2]{0:T(128)} %pad_add_fusion.place, f32[4,256,128]{2,1,0:T(8,128)} %copy-done.3, f32[4,256,128]{2,1,0:T(8,128)} %copy-done.2), custom_call_target="tpu_custom_call" | custom-call | tf_op jit(solution)/shard_map/moments/pallas_call | solution.py:81
  73.7 1.6 slice_bitcast_fusion
  75.2 2.6 %collective-permute-start.8 = (f32[4,128,640]{2,1,0:T(8,128)S(1)}, f32[4,128,640]{2,1,0:T(8,128)S(1)}, u32[]{:S(2)}, u32[]{:S(2)}) collective-permute-start(f32[4,128,640]{2,1,0:T(8,128)S(1)} %slice_bitcast_fusion), channel_id=1, source_target_pairs={{0,32},{32,0},{64,96},{96,64},{128,160},{160,128},{192,224},{224,1... | collective-permute-start | bytes 3932168 | tf_op jit(solution)/shard_map/ppermute | solution.py:260
  77.8 2.7 %collective-permute-done.8 = f32[4,128,640]{2,1,0:T(8,128)S(1)} collective-permute-done((f32[4,128,640]{2,1,0:T(8,128)S(1)}, f32[4,128,640]{2,1,0:T(8,128)S(1)}, u32[]{:S(2)}, u32[]{:S(2)}) %collective-permute-start.8) | collective-permute-done | bytes 1310752 | tf_op jit(solution)/shard_map/ppermute | solution.py:260
  81.4 2.7 %collective-permute-start.11 = (f32[128,640]{1,0:T(8,128)S(1)}, f32[128,640]{1,0:T(8,128)S(1)}, u32[]{:S(2)}, u32[]{:S(2)}) collective-permute-start(f32[128,640]{1,0:T(8,128)S(1)} %get-tuple-element.10), channel_id=1, source_target_pairs={{0,3},{1,0},{2,1},{3,2},{4,7},{5,4},{6,5},{7,6},{8,11},{9,8},{10,9... | collective-permute-start | bytes 983048 | tf_op jit(solution)/shard_map/ppermute | solution.py:241
  84.0 8.9 %collective-permute-done.10 = f32[128,640]{1,0:T(8,128)S(1)} collective-permute-done((f32[128,640]{1,0:T(8,128)S(1)}, f32[128,640]{1,0:T(8,128)S(1)}, u32[]{:S(2)}, u32[]{:S(2)}) %collective-permute-start.10) | collective-permute-done | bytes 327712 | tf_op jit(solution)/shard_map/ppermute | solution.py:241
  92.9 4.9 %collective-permute-done.11 = f32[128,640]{1,0:T(8,128)S(1)} collective-permute-done((f32[128,640]{1,0:T(8,128)S(1)}, f32[128,640]{1,0:T(8,128)S(1)}, u32[]{:S(2)}, u32[]{:S(2)}) %collective-permute-start.11) | collective-permute-done | bytes 327712 | tf_op jit(solution)/shard_map/ppermute | solution.py:241
  97.9 1.5 collective-permute-done.9
  99.5 31.5 %all_to_all.20 = f32[32,4,640]{2,1,0:T(4,128)S(1)} all-to-all(f32[32,4,640]{2,1,0:T(4,128)S(1)} %reshape.32), channel_id=1, replica_groups={{0,4,8,12,16,20,24,28,64,68,72,76,80,84,88,92,128,132,136,140,144,148,1..., dimensions={0} | all-to-all | bytes 655360 | tf_op jit(solution)/shard_map/all_to_all | solution.py:270
  131.1 17.6 %all_to_all.21 = f32[32,4,640]{2,1,0:T(4,128)S(1)} all-to-all(f32[32,4,640]{2,1,0:T(4,128)S(1)} %broadcast_in_dim.14), channel_id=1, replica_groups={{0,4,8,12,16,20,24,28,64,68,72,76,80,84,88,92,128,132,136,140,144,148,1..., dimensions={0} | all-to-all | bytes 655360 | tf_op jit(solution)/shard_map/all_to_all | solution.py:272
  149.0 2.6 %collective-permute-start.13 = (f32[128,640]{1,0:T(8,128)S(1)}, f32[128,640]{1,0:T(8,128)S(1)}, u32[]{:S(2)}, u32[]{:S(2)}) collective-permute-start(f32[128,640]{1,0:T(8,128)S(1)} %reshape.33), channel_id=1, source_target_pairs={{0,2},{1,3},{2,0},{3,1},{4,6},{5,7},{6,4},{7,5},{8,10},{9,11},{10,... | collective-permute-start | bytes 983048 | tf_op jit(solution)/shard_map/ppermute | solution.py:241
  152.3 12.9 %collective-permute-done.12 = f32[128,640]{1,0:T(8,128)S(1)} collective-permute-done((f32[128,640]{1,0:T(8,128)S(1)}, f32[128,640]{1,0:T(8,128)S(1)}, u32[]{:S(2)}, u32[]{:S(2)}) %collective-permute-start.12) | collective-permute-done | bytes 327712 | tf_op jit(solution)/shard_map/ppermute | solution.py:241
  166.6 12.9 %all_gather.3.start = f32[32,1024]{1,0:T(8,128)} all-gather(f32[32,256]{1,0:T(8,128)S(1)} %bitcast.54), channel_id=1, replica_groups=mesh['sx'=8,'sy'=8,'af'=4] {'af'}, dimensions={1}, use_global_device_ids=true | all-gather | bytes 163840 | tf_op jit(solution)/shard_map/all_gather | solution.py:244
  180.6 41.3 %fit.1 = (f32[32,1024]{1,0:T(8,128)}, f32[1,1]{1,0:T(1,128)}, f32[32,256]{1,0:T(8,128)}) custom-call(s32[2]{0:T(128)} %pad_add_fusion.place, f32[4,128,640]{2,1,0:T(8,128)} %copy-done.1, f32[4,128,640]{2,1,0:T(8,128)} %copy-done.6, f32[32,1024]{1,0:T(8,128)} %all_gather.3.start, f32[4,256,128]{2,1,0:T(8,128)} %copy-done.3, f32[4,256,128]{2,1,0:T(8,128)} %copy-done.2), custom_call_target="tpu_custom_call" | custom-call | tf_op jit(solution)/shard_map/fit/pallas_call | solution.py:173
  223.2 2.7 %collective-permute-start.17 = (f32[32,256]{1,0:T(8,128)}, f32[32,256]{1,0:T(8,128)S(1)}, u32[]{:S(2)}, u32[]{:S(2)}) collective-permute-start(f32[32,256]{1,0:T(8,128)} %get-tuple-element.6), channel_id=1, source_target_pairs={{0,2},{1,3},{2,0},{3,1},{4,6},{5,7},{6,4},{7,5},{8,10},{9,11},{10,... | collective-permute-start | bytes 98312 | tf_op jit(solution)/shard_map/ppermute | solution.py:241
  230.0 1.4 pad_maximum_fusion.1.latents
  231.4 4.9 %clean.1 = f32[1024,256]{1,0:T(8,128)} custom-call(s32[2]{0:T(128)} %pad_add_fusion.place, f32[1024,128]{1,0:T(8,128)} %bitcast.49, f32[1024,128]{1,0:T(8,128)} %bitcast.47, f32[4,32,256]{2,1,0:T(8,128)} %pad_maximum_fusion.1.latents, f32[32,256]{1,0:T(8,128)} %constant_dynamic-slice_fusion.loads), custom_call_target="tpu_custom_call" | custom-call | tf_op jit(solution)/shard_map/clean/pallas_call | solution.py:203
  (78 shorter events, 19.3 us)
Async XLA Ops:
  0.6 11.0 %copy-start.15 = (f32[256,65]{0,1:T(8,128)S(1)}, f32[256,65]{0,1:T(8,128)}, u32[]{:S(2)}) copy-start(f32[256,65]{0,1:T(8,128)} %param.7) | copy-start | bytes 199684
  2.8 9.7 %copy-start.5 = (f32[32,32,128]{2,1,0:T(8,128)}, f32[32,32,128]{2,1,0:T(8,128)S(1)}, u32[]{:S(2)}) copy-start(f32[32,32,128]{2,1,0:T(8,128)S(1)} %get-tuple-element.12.own) | copy-start | bytes 1572868
  2.8 14.7 %copy-start.4 = (f32[32,32,128]{2,1,0:T(8,128)}, f32[32,32,128]{2,1,0:T(8,128)S(1)}, u32[]{:S(2)}) copy-start(f32[32,32,128]{2,1,0:T(8,128)S(1)} %get-tuple-element.13.own) | copy-start | bytes 1572868
  2.8 8.8 %collective-permute-start.4 = (f32[32,32,128]{2,1,0:T(8,128)S(1)}, f32[32,32,128]{2,1,0:T(8,128)S(1)}, u32[]{:S(2)}, u32[]{:S(2)}) collective-permute-start(f32[32,32,128]{2,1,0:T(8,128)S(1)} %get-tuple-element.12.own), channel_id=1, source_target_pairs={{0,32},{32,64},{64,96},{96,128},{128,160},{160,192},{192,224},{1,3... | collective-permute-start | bytes 1572872 | tf_op jit(solution)/shard_map/ppermute | solution.py:232
  4.6 7.1 %collective-permute-start.5 = (f32[32,32,128]{2,1,0:T(8,128)S(1)}, f32[32,32,128]{2,1,0:T(8,128)S(1)}, u32[]{:S(2)}, u32[]{:S(2)}) collective-permute-start(f32[32,32,128]{2,1,0:T(8,128)S(1)} %get-tuple-element.12.own), channel_id=1, source_target_pairs={{32,0},{64,32},{96,64},{128,96},{160,128},{192,160},{224,192},{33,... | collective-permute-start | bytes 1572872 | tf_op jit(solution)/shard_map/ppermute | solution.py:233
  5.9 17.4 %collective-permute-start = (f32[32,32,128]{2,1,0:T(8,128)S(1)}, f32[32,32,128]{2,1,0:T(8,128)S(1)}, u32[]{:S(2)}, u32[]{:S(2)}) collective-permute-start(f32[32,32,128]{2,1,0:T(8,128)S(1)} %get-tuple-element.13.own), channel_id=1, source_target_pairs={{0,32},{32,64},{64,96},{96,128},{128,160},{160,192},{192,224},{1,3... | collective-permute-start | bytes 1572872 | tf_op jit(solution)/shard_map/ppermute | solution.py:232
  10.3 13.1 %collective-permute-start.1 = (f32[32,32,128]{2,1,0:T(8,128)S(1)}, f32[32,32,128]{2,1,0:T(8,128)S(1)}, u32[]{:S(2)}, u32[]{:S(2)}) collective-permute-start(f32[32,32,128]{2,1,0:T(8,128)S(1)} %get-tuple-element.13.own), channel_id=1, source_target_pairs={{32,0},{64,32},{96,64},{128,96},{160,128},{192,160},{224,192},{33,... | collective-permute-start | bytes 1572872 | tf_op jit(solution)/shard_map/ppermute | solution.py:233
  11.7 1.0 copy-start.14
  17.5 17.6 %collective-permute-start.6 = (f32[32,32,128]{2,1,0:T(8,128)}, f32[32,32,128]{2,1,0:T(8,128)S(1)}, u32[]{:S(2)}, u32[]{:S(2)}) collective-permute-start(f32[32,32,128]{2,1,0:T(8,128)} %beam.6.own), channel_id=1, source_target_pairs={{0,4},{4,8},{8,12},{12,16},{16,20},{20,24},{24,28},{1,5},{5,9},{9,... | collective-permute-start | bytes 1572872 | tf_op jit(solution)/shard_map/ppermute | solution.py:232
  21.3 13.8 %collective-permute-start.7 = (f32[32,32,128]{2,1,0:T(8,128)}, f32[32,32,128]{2,1,0:T(8,128)S(1)}, u32[]{:S(2)}, u32[]{:S(2)}) collective-permute-start(f32[32,32,128]{2,1,0:T(8,128)} %beam.6.own), channel_id=1, source_target_pairs={{4,0},{8,4},{12,8},{16,12},{20,16},{24,20},{28,24},{5,1},{9,5},{13... | collective-permute-start | bytes 1572872 | tf_op jit(solution)/shard_map/ppermute | solution.py:233
  23.4 11.7 %copy-start.16 = (f32[256,65]{0,1:T(8,128)S(1)}, f32[256,65]{0,1:T(8,128)}, u32[]{:S(2)}) copy-start(f32[256,65]{0,1:T(8,128)} %param.8) | copy-start | bytes 199684
  29.2 16.1 %collective-permute-start.2 = (f32[32,32,128]{2,1,0:T(8,128)}, f32[32,32,128]{2,1,0:T(8,128)S(1)}, u32[]{:S(2)}, u32[]{:S(2)}) collective-permute-start(f32[32,32,128]{2,1,0:T(8,128)} %beam.4.own), channel_id=1, source_target_pairs={{0,4},{4,8},{8,12},{12,16},{16,20},{20,24},{24,28},{1,5},{5,9},{9,... | collective-permute-start | bytes 1572872 | tf_op jit(solution)/shard_map/ppermute | solution.py:232
  33.0 14.0 %collective-permute-start.3 = (f32[32,32,128]{2,1,0:T(8,128)}, f32[32,32,128]{2,1,0:T(8,128)S(1)}, u32[]{:S(2)}, u32[]{:S(2)}) collective-permute-start(f32[32,32,128]{2,1,0:T(8,128)} %beam.4.own), channel_id=1, source_target_pairs={{4,0},{8,4},{12,8},{16,12},{20,16},{24,20},{28,24},{5,1},{9,5},{13... | collective-permute-start | bytes 1572872 | tf_op jit(solution)/shard_map/ppermute | solution.py:233
  35.1 1.0 copy-start.10
  41.0 12.4 %all-to-all-start.1 = ((f32[4,256,128]{2,1,0:T(8,128)}), f32[4,256,128]{2,1,0:T(8,128)S(1)}, u32[]{:S(2)}, u32[]{:S(2)}) async-start(f32[4,256,128]{2,1,0:T(8,128)} %bitcast.46), calls=%async_computation.1 | async-start | bytes 1048576 | tf_op jit(solution)/shard_map/all_to_all | solution.py:255
  45.3 2.5 %copy-start.11 = (f32[32,32,128]{2,1,0:T(8,128)}, f32[32,32,128]{2,1,0:T(8,128)S(1)}, u32[]{:S(2)}) copy-start(f32[32,32,128]{2,1,0:T(8,128)S(1)} %collective-permute-done.2.low) | copy-start | bytes 1572868
  53.4 11.9 %copy-start.2 = (f32[4,256,128]{2,1,0:T(8,128)}, f32[4,256,128]{2,1,0:T(8,128)S(1)}, u32[]{:S(2)}) copy-start(f32[4,256,128]{2,1,0:T(8,128)S(1)} %all-to-all-done.1.odd) | copy-start | bytes 1572868
  53.4 11.9 %all-to-all-start = ((f32[4,256,128]{2,1,0:T(8,128)}), f32[4,256,128]{2,1,0:T(8,128)S(1)}, u32[]{:S(2)}, u32[]{:S(2)}) async-start(f32[4,256,128]{2,1,0:T(8,128)} %bitcast.48), calls=%async_computation | async-start | bytes 1048576 | tf_op jit(solution)/shard_map/all_to_all | solution.py:255
  73.7 6.8 %copy-start = (f32[2,4,128,640]{3,2,1,0:T(8,128)S(1)}, f32[2,4,128,640]{3,2,1,0:T(8,128)}, u32[]{:S(2)}) copy-start(f32[2,4,128,640]{3,2,1,0:T(8,128)} %moments.1) | copy-start | bytes 7864324
  75.2 5.3 %collective-permute-start.8 = (f32[4,128,640]{2,1,0:T(8,128)S(1)}, f32[4,128,640]{2,1,0:T(8,128)S(1)}, u32[]{:S(2)}, u32[]{:S(2)}) collective-permute-start(f32[4,128,640]{2,1,0:T(8,128)S(1)} %slice_bitcast_fusion), channel_id=1, source_target_pairs={{0,32},{32,0},{64,96},{96,64},{128,160},{160,128},{192,224},{224,1... | collective-permute-start | bytes 3932168 | tf_op jit(solution)/shard_map/ppermute | solution.py:260
  80.7 12.2 %collective-permute-start.10 = (f32[128,640]{1,0:T(8,128)S(1)}, f32[128,640]{1,0:T(8,128)S(1)}, u32[]{:S(2)}, u32[]{:S(2)}) collective-permute-start(f32[128,640]{1,0:T(8,128)S(1)} %get-tuple-element.11), channel_id=1, source_target_pairs={{0,2},{1,3},{2,0},{3,1},{4,6},{5,7},{6,4},{7,5},{8,10},{9,11},{10,... | collective-permute-start | bytes 983048 | tf_op jit(solution)/shard_map/ppermute | solution.py:241
  81.4 16.5 %collective-permute-start.11 = (f32[128,640]{1,0:T(8,128)S(1)}, f32[128,640]{1,0:T(8,128)S(1)}, u32[]{:S(2)}, u32[]{:S(2)}) collective-permute-start(f32[128,640]{1,0:T(8,128)S(1)} %get-tuple-element.10), channel_id=1, source_target_pairs={{0,3},{1,0},{2,1},{3,2},{4,7},{5,4},{6,5},{7,6},{8,11},{9,8},{10,9... | collective-permute-start | bytes 983048 | tf_op jit(solution)/shard_map/ppermute | solution.py:241
  84.0 15.3 %collective-permute-start.9 = (f32[128,640]{1,0:T(8,128)S(1)}, f32[128,640]{1,0:T(8,128)S(1)}, u32[]{:S(2)}, u32[]{:S(2)}) collective-permute-start(f32[128,640]{1,0:T(8,128)S(1)} %get-tuple-element.9), channel_id=1, source_target_pairs={{0,1},{1,2},{2,3},{3,0},{4,5},{5,6},{6,7},{7,4},{8,9},{9,10},{10,1... | collective-permute-start | bytes 983048 | tf_op jit(solution)/shard_map/ppermute | solution.py:241
  148.9 16.4 %collective-permute-start.12 = (f32[128,640]{1,0:T(8,128)S(1)}, f32[128,640]{1,0:T(8,128)S(1)}, u32[]{:S(2)}, u32[]{:S(2)}) collective-permute-start(f32[128,640]{1,0:T(8,128)S(1)} %reshape.33), channel_id=1, source_target_pairs={{0,1},{1,2},{2,3},{3,0},{4,5},{5,6},{6,7},{7,4},{8,9},{9,10},{10,1... | collective-permute-start | bytes 983048 | tf_op jit(solution)/shard_map/ppermute | solution.py:241
  149.0 16.3 %collective-permute-start.13 = (f32[128,640]{1,0:T(8,128)S(1)}, f32[128,640]{1,0:T(8,128)S(1)}, u32[]{:S(2)}, u32[]{:S(2)}) collective-permute-start(f32[128,640]{1,0:T(8,128)S(1)} %reshape.33), channel_id=1, source_target_pairs={{0,2},{1,3},{2,0},{3,1},{4,6},{5,7},{6,4},{7,5},{8,10},{9,11},{10,... | collective-permute-start | bytes 983048 | tf_op jit(solution)/shard_map/ppermute | solution.py:241
  151.6 14.3 %collective-permute-start.14 = (f32[128,640]{1,0:T(8,128)S(1)}, f32[128,640]{1,0:T(8,128)S(1)}, u32[]{:S(2)}, u32[]{:S(2)}) collective-permute-start(f32[128,640]{1,0:T(8,128)S(1)} %reshape.33), channel_id=1, source_target_pairs={{0,3},{1,0},{2,1},{3,2},{4,7},{5,4},{6,5},{7,6},{8,11},{9,8},{10,9... | collective-permute-start | bytes 983048 | tf_op jit(solution)/shard_map/ppermute | solution.py:241
  166.0 13.6 %copy-start.1 = (f32[4,128,640]{2,1,0:T(8,128)}, f32[4,128,640]{2,1,0:T(8,128)S(1)}, u32[]{:S(2)}) copy-start(f32[4,128,640]{2,1,0:T(8,128)S(1)} %pad_maximum_fusion.mine) | copy-start | bytes 3932164
  166.0 13.6 %collective-permute-start.15 = (f32[4,128,640]{2,1,0:T(8,128)S(1)}, f32[4,128,640]{2,1,0:T(8,128)S(1)}, u32[]{:S(2)}, u32[]{:S(2)}) collective-permute-start(f32[4,128,640]{2,1,0:T(8,128)S(1)} %pad_maximum_fusion.mine), channel_id=1, source_target_pairs={{0,32},{32,0},{64,96},{96,64},{128,160},{160,128},{192,224},{224,1... | collective-permute-start | bytes 3932168 | tf_op jit(solution)/shard_map/ppermute | solution.py:277
  179.5 1.1 copy-start.6
  221.9 6.8 %collective-permute-start.16 = (f32[32,256]{1,0:T(8,128)}, f32[32,256]{1,0:T(8,128)S(1)}, u32[]{:S(2)}, u32[]{:S(2)}) collective-permute-start(f32[32,256]{1,0:T(8,128)} %get-tuple-element.6), channel_id=1, source_target_pairs={{0,1},{1,2},{2,3},{3,0},{4,5},{5,6},{6,7},{7,4},{8,9},{9,10},{10,1... | collective-permute-start | bytes 98312 | tf_op jit(solution)/shard_map/ppermute | solution.py:241
  223.2 5.6 %collective-permute-start.17 = (f32[32,256]{1,0:T(8,128)}, f32[32,256]{1,0:T(8,128)S(1)}, u32[]{:S(2)}, u32[]{:S(2)}) collective-permute-start(f32[32,256]{1,0:T(8,128)} %get-tuple-element.6), channel_id=1, source_target_pairs={{0,2},{1,3},{2,0},{3,1},{4,6},{5,7},{6,4},{7,5},{8,10},{9,11},{10,... | collective-permute-start | bytes 98312 | tf_op jit(solution)/shard_map/ppermute | solution.py:241
  225.8 4.1 %collective-permute-start.18 = (f32[32,256]{1,0:T(8,128)}, f32[32,256]{1,0:T(8,128)S(1)}, u32[]{:S(2)}, u32[]{:S(2)}) collective-permute-start(f32[32,256]{1,0:T(8,128)} %get-tuple-element.6), channel_id=1, source_target_pairs={{0,3},{1,0},{2,1},{3,2},{4,7},{5,4},{6,5},{7,6},{8,11},{9,8},{10,9... | collective-permute-start | bytes 98312 | tf_op jit(solution)/shard_map/ppermute | solution.py:241
  (7 other events, 6.2 us)

commit v2 on v0

v2 whole, which is shorter than its diff:
```python
import functools

import jax
import jax.numpy as jnp
from jax import lax
from jax.experimental import pallas as pl
from jax.experimental.pallas import tpu as pltpu
from jax.sharding import PartitionSpec as P

ITERS = 4
HI = lax.Precision.HIGHEST
VM = pltpu.VMEM
INTERPRET = False
LIMIT = 32 << 20


def call(kernel, out_shapes, *args, name, scratch=(), dtypes=None):
    dtypes = dtypes or [jnp.float32] * len(out_shapes)
    fast = pl.BlockSpec(memory_space=VM)
    specs = [
        pl.BlockSpec(memory_space=pltpu.SMEM) if x.dtype == jnp.int32 else fast for x in args
    ]
    if INTERPRET:
        outs = [jax.ShapeDtypeStruct(s, d) for s, d in zip(out_shapes, dtypes)]
    else:
        outs = [VM(s, d) for s, d in zip(out_shapes, dtypes)]
        args = [
            x if x.dtype == jnp.int32 else pltpu.with_memory_space_constraint(x, VM) for x in args
        ]
    return pl.pallas_call(
        kernel,
        out_shape=outs,
        in_specs=specs,
        out_specs=[fast] * len(outs),
        scratch_shapes=list(scratch),
        compiler_params=pltpu.CompilerParams(vmem_limit_bytes=LIMIT),
        interpret=INTERPRET,
        name=name,
    )(*args)


def contract(left, right, dims):
    return lax.dot_general(
        left, right, (dims, ((), ())), precision=HI, preferred_element_type=jnp.float32
    )


def split3(x):
    hi = x.astype(jnp.bfloat16)
    rest = x - hi.astype(jnp.float32)
    mid = rest.astype(jnp.bfloat16)
    low = (rest - mid.astype(jnp.float32)).astype(jnp.bfloat16)
    return hi, mid, low


def thin(left, right, dims):
    (ld,), (rd,) = dims
    lh, lm, ll = split3(left)
    rh, rm, rl = split3(right)
    a = jnp.concatenate([ll, lm, lh, lm, lh, lh], axis=ld)
    b = jnp.concatenate([rh, rm, rl, rh, rm, rh], axis=rd)
    return lax.dot_general(a, b, (dims, ((), ())), preferred_element_type=jnp.float32)


def beam_kernel(half, low, own, high, taps, *rest):
    out = rest[-1]
    length, wide, width = own.shape
    count = taps.shape[0]
    refs = (low, own, high)
    lanes = slice(half * width, (half + 1) * width)

    def strip(j, _):
        at = pl.ds(pl.multiple_of(j * 8, 8), 8)
        for block in range(length // 8):
            acc = [None] * 8
            held = {}
            for k in range(count + 7):
                row = block * 8 + k
                value = refs[row // length][row % length, at, :]
                if k < count:
                    held[k] = jnp.broadcast_to(taps[k : k + 1, lanes], value.shape)
                for i in range(8):
                    t = k - i
                    if 0 <= t < count:
                        term = held[t] * value
                        acc[i] = term if acc[i] is None else acc[i] + term
            out[j, 0:8, block * 8 : block * 8 + 8, :] = jnp.swapaxes(jnp.stack(acc), 0, 1)
        if len(rest) == 2:
            for e in range(out.shape[1] - 8):
                out[j, 8 + e] = rest[0][e * length : (e + 1) * length, lanes]

    lax.fori_loop(0, wide // 8, strip, None)


def beam(low, own, high, taps, half, loads=None):
    a, b, f = own.shape
    assert taps.shape[0] == 2 * a + 1
    more = [] if loads is None else [loads]
    extra = 0 if loads is None else loads.shape[0] // a
    shape = (b // 8, 8 + extra, a, f)
    kernel = functools.partial(beam_kernel, half)
    return call(kernel, [shape], low, own, high, taps, *more, name="beam")[0]


def row_block(place, c, k, parts):
    return lax.rem(place[0] + c, 2) * parts + lax.rem(place[1] + k, parts)


def moment_kernel(c, pixels, place, *refs):
    if len(refs) == 5:
        even, odd, out, hi, lo = refs
        parts = even.shape[0]
        for b in range(2 * parts):
            value = (even, odd)[b % 2][b // 2, 0:pixels]
            top = value.astype(jnp.bfloat16)
            hi[b] = top
            lo[b] = (value - top.astype(jnp.float32)).astype(jnp.bfloat16)
    else:
        hi, lo, out = refs
        parts = hi.shape[0] // 2
    blocks = 2 * parts
    for k in range(parts):
        i = row_block(place, c, k, parts)
        at = [lax.rem(i + j, blocks) for j in range(parts + 1)]
        left = jnp.concatenate([lo[i], hi[i], hi[i]], axis=0)
        high = jnp.concatenate([hi[b] for b in at], axis=1)
        low = jnp.concatenate([lo[b] for b in at], axis=1)
        right = jnp.concatenate([high, low, high], axis=0)
        out[k] = lax.dot_general(
            left, right, (((0,), (0,)), ((), ())), preferred_element_type=jnp.float32
        )


def moments(place, even, odd, pixels):
    parts, _, width = even.shape
    shape = (parts, width, width * (parts + 1))
    halves = (2 * parts, pixels, width)
    half = jnp.bfloat16
    theirs, hi, lo = call(
        functools.partial(moment_kernel, 1, pixels), [shape, halves, halves], place, even, odd,
        name="moments", dtypes=[jnp.float32, half, half],
    )
    ours = call(functools.partial(moment_kernel, 0, pixels), [shape], place, hi, lo, name="moments")
    return theirs, ours[0], hi, lo


def inverse_spd(matrix):
    n = matrix.shape[0]
    lane = lax.broadcasted_iota(jnp.int32, (8, n), 1)
    row = lax.broadcasted_iota(jnp.int32, (8, n), 0)
    unit = 1.0 / jnp.broadcast_to(matrix[0:1, 0:1], (8, n))
    tiles = [matrix[i : i + 8] * unit for i in range(0, n, 8)]
    for k in range(0, n, 2):
        at, r = divmod(k, 8)

        def every(tile, s):
            return jnp.broadcast_to(tile[s : s + 1], (8, n))

        left = [jnp.broadcast_to(t[:, k : k + 1], (8, n)) for t in tiles]
        right = [jnp.broadcast_to(t[:, k + 1 : k + 2], (8, n)) for t in tiles]
        a, b = every(left[at], r), every(right[at], r)
        c, d = every(left[at], r + 1), every(right[at], r + 1)
        pivot = 1.0 / (a * d - b * c)
        inside = (lane == k) | (lane == k + 1)
        top = jnp.where(inside, (lane == k).astype(jnp.float32), every(tiles[at], r))
        low = jnp.where(inside, (lane == k + 1).astype(jnp.float32), every(tiles[at], r + 1))
        first = (d * top - b * low) * pivot
        second = (a * low - c * top) * pivot
        tiles = [
            jnp.where(inside, 0.0, t) - x * first - y * second
            for t, x, y in zip(tiles, left, right)
        ]
        tiles[at] = jnp.where(row == r, first, jnp.where(row == r + 1, second, tiles[at]))
    return jnp.concatenate([t * unit for t in tiles], axis=0)


def total(x):
    return jnp.sum(jnp.sum(x, axis=1, keepdims=True), axis=0, keepdims=True)


def identity(n):
    return lax.broadcasted_iota(jnp.int32, (n, n), 0) == lax.broadcasted_iota(jnp.int32, (n, n), 1)


def weights(loads, gram, noise):
    inverse = inverse_spd(gram + jnp.where(identity(gram.shape[0]), noise, 0.0))
    return inverse, thin(inverse, loads, ((1,), (0,)))


def first_kernel(even, odd, inverse_out, weight_out):
    n = weight_out.shape[0]
    rows = even.shape[1]
    loads = jnp.concatenate(
        [ref[b, rows - n : rows] for b in range(even.shape[0]) for ref in (even, odd)], axis=1
    )
    gram = contract(loads, loads, ((1,), (1,)))
    inverse_out[...], weight_out[...] = weights(loads, gram, jnp.ones((1, 1), jnp.float32))


def first_weights(even, odd, n):
    parts, _, width = even.shape
    return call(first_kernel, [(n, n), (n, 2 * parts * width)], even, odd, name="first")


def cross_of(weight, hi, mid, low):
    n = weight.shape[0]
    stacked = jnp.concatenate(split3(weight), axis=0)

    def product(count, ref):
        return jnp.dot(stacked[: count * n], ref[...], preferred_element_type=jnp.float32)

    top, middle, last = product(3, hi), product(2, mid), product(1, low)
    small = top[2 * n :] + middle[n:] + last
    return top[:n] + (top[n : 2 * n] + middle[:n] + small)


def fit_kernel(pixel_total, parts, place, *refs):
    slots = refs[: 2 * parts]
    inverse0, weight0, map_hi, map_lo = refs[2 * parts : 2 * parts + 4]
    block_out, noise_out, lat_out, hi, mid, low, held = refs[2 * parts + 4 :]
    width = slots[0].shape[0]
    blocks = 2 * parts
    freqs = blocks * width
    n = weight0.shape[0]
    diagonal = identity(width)
    power = jnp.zeros((width, width), jnp.float32)
    for s, ref in enumerate(slots):
        i = row_block(place, s // parts, parts - s % parts, parts)
        for j in range(parts + 1):
            block = ref[:, j * width : (j + 1) * width]
            at_row = pl.multiple_of(i * width, width)
            at_col = pl.multiple_of(lax.rem(i + j, blocks) * width, width)
            for dest, value in zip((hi, mid, low), split3(block)):
                dest[pl.ds(at_row, width), pl.ds(at_col, width)] = value
            if j == 0:
                power = power + jnp.where(diagonal, block, 0.0)
            elif j < parts:
                for dest, value in zip((hi, mid, low), split3(block.T)):
                    dest[pl.ds(at_col, width), pl.ds(at_row, width)] = value
    power = total(power)

    def step(_, state):
        inverse, weight, noise = state
        cross = cross_of(weight, hi, mid, low)
        second = contract(cross, weight, ((1,), (1,)))
        scaled = pixel_total * noise * inverse + second
        updated = thin(inverse_spd(scaled), cross, ((1,), (0,)))
        held[...] = updated
        gram = contract(updated, updated, ((1,), (1,)))
        noise = (power - 2.0 * total(updated * cross) + total(scaled * gram)) / (
            pixel_total * freqs
        )
        return (*weights(updated, gram, noise), noise)

    state = (inverse0[...], weight0[...], jnp.ones((1, 1), jnp.float32))
    _, weight, noise = lax.fori_loop(0, ITERS, step, state)
    noise_out[...] = noise
    here = block_out.shape[1]
    block_out[...] = held[:, pl.ds(pl.multiple_of(place[1] * here, here), here)]
    whigh, wlow, _ = split3(weight)
    pair = jnp.concatenate([whigh, wlow], axis=0)
    latent = None
    for b in range(blocks):
        lanes = slice(b * width, (b + 1) * width)
        dims = (((1,), (1,)), ((), ()))
        both = lax.dot_general(
            pair[:, lanes], map_hi[b], dims, preferred_element_type=jnp.float32
        )
        term = lax.dot_general(
            whigh[:, lanes], map_lo[b], dims, preferred_element_type=jnp.float32
        )
        term = both[:n] + (both[n:] + term)
        latent = term if latent is None else latent + term
    lat_out[...] = latent


def fit(place, slots, inverse0, weight0, hi, lo, pixel_total):
    n, freqs = weight0.shape
    parts = hi.shape[0] // 2
    return call(
        functools.partial(fit_kernel, pixel_total, parts),
        [(n, freqs // parts), (1, 1), (n, hi.shape[1])],
        place, *slots, inverse0, weight0, hi, lo,
        name="fit",
        scratch=[VM((freqs, freqs), jnp.bfloat16)] * 3 + [VM((n, freqs), jnp.float32)],
    )


def clean_kernel(parts, place, *refs):
    latents, loads, first, second, out = refs[:parts], *refs[parts:]
    width = first.shape[2]
    rows = latents[0].shape[1]
    for k in range(parts):
        at = lax.rem(place[1] + parts - k, parts)
        model = thin(latents[k][...], loads[...], ((0,), (0,)))
        here = pl.ds(pl.multiple_of(at * rows, rows), rows)
        out[here, 0:width] = first[at, 0:rows] - model[:, 0:width]
        out[here, width:] = second[at, 0:rows] - model[:, width:]


def clean(place, first, second, latents, loads):
    parts, _, width = first.shape
    rows = latents[0].shape[1]
    kernel = functools.partial(clean_kernel, parts)
    shape = (parts * rows, 2 * width)
    return call(kernel, [shape], place, *latents, loads, first, second, name="clean")[0]


def body(sky_maps, validity, row_taps, column_taps, init_loadings):
    rows_here, cols_here, freqs_here = sky_maps.shape
    sx, sy, af = (lax.axis_size(a) for a in ("sx", "sy", "af"))
    width = freqs_here // 2
    n = init_loadings.shape[1]
    pixels_here = rows_here * cols_here
    pixels = pixels_here // af
    place = jnp.stack([lax.rem(lax.axis_index("sx"), 2), lax.axis_index("af")]).astype(jnp.int32)
    mask = validity.astype(jnp.float32)[:, :, None]

    def halos(block, axis, count):
        low = lax.ppermute(block, axis, [(i, i + 1) for i in range(count - 1)])
        high = lax.ppermute(block, axis, [(i + 1, i) for i in range(count - 1)])
        return low, high

    def shifted(block, k):
        return lax.ppermute(block, "af", [(i, (i + k) % af) for i in range(af)])

    def swapped(block):
        return lax.ppermute(block, "sx", [(i, i ^ 1) for i in range(sx)])

    beamed, traded = [], []
    masked = [sky_maps[:, :, h * width : (h + 1) * width] * mask for h in range(2)]
    around = [halos(m, "sx", sx) for m in masked]
    for h in range(2):
        smoothed = beam(around[h][0], masked[h], around[h][1], row_taps.T, h)
        smoothed = smoothed.reshape(cols_here, rows_here, width)
        low, high = halos(smoothed, "sy", sy)
        spectra = beam(low, smoothed, high, column_taps.T, h, init_loadings.T)
        spectra = spectra.reshape(af, pixels + n, width)
        beamed.append(spectra)
        traded.append(lax.all_to_all(spectra, "af", 0, 0))
    even, odd = traded

    theirs, partial, hi, lo = moments(place, even, odd, pixels)
    partial = partial + swapped(theirs)
    inverse0, weight0 = first_weights(even, odd, n)
    piece = partial[0]
    for k in range(1, af):
        piece = piece + shifted(partial[k], k)
    piece, inverse0, weight0 = lax.optimization_barrier((piece, inverse0, weight0))
    ranks = sx * sy // 2
    groups = [[s * sy + t for s in range(c, sx, 2) for t in range(sy)] for c in range(2)]
    shape = piece.shape
    pieces = piece.reshape(ranks, -1, shape[1])
    pieces = lax.all_to_all(pieces, ("sx", "sy"), 0, 0, axis_index_groups=groups)
    owned = jnp.sum(pieces, axis=0)
    pieces = lax.all_to_all(
        jnp.broadcast_to(owned[None], pieces.shape), ("sx", "sy"), 0, 0, axis_index_groups=groups
    )
    piece = pieces.reshape(shape)
    mine = [piece] + [shifted(piece, k) for k in range(1, af)]
    other = [swapped(x) for x in mine]

    loads_here, noise, latent = fit(
        place, mine + other, inverse0, weight0, hi, lo, float(pixels_here * sx * sy)
    )
    latents = [latent] + [shifted(latent, k) for k in range(1, af)]
    cleaned = clean(place, beamed[0], beamed[1], latents, loads_here)
    return cleaned.reshape(rows_here, cols_here, freqs_here), loads_here.T, noise.reshape(())


def solution(mesh):
    placed = (P("sx", "sy", "af"), P("sx", "sy"), P("af", None), P("af", None), P("af", None))
    return jax.shard_map(
        body,
        mesh=mesh,
        in_specs=placed,
        out_specs=(P("sx", "sy", "af"), P("af", None), P()),
        check_vma=False,
    )
```

time: 1610 us -> 190 us (0.12)
  waiting for transfers between devices: 1020 us -> 55.3 us
  blocking collectives: 342 us -> 39.3 us
  matrix products: 98 us -> 0 us
  other arithmetic: 78.2 us -> 2.51 us
  Pallas kernels: 0 us -> 48.6 us
  local copies, waits for them, and re-layouts: 25.8 us -> 1.93 us
  between operations: 23.1 us -> 2.07 us
  starting transfers between devices: 19.2 us -> 39.2 us
    psum x4 -> x0, waiting for transfers between devices: 962 us -> none  [body(): lax.psum((contract_rows(pixel_rows, latent), contract_rows(latent, latent...]
    psum x4 -> x0, blocking collectives: 330 us -> none  [body(): lax.psum((contract_rows(pixel_rows, latent), contract_rows(latent, latent...]
    dot_general x69 -> x0, matrix products: 96 us -> none  [the longest x8 31.5 us: add_block(): jnp.einsum('icf,fio->ocf', slab_part, band_matrix, precision=HIGHEST_PREC...]
    another operation x45 -> x1, other arithmetic: 62.8 us -> 0.08 us  [body(): jnp.stack([lax.rem(lax.axis_index('sx'), 2), lax.axis_index('af')])]
    pallas_call x0 -> x9, Pallas kernels: none -> 48.6 us  [call(): pl.pallas_call(kernel, out_shape=outs, in_specs=specs, out_specs=[fast] *...]
    all_to_all x0 -> x2, blocking collectives: none -> 39.3 us  [the longest x1 22.9 us: body(): lax.all_to_all(pieces, ('sx', 'sy'), 0, 0, axis_index_groups=groups)]
    ppermute x4 -> x22, starting transfers between devices: 10.6 us -> 32.3 us  [the longest x4 12.3 us: halos(): low = lax.ppermute(block, axis, [(i, i + 1) for i in range(count - 1)])]
    ppermute x4 -> x22, waiting for transfers between devices: 38.2 us -> 41 us  [the longest x9 28 us: shifted(): return lax.ppermute(block, 'af', [(i, (i + k) % af) for i in range(af)])]
  transfers between devices with their start and end apart: 10 -> 24, of which waited for: 10 -> 14; matrix products, arithmetic and copies ran while one was open for 1% -> 0% of each run, Pallas kernels for 0% -> 8%
where the time goes in v2:
time: 190 us; the launch traced here: 189 us
  waiting for transfers between devices  55.3 us (29%)
  Pallas kernels  48.6 us (26%)
  blocking collectives  39.3 us (21%)
  starting transfers between devices  39.2 us (21%)
  other arithmetic  2.51 us (1%)
  between operations  2.07 us (1%)
  local copies, waits for them, and re-layouts  1.93 us (1%)
    pallas_call x9, Pallas kernels, call(): pl.pallas_call(kernel, out_shape=outs, in_specs=specs, out_specs=[fast] *...  48.6 us
    ppermute x9, waiting for transfers between devices, shifted(): return lax.ppermute(block, 'af', [(i, (i + k) % af) for i in range(af)])  28 us
    all_to_all x1, blocking collectives, body(): lax.all_to_all(pieces, ('sx', 'sy'), 0, 0, axis_index_groups=groups)  22.9 us
    all_to_all x1, blocking collectives, body(): lax.all_to_all(jnp.broadcast_to(owned[None], pieces.shape), ('sx', 'sy'),...  16.4 us
    all_to_all x2, waiting for transfers between devices, body(): traded.append(lax.all_to_all(spectra, 'af', 0, 0))  14.2 us
    ppermute x4, starting transfers between devices, halos(): low = lax.ppermute(block, axis, [(i, i + 1) for i in range(count - 1)])  12.3 us
    ppermute x9, starting transfers between devices, shifted(): return lax.ppermute(block, 'af', [(i, (i + k) % af) for i in range(af)])  11 us
    ppermute x4, starting transfers between devices, halos(): high = lax.ppermute(block, axis, [(i + 1, i) for i in range(count - 1)])  8.86 us
  transfers between devices with their start and end apart: 24, of which 14 were waited for; matrix products, arithmetic and copies ran while one was open for 0% of the time, Pallas kernels for 8%

profile of v2, /device:TPU:32, one launch (start us, length us, event | category | flops | bytes accessed | tf_op | source)
XLA Modules:
  0.0 188.9 jit_solution(4545949115434400678)
XLA Ops:
  4.1 3.1 %collective-permute-start.4 = (f32[32,32,128]{2,1,0:T(8,128)S(1)}, f32[32,32,128]{2,1,0:T(8,128)S(1)}, u32[]{:S(2)}, u32[]{:S(2)}) collective-permute-start(f32[32,32,128]{2,1,0:T(8,128)S(1)} %get-tuple-element.28.own), channel_id=1, source_target_pairs={{0,32},{32,64},{64,96},{96,128},{128,160},{160,192},{192,224},{1,3... | collective-permute-start | bytes 1572872 | tf_op jit(solution)/shard_map/ppermute | solution.py:320
  8.5 3.7 %collective-permute-start = (f32[32,32,128]{2,1,0:T(8,128)S(1)}, f32[32,32,128]{2,1,0:T(8,128)S(1)}, u32[]{:S(2)}, u32[]{:S(2)}) collective-permute-start(f32[32,32,128]{2,1,0:T(8,128)S(1)} %get-tuple-element.29.own), channel_id=1, source_target_pairs={{0,32},{32,64},{64,96},{96,128},{128,160},{160,192},{192,224},{1,3... | collective-permute-start | bytes 1572872 | tf_op jit(solution)/shard_map/ppermute | solution.py:320
  12.3 2.4 %beam.6 = f32[4,8,32,128]{3,2,1,0:T(8,128)S(1)} custom-call(f32[32,32,128]{2,1,0:T(8,128)S(1)} %collective-permute-done.4.low, f32[32,32,128]{2,1,0:T(8,128)S(1)} %get-tuple-element.28.own, f32[32,32,128]{2,1,0:T(8,128)S(1)} %collective-permute-done.5.high, f32[65,256]{1,0:T(8,128)S(1)} %bitcast.34), custom_call_target="tpu_custom_call" | custom-call | tf_op jit(solution)/shard_map/beam/pallas_call | solution.py:30
  14.7 3.2 %collective-permute-start.7 = (f32[32,32,128]{2,1,0:T(8,128)S(1)}, f32[32,32,128]{2,1,0:T(8,128)S(1)}, u32[]{:S(2)}, u32[]{:S(2)}) collective-permute-start(f32[32,32,128]{2,1,0:T(8,128)S(1)} %bitcast.28), channel_id=1, source_target_pairs={{4,0},{8,4},{12,8},{16,12},{20,16},{24,20},{28,24},{5,1},{9,5},{13... | collective-permute-start | bytes 1572872 | tf_op jit(solution)/shard_map/ppermute | solution.py:321
  17.8 2.8 %collective-permute-start.6 = (f32[32,32,128]{2,1,0:T(8,128)S(1)}, f32[32,32,128]{2,1,0:T(8,128)S(1)}, u32[]{:S(2)}, u32[]{:S(2)}) collective-permute-start(f32[32,32,128]{2,1,0:T(8,128)S(1)} %bitcast.29), channel_id=1, source_target_pairs={{0,4},{4,8},{8,12},{12,16},{16,20},{20,24},{24,28},{1,5},{5,9},{9,... | collective-permute-start | bytes 1572872 | tf_op jit(solution)/shard_map/ppermute | solution.py:320
  20.7 2.3 %beam.4 = f32[4,8,32,128]{3,2,1,0:T(8,128)S(1)} custom-call(f32[32,32,128]{2,1,0:T(8,128)S(1)} %collective-permute-done.low, f32[32,32,128]{2,1,0:T(8,128)S(1)} %get-tuple-element.29.own, f32[32,32,128]{2,1,0:T(8,128)S(1)} %collective-permute-done.1.high, f32[65,256]{1,0:T(8,128)S(1)} %bitcast.35), custom_call_target="tpu_custom_call" | custom-call | tf_op jit(solution)/shard_map/beam/pallas_call | solution.py:30
  23.0 3.1 %collective-permute-start.3 = (f32[32,32,128]{2,1,0:T(8,128)S(1)}, f32[32,32,128]{2,1,0:T(8,128)S(1)}, u32[]{:S(2)}, u32[]{:S(2)}) collective-permute-start(f32[32,32,128]{2,1,0:T(8,128)S(1)} %bitcast.31), channel_id=1, source_target_pairs={{4,0},{8,4},{12,8},{16,12},{20,16},{24,20},{28,24},{5,1},{9,5},{13... | collective-permute-start | bytes 1572872 | tf_op jit(solution)/shard_map/ppermute | solution.py:321
  26.1 2.8 %collective-permute-start.2 = (f32[32,32,128]{2,1,0:T(8,128)S(1)}, f32[32,32,128]{2,1,0:T(8,128)S(1)}, u32[]{:S(2)}, u32[]{:S(2)}) collective-permute-start(f32[32,32,128]{2,1,0:T(8,128)S(1)} %bitcast.32), channel_id=1, source_target_pairs={{0,4},{4,8},{8,12},{12,16},{16,20},{20,24},{24,28},{1,5},{5,9},{9,... | collective-permute-start | bytes 1572872 | tf_op jit(solution)/shard_map/ppermute | solution.py:320
  30.1 4.0 %collective-permute-done.6.low = f32[32,32,128]{2,1,0:T(8,128)S(1)} collective-permute-done((f32[32,32,128]{2,1,0:T(8,128)S(1)}, f32[32,32,128]{2,1,0:T(8,128)S(1)}, u32[]{:S(2)}, u32[]{:S(2)}) %collective-permute-start.6) | collective-permute-done | bytes 524320 | tf_op jit(solution)/shard_map/ppermute | solution.py:320
  34.1 3.2 %beam.7 = f32[4,9,32,128]{3,2,1,0:T(8,128)} custom-call(f32[32,32,128]{2,1,0:T(8,128)S(1)} %collective-permute-done.6.low, f32[32,32,128]{2,1,0:T(8,128)S(1)} %bitcast.30, f32[32,32,128]{2,1,0:T(8,128)S(1)} %collective-permute-done.7.high, f32[65,256]{1,0:T(8,128)S(1)} %bitcast.36, f32[32,256]{1,0:T(8,128)S(1)} %bitcast.38), custom_call_target="tpu_custom_call" | custom-call | tf_op jit(solution)/shard_map/beam/pallas_call | solution.py:30
  37.3 3.5 %all-to-all-start.1 = ((f32[4,288,128]{2,1,0:T(8,128)}), f32[4,288,128]{2,1,0:T(8,128)S(1)}, u32[]{:S(2)}, u32[]{:S(2)}) async-start(f32[4,288,128]{2,1,0:T(8,128)} %bitcast.8.refs_6_), calls=%async_computation.1 | async-start | bytes 1179648 | tf_op jit(solution)/shard_map/all_to_all | solution.py:340
  41.3 4.0 %collective-permute-done.2.low = f32[32,32,128]{2,1,0:T(8,128)S(1)} collective-permute-done((f32[32,32,128]{2,1,0:T(8,128)S(1)}, f32[32,32,128]{2,1,0:T(8,128)S(1)}, u32[]{:S(2)}, u32[]{:S(2)}) %collective-permute-start.2) | collective-permute-done | bytes 524320 | tf_op jit(solution)/shard_map/ppermute | solution.py:320
  45.3 3.1 %beam.5 = f32[4,9,32,128]{3,2,1,0:T(8,128)} custom-call(f32[32,32,128]{2,1,0:T(8,128)S(1)} %collective-permute-done.2.low, f32[32,32,128]{2,1,0:T(8,128)S(1)} %bitcast.33, f32[32,32,128]{2,1,0:T(8,128)S(1)} %collective-permute-done.3.high, f32[65,256]{1,0:T(8,128)S(1)} %bitcast.37, f32[32,256]{1,0:T(8,128)S(1)} %bitcast.39), custom_call_target="tpu_custom_call" | custom-call | tf_op jit(solution)/shard_map/beam/pallas_call | solution.py:30
  48.5 3.6 %all-to-all-done.1.refs_1_.odd = f32[4,288,128]{2,1,0:T(8,128)S(1)} async-done(((f32[4,288,128]{2,1,0:T(8,128)}), f32[4,288,128]{2,1,0:T(8,128)S(1)}, u32[]{:S(2)}, u32[]{:S(2)}) %all-to-all-start.1) | async-done | bytes 589856 | tf_op jit(solution)/shard_map/all_to_all | solution.py:340
  52.1 3.5 %all-to-all-start = ((f32[4,288,128]{2,1,0:T(8,128)}), f32[4,288,128]{2,1,0:T(8,128)S(1)}, u32[]{:S(2)}, u32[]{:S(2)}) async-start(f32[4,288,128]{2,1,0:T(8,128)} %bitcast.6.refs_5_), calls=%async_computation | async-start | bytes 1179648 | tf_op jit(solution)/shard_map/all_to_all | solution.py:340
  55.7 10.6 %all-to-all-done.refs_0_.even = f32[4,288,128]{2,1,0:T(8,128)S(1)} async-done(((f32[4,288,128]{2,1,0:T(8,128)}), f32[4,288,128]{2,1,0:T(8,128)S(1)}, u32[]{:S(2)}, u32[]{:S(2)}) %all-to-all-start) | async-done | bytes 589856 | tf_op jit(solution)/shard_map/all_to_all | solution.py:340
  69.2 1.7 collective-permute-done.8
  71.7 2.7 %collective-permute-start.11 = (f32[128,640]{1,0:T(8,128)S(1)}, f32[128,640]{1,0:T(8,128)S(1)}, u32[]{:S(2)}, u32[]{:S(2)}) collective-permute-start(f32[128,640]{1,0:T(8,128)S(1)} %get-tuple-element.26), channel_id=1, source_target_pairs={{0,3},{1,0},{2,1},{3,2},{4,7},{5,4},{6,5},{7,6},{8,11},{9,8},{10,9... | collective-permute-start | bytes 983048 | tf_op jit(solution)/shard_map/ppermute | solution.py:325
  74.4 2.8 %first.1 = (f32[32,32]{1,0:T(8,128)S(1)}, f32[32,1024]{1,0:T(8,128)S(1)}) custom-call(f32[4,288,128]{2,1,0:T(8,128)S(1)} %all-to-all-done.refs_0_.even, f32[4,288,128]{2,1,0:T(8,128)S(1)} %all-to-all-done.1.refs_1_.odd), custom_call_target="tpu_custom_call" | custom-call | tf_op jit(solution)/shard_map/first/pallas_call | solution.py:30
  77.2 11.9 %collective-permute-done.9 = f32[128,640]{1,0:T(8,128)S(1)} collective-permute-done((f32[128,640]{1,0:T(8,128)S(1)}, f32[128,640]{1,0:T(8,128)S(1)}, u32[]{:S(2)}, u32[]{:S(2)}) %collective-permute-start.9) | collective-permute-done | bytes 327712 | tf_op jit(solution)/shard_map/ppermute | solution.py:325
  89.3 22.9 %all_to_all.20 = f32[32,4,640]{2,1,0:T(4,128)S(1)} all-to-all(f32[32,4,640]{2,1,0:T(4,128)S(1)} %reshape.36), channel_id=1, replica_groups={{0,4,8,12,16,20,24,28,64,68,72,76,80,84,88,92,128,132,136,140,144,148,1..., dimensions={0} | all-to-all | bytes 655360 | tf_op jit(solution)/shard_map/all_to_all | solution.py:354
  112.4 16.4 %all_to_all.21 = f32[32,4,640]{2,1,0:T(4,128)S(1)} all-to-all(f32[32,4,640]{2,1,0:T(4,128)S(1)} %broadcast_in_dim.2), channel_id=1, replica_groups={{0,4,8,12,16,20,24,28,64,68,72,76,80,84,88,92,128,132,136,140,144,148,1..., dimensions={0} | all-to-all | bytes 655360 | tf_op jit(solution)/shard_map/all_to_all | solution.py:356
  128.9 2.0 %collective-permute-start.14 = (f32[128,640]{1,0:T(8,128)S(1)}, f32[128,640]{1,0:T(8,128)S(1)}, u32[]{:S(2)}, u32[]{:S(2)}) collective-permute-start(f32[128,640]{1,0:T(8,128)S(1)} %reshape.37.refs_0_), channel_id=1, source_target_pairs={{0,3},{1,0},{2,1},{3,2},{4,7},{5,4},{6,5},{7,6},{8,11},{9,8},{10,9... | collective-permute-start | bytes 983048 | tf_op jit(solution)/shard_map/ppermute | solution.py:325
  130.9 1.8 collective-permute-start.13
  132.8 6.2 %collective-permute-done.14.refs_3_ = f32[128,640]{1,0:T(8,128)S(1)} collective-permute-done((f32[128,640]{1,0:T(8,128)S(1)}, f32[128,640]{1,0:T(8,128)S(1)}, u32[]{:S(2)}, u32[]{:S(2)}) %collective-permute-start.14) | collective-permute-done | bytes 327712 | tf_op jit(solution)/shard_map/ppermute | solution.py:325
  138.9 2.0 %collective-permute-done.13.refs_2_ = f32[128,640]{1,0:T(8,128)S(1)} collective-permute-done((f32[128,640]{1,0:T(8,128)S(1)}, f32[128,640]{1,0:T(8,128)S(1)}, u32[]{:S(2)}, u32[]{:S(2)}) %collective-permute-start.13) | collective-permute-done | bytes 327712 | tf_op jit(solution)/shard_map/ppermute | solution.py:325
  140.9 3.4 %collective-permute-done.12.refs_1_ = f32[128,640]{1,0:T(8,128)S(1)} collective-permute-done((f32[128,640]{1,0:T(8,128)S(1)}, f32[128,640]{1,0:T(8,128)S(1)}, u32[]{:S(2)}, u32[]{:S(2)}) %collective-permute-start.12) | collective-permute-done | bytes 327712 | tf_op jit(solution)/shard_map/ppermute | solution.py:325
  144.4 1.6 collective-permute-done.16.refs_5_
  146.0 30.3 %fit.1 = (f32[32,256]{1,0:T(8,128)S(1)}, f32[1,1]{1,0:T(1,128)S(1)}, f32[32,256]{1,0:T(8,128)S(1)}) custom-call(s32[2]{0:T(128)S(1)} %pad_add_fusion.place, f32[128,640]{1,0:T(8,128)S(1)} %reshape.37.refs_0_, f32[128,640]{1,0:T(8,128)S(1)} %collective-permute-done.12.refs_1_, f32[128,640]{1,0:T(8,128)S(1)} %collective-permute-done.13.refs_2_, ...), custom_call_target="tpu_custom_call" | custom-call | tf_op jit(solution)/shard_map/fit/pallas_call | solution.py:30
  176.3 2.0 %collective-permute-start.21 = (f32[32,256]{1,0:T(8,128)S(1)}, f32[32,256]{1,0:T(8,128)S(1)}, u32[]{:S(2)}, u32[]{:S(2)}) collective-permute-start(f32[32,256]{1,0:T(8,128)S(1)} %get-tuple-element.22.refs_0_), channel_id=1, source_target_pairs={{0,3},{1,0},{2,1},{3,2},{4,7},{5,4},{6,5},{7,6},{8,11},{9,8},{10,9... | collective-permute-start | bytes 98312 | tf_op jit(solution)/shard_map/ppermute | solution.py:325
  178.3 1.8 collective-permute-start.20
  180.8 3.0 %collective-permute-done.20.refs_2_ = f32[32,256]{1,0:T(8,128)S(1)} collective-permute-done((f32[32,256]{1,0:T(8,128)S(1)}, f32[32,256]{1,0:T(8,128)S(1)}, u32[]{:S(2)}, u32[]{:S(2)}) %collective-permute-start.20) | collective-permute-done | bytes 32800 | tf_op jit(solution)/shard_map/ppermute | solution.py:325
  (45 shorter events, 15.5 us)
Async XLA Ops:
  0.6 11.6 %copy-start = (f32[256,65]{0,1:T(8,128)S(1)}, f32[256,65]{0,1:T(8,128)}, u32[]{:S(2)}) copy-start(f32[256,65]{0,1:T(8,128)} %param.7) | copy-start | bytes 199684
  2.8 9.4 %collective-permute-start.5 = (f32[32,32,128]{2,1,0:T(8,128)S(1)}, f32[32,32,128]{2,1,0:T(8,128)S(1)}, u32[]{:S(2)}, u32[]{:S(2)}) collective-permute-start(f32[32,32,128]{2,1,0:T(8,128)S(1)} %get-tuple-element.28.own), channel_id=1, source_target_pairs={{32,0},{64,32},{96,64},{128,96},{160,128},{192,160},{224,192},{33,... | collective-permute-start | bytes 1572872 | tf_op jit(solution)/shard_map/ppermute | solution.py:321
  4.1 8.1 %collective-permute-start.4 = (f32[32,32,128]{2,1,0:T(8,128)S(1)}, f32[32,32,128]{2,1,0:T(8,128)S(1)}, u32[]{:S(2)}, u32[]{:S(2)}) collective-permute-start(f32[32,32,128]{2,1,0:T(8,128)S(1)} %get-tuple-element.28.own), channel_id=1, source_target_pairs={{0,32},{32,64},{64,96},{96,128},{128,160},{160,192},{192,224},{1,3... | collective-permute-start | bytes 1572872 | tf_op jit(solution)/shard_map/ppermute | solution.py:320
  7.2 13.5 %collective-permute-start.1 = (f32[32,32,128]{2,1,0:T(8,128)S(1)}, f32[32,32,128]{2,1,0:T(8,128)S(1)}, u32[]{:S(2)}, u32[]{:S(2)}) collective-permute-start(f32[32,32,128]{2,1,0:T(8,128)S(1)} %get-tuple-element.29.own), channel_id=1, source_target_pairs={{32,0},{64,32},{96,64},{128,96},{160,128},{192,160},{224,192},{33,... | collective-permute-start | bytes 1572872 | tf_op jit(solution)/shard_map/ppermute | solution.py:321
  8.5 12.2 %collective-permute-start = (f32[32,32,128]{2,1,0:T(8,128)S(1)}, f32[32,32,128]{2,1,0:T(8,128)S(1)}, u32[]{:S(2)}, u32[]{:S(2)}) collective-permute-start(f32[32,32,128]{2,1,0:T(8,128)S(1)} %get-tuple-element.29.own), channel_id=1, source_target_pairs={{0,32},{32,64},{64,96},{96,128},{128,160},{160,192},{192,224},{1,3... | collective-permute-start | bytes 1572872 | tf_op jit(solution)/shard_map/ppermute | solution.py:320
  14.6 19.5 %copy-start.1 = (f32[256,65]{0,1:T(8,128)S(1)}, f32[256,65]{0,1:T(8,128)}, u32[]{:S(2)}) copy-start(f32[256,65]{0,1:T(8,128)} %param.8) | copy-start | bytes 199684
  14.6 19.5 %copy-start.2 = (f32[256,32]{0,1:T(8,128)S(1)}, f32[256,32]{0,1:T(8,128)}, u32[]{:S(2)}) copy-start(f32[256,32]{0,1:T(8,128)} %param.9) | copy-start | bytes 98308
  14.7 15.4 %collective-permute-start.7 = (f32[32,32,128]{2,1,0:T(8,128)S(1)}, f32[32,32,128]{2,1,0:T(8,128)S(1)}, u32[]{:S(2)}, u32[]{:S(2)}) collective-permute-start(f32[32,32,128]{2,1,0:T(8,128)S(1)} %bitcast.28), channel_id=1, source_target_pairs={{4,0},{8,4},{12,8},{16,12},{20,16},{24,20},{28,24},{5,1},{9,5},{13... | collective-permute-start | bytes 1572872 | tf_op jit(solution)/shard_map/ppermute | solution.py:321
  17.8 16.3 %collective-permute-start.6 = (f32[32,32,128]{2,1,0:T(8,128)S(1)}, f32[32,32,128]{2,1,0:T(8,128)S(1)}, u32[]{:S(2)}, u32[]{:S(2)}) collective-permute-start(f32[32,32,128]{2,1,0:T(8,128)S(1)} %bitcast.29), channel_id=1, source_target_pairs={{0,4},{4,8},{8,12},{12,16},{16,20},{20,24},{24,28},{1,5},{5,9},{9,... | collective-permute-start | bytes 1572872 | tf_op jit(solution)/shard_map/ppermute | solution.py:320
  23.0 18.3 %collective-permute-start.3 = (f32[32,32,128]{2,1,0:T(8,128)S(1)}, f32[32,32,128]{2,1,0:T(8,128)S(1)}, u32[]{:S(2)}, u32[]{:S(2)}) collective-permute-start(f32[32,32,128]{2,1,0:T(8,128)S(1)} %bitcast.31), channel_id=1, source_target_pairs={{4,0},{8,4},{12,8},{16,12},{20,16},{24,20},{28,24},{5,1},{9,5},{13... | collective-permute-start | bytes 1572872 | tf_op jit(solution)/shard_map/ppermute | solution.py:321
  26.1 19.2 %collective-permute-start.2 = (f32[32,32,128]{2,1,0:T(8,128)S(1)}, f32[32,32,128]{2,1,0:T(8,128)S(1)}, u32[]{:S(2)}, u32[]{:S(2)}) collective-permute-start(f32[32,32,128]{2,1,0:T(8,128)S(1)} %bitcast.32), channel_id=1, source_target_pairs={{0,4},{4,8},{8,12},{12,16},{16,20},{20,24},{24,28},{1,5},{5,9},{9,... | collective-permute-start | bytes 1572872 | tf_op jit(solution)/shard_map/ppermute | solution.py:320
  37.3 14.8 %all-to-all-start.1 = ((f32[4,288,128]{2,1,0:T(8,128)}), f32[4,288,128]{2,1,0:T(8,128)S(1)}, u32[]{:S(2)}, u32[]{:S(2)}) async-start(f32[4,288,128]{2,1,0:T(8,128)} %bitcast.8.refs_6_), calls=%async_computation.1 | async-start | bytes 1179648 | tf_op jit(solution)/shard_map/all_to_all | solution.py:340
  52.1 14.2 %all-to-all-start = ((f32[4,288,128]{2,1,0:T(8,128)}), f32[4,288,128]{2,1,0:T(8,128)S(1)}, u32[]{:S(2)}, u32[]{:S(2)}) async-start(f32[4,288,128]{2,1,0:T(8,128)} %bitcast.6.refs_5_), calls=%async_computation | async-start | bytes 1179648 | tf_op jit(solution)/shard_map/all_to_all | solution.py:340
  67.8 3.1 %collective-permute-start.8 = (f32[4,128,640]{2,1,0:T(8,128)S(1)}, f32[4,128,640]{2,1,0:T(8,128)S(1)}, u32[]{:S(2)}, u32[]{:S(2)}) collective-permute-start(f32[4,128,640]{2,1,0:T(8,128)S(1)} %get-tuple-element.16), channel_id=1, source_target_pairs={{0,32},{32,0},{64,96},{96,64},{128,160},{160,128},{192,224},{224,1... | collective-permute-start | bytes 3932168 | tf_op jit(solution)/shard_map/ppermute | solution.py:328
  71.1 18.1 %collective-permute-start.9 = (f32[128,640]{1,0:T(8,128)S(1)}, f32[128,640]{1,0:T(8,128)S(1)}, u32[]{:S(2)}, u32[]{:S(2)}) collective-permute-start(f32[128,640]{1,0:T(8,128)S(1)} %get-tuple-element.25), channel_id=1, source_target_pairs={{0,1},{1,2},{2,3},{3,0},{4,5},{5,6},{6,7},{7,4},{8,9},{9,10},{10,1... | collective-permute-start | bytes 983048 | tf_op jit(solution)/shard_map/ppermute | solution.py:325
  71.7 17.4 %collective-permute-start.11 = (f32[128,640]{1,0:T(8,128)S(1)}, f32[128,640]{1,0:T(8,128)S(1)}, u32[]{:S(2)}, u32[]{:S(2)}) collective-permute-start(f32[128,640]{1,0:T(8,128)S(1)} %get-tuple-element.26), channel_id=1, source_target_pairs={{0,3},{1,0},{2,1},{3,2},{4,7},{5,4},{6,5},{7,6},{8,11},{9,8},{10,9... | collective-permute-start | bytes 983048 | tf_op jit(solution)/shard_map/ppermute | solution.py:325
  74.4 14.8 %collective-permute-start.10 = (f32[128,640]{1,0:T(8,128)S(1)}, f32[128,640]{1,0:T(8,128)S(1)}, u32[]{:S(2)}, u32[]{:S(2)}) collective-permute-start(f32[128,640]{1,0:T(8,128)S(1)} %get-tuple-element.27), channel_id=1, source_target_pairs={{0,2},{1,3},{2,0},{3,1},{4,6},{5,7},{6,4},{7,5},{8,10},{9,11},{10,... | collective-permute-start | bytes 983048 | tf_op jit(solution)/shard_map/ppermute | solution.py:325
  128.9 10.0 %collective-permute-start.14 = (f32[128,640]{1,0:T(8,128)S(1)}, f32[128,640]{1,0:T(8,128)S(1)}, u32[]{:S(2)}, u32[]{:S(2)}) collective-permute-start(f32[128,640]{1,0:T(8,128)S(1)} %reshape.37.refs_0_), channel_id=1, source_target_pairs={{0,3},{1,0},{2,1},{3,2},{4,7},{5,4},{6,5},{7,6},{8,11},{9,8},{10,9... | collective-permute-start | bytes 983048 | tf_op jit(solution)/shard_map/ppermute | solution.py:325
  130.9 10.0 %collective-permute-start.13 = (f32[128,640]{1,0:T(8,128)S(1)}, f32[128,640]{1,0:T(8,128)S(1)}, u32[]{:S(2)}, u32[]{:S(2)}) collective-permute-start(f32[128,640]{1,0:T(8,128)S(1)} %reshape.37.refs_0_), channel_id=1, source_target_pairs={{0,2},{1,3},{2,0},{3,1},{4,6},{5,7},{6,4},{7,5},{8,10},{9,11},{10,... | collective-permute-start | bytes 983048 | tf_op jit(solution)/shard_map/ppermute | solution.py:325
  132.8 11.6 %collective-permute-start.12 = (f32[128,640]{1,0:T(8,128)S(1)}, f32[128,640]{1,0:T(8,128)S(1)}, u32[]{:S(2)}, u32[]{:S(2)}) collective-permute-start(f32[128,640]{1,0:T(8,128)S(1)} %reshape.37.refs_0_), channel_id=1, source_target_pairs={{0,1},{1,2},{2,3},{3,0},{4,5},{5,6},{6,7},{7,4},{8,9},{9,10},{10,1... | collective-permute-start | bytes 983048 | tf_op jit(solution)/shard_map/ppermute | solution.py:325
  132.8 11.6 %collective-permute-start.15 = (f32[128,640]{1,0:T(8,128)S(1)}, f32[128,640]{1,0:T(8,128)S(1)}, u32[]{:S(2)}, u32[]{:S(2)}) collective-permute-start(f32[128,640]{1,0:T(8,128)S(1)} %reshape.37.refs_0_), channel_id=1, source_target_pairs={{0,32},{32,0},{64,96},{96,64},{128,160},{160,128},{192,224},{224,1... | collective-permute-start | bytes 983048 | tf_op jit(solution)/shard_map/ppermute | solution.py:328
  138.9 5.4 %collective-permute-start.18 = (f32[128,640]{1,0:T(8,128)S(1)}, f32[128,640]{1,0:T(8,128)S(1)}, u32[]{:S(2)}, u32[]{:S(2)}) collective-permute-start(f32[128,640]{1,0:T(8,128)S(1)} %collective-permute-done.14.refs_3_), channel_id=1, source_target_pairs={{0,32},{32,0},{64,96},{96,64},{128,160},{160,128},{192,224},{224,1... | collective-permute-start | bytes 983048 | tf_op jit(solution)/shard_map/ppermute | solution.py:328
  140.9 3.4 %collective-permute-start.17 = (f32[128,640]{1,0:T(8,128)S(1)}, f32[128,640]{1,0:T(8,128)S(1)}, u32[]{:S(2)}, u32[]{:S(2)}) collective-permute-start(f32[128,640]{1,0:T(8,128)S(1)} %collective-permute-done.13.refs_2_), channel_id=1, source_target_pairs={{0,32},{32,0},{64,96},{96,64},{128,160},{160,128},{192,224},{224,1... | collective-permute-start | bytes 983048 | tf_op jit(solution)/shard_map/ppermute | solution.py:328
  144.4 1.6 collective-permute-start.16
  176.3 4.5 %collective-permute-start.21 = (f32[32,256]{1,0:T(8,128)S(1)}, f32[32,256]{1,0:T(8,128)S(1)}, u32[]{:S(2)}, u32[]{:S(2)}) collective-permute-start(f32[32,256]{1,0:T(8,128)S(1)} %get-tuple-element.22.refs_0_), channel_id=1, source_target_pairs={{0,3},{1,0},{2,1},{3,2},{4,7},{5,4},{6,5},{7,6},{8,11},{9,8},{10,9... | collective-permute-start | bytes 98312 | tf_op jit(solution)/shard_map/ppermute | solution.py:325
  178.3 5.4 %collective-permute-start.20 = (f32[32,256]{1,0:T(8,128)S(1)}, f32[32,256]{1,0:T(8,128)S(1)}, u32[]{:S(2)}, u32[]{:S(2)}) collective-permute-start(f32[32,256]{1,0:T(8,128)S(1)} %get-tuple-element.22.refs_0_), channel_id=1, source_target_pairs={{0,2},{1,3},{2,0},{3,1},{4,6},{5,7},{6,4},{7,5},{8,10},{9,11},{10,... | collective-permute-start | bytes 98312 | tf_op jit(solution)/shard_map/ppermute | solution.py:325
  180.1 5.1 %collective-permute-start.19 = (f32[32,256]{1,0:T(8,128)S(1)}, f32[32,256]{1,0:T(8,128)S(1)}, u32[]{:S(2)}, u32[]{:S(2)}) collective-permute-start(f32[32,256]{1,0:T(8,128)S(1)} %get-tuple-element.22.refs_0_), channel_id=1, source_target_pairs={{0,1},{1,2},{2,3},{3,0},{4,5},{5,6},{6,7},{7,4},{8,9},{9,10},{10,1... | collective-permute-start | bytes 98312 | tf_op jit(solution)/shard_map/ppermute | solution.py:325

commit v3 on v2

--- a/solution.py
+++ b/solution.py
@@ -119,21 +119,33 @@
         hi, lo, out = refs
         parts = hi.shape[0] // 2
     blocks = 2 * parts
+    width = hi.shape[2]
+    half = width // 2
+    dims = (((0,), (0,)), ((), ()))
+    upper = lax.rem(place[0] + c, 2) == 0
     for k in range(parts):
         i = row_block(place, c, k, parts)
-        at = [lax.rem(i + j, blocks) for j in range(parts + 1)]
+        at = [lax.rem(i + j, blocks) for j in range(parts)]
         left = jnp.concatenate([lo[i], hi[i], hi[i]], axis=0)
         high = jnp.concatenate([hi[b] for b in at], axis=1)
         low = jnp.concatenate([lo[b] for b in at], axis=1)
         right = jnp.concatenate([high, low, high], axis=0)
-        out[k] = lax.dot_general(
-            left, right, (((0,), (0,)), ((), ())), preferred_element_type=jnp.float32
+        block = lax.dot_general(left, right, dims, preferred_element_type=jnp.float32)
+        for j in range(parts):
+            out[k, j * width : (j + 1) * width, :] = block[:, j * width : (j + 1) * width]
+        m = lax.rem(i, parts)
+        left = jnp.concatenate([lo[m], hi[m], hi[m]], axis=0)
+        left = jnp.where(upper, left[:, :half], left[:, half:])
+        m = m + parts
+        right = jnp.concatenate([hi[m], lo[m], hi[m]], axis=0)
+        out[k, parts * width :, :] = lax.dot_general(
+            left, right, dims, preferred_element_type=jnp.float32
         )
 
 
 def moments(place, even, odd, pixels):
     parts, _, width = even.shape
-    shape = (parts, width, width * (parts + 1))
+    shape = (parts, width * parts + width // 2, width)
     halves = (2 * parts, pixels, width)
     half = jnp.bfloat16
     theirs, hi, lo = call(
@@ -144,34 +156,37 @@
     return theirs, ours[0], hi, lo
 
 
+def every(tile, r):
+    return jnp.broadcast_to(tile[r : r + 1], tile.shape)
+
+
+def along(tile, k):
+    return jnp.broadcast_to(tile[:, k : k + 1], tile.shape)
+
+
 def inverse_spd(matrix):
     n = matrix.shape[0]
     lane = lax.broadcasted_iota(jnp.int32, (8, n), 1)
     row = lax.broadcasted_iota(jnp.int32, (8, n), 0)
-    unit = 1.0 / jnp.broadcast_to(matrix[0:1, 0:1], (8, n))
-    tiles = [matrix[i : i + 8] * unit for i in range(0, n, 8)]
-    for k in range(0, n, 2):
-        at, r = divmod(k, 8)
-
-        def every(tile, s):
-            return jnp.broadcast_to(tile[s : s + 1], (8, n))
-
-        left = [jnp.broadcast_to(t[:, k : k + 1], (8, n)) for t in tiles]
-        right = [jnp.broadcast_to(t[:, k + 1 : k + 2], (8, n)) for t in tiles]
-        a, b = every(left[at], r), every(right[at], r)
-        c, d = every(left[at], r + 1), every(right[at], r + 1)
-        pivot = 1.0 / (a * d - b * c)
-        inside = (lane == k) | (lane == k + 1)
-        top = jnp.where(inside, (lane == k).astype(jnp.float32), every(tiles[at], r))
-        low = jnp.where(inside, (lane == k + 1).astype(jnp.float32), every(tiles[at], r + 1))
-        first = (d * top - b * low) * pivot
-        second = (a * low - c * top) * pivot
-        tiles = [
-            jnp.where(inside, 0.0, t) - x * first - y * second
-            for t, x, y in zip(tiles, left, right)
-        ]
-        tiles[at] = jnp.where(row == r, first, jnp.where(row == r + 1, second, tiles[at]))
-    return jnp.concatenate([t * unit for t in tiles], axis=0)
+    tiles = [matrix[i : i + 8] for i in range(0, n, 8)]
+    for p in range(n // 8):
+        cols = [[along(t, 8 * p + j) for t in tiles] for j in range(8)]
+        for r in range(8):
+            k = 8 * p + r
+            top = every(tiles[p], r)
+            heads = [
+                along(top, 8 * p + j) if r == 0 else every(cols[j][p], r) for j in range(r, 8)
+            ]
+            pivot = 1.0 / heads[0]
+            first = jnp.where(lane == k, 1.0, top) * pivot
+            left = cols[r]
+            for j in range(r + 1, 8):
+                factor = heads[j - r] * pivot
+                cols[j] = [t - x * factor for t, x in zip(cols[j], left)]
+                cols[j][p] = jnp.where(row == r, factor, cols[j][p])
+            tiles = [jnp.where(lane == k, 0.0, t) - x * first for t, x in zip(tiles, left)]
+            tiles[p] = jnp.where(row == r, first, tiles[p])
+    return jnp.concatenate(tiles, axis=0)
 
 
 def total(x):
@@ -182,9 +197,30 @@
     return lax.broadcasted_iota(jnp.int32, (n, n), 0) == lax.broadcasted_iota(jnp.int32, (n, n), 1)
 
 
-def weights(loads, gram, noise):
+def parts_of(x):
+    return jnp.concatenate(split3(x), axis=0)
+
+
+def gram_of(left, right):
+    n = left.shape[0] // 3
+    grid = lax.dot_general(
+        left, right, (((1,), (1,)), ((), ())), preferred_element_type=jnp.float32
+    )
+    rows = grid[:n] + (grid[n : 2 * n] + grid[2 * n :])
+    return rows[:, :n] + (rows[:, n : 2 * n] + rows[:, 2 * n :])
+
+
+def times(matrix, right):
+    n = matrix.shape[0]
+    top, mid, low = split3(matrix)
+    left = jnp.concatenate([low, mid, top, mid, top, top], axis=1)
+    right = jnp.concatenate([right, right[: 2 * n], right[:n]], axis=0)
+    return jnp.dot(left, right, preferred_element_type=jnp.float32)
+
+
+def weights(pieces, gram, noise):
     inverse = inverse_spd(gram + jnp.where(identity(gram.shape[0]), noise, 0.0))
-    return inverse, thin(inverse, loads, ((1,), (0,)))
+    return inverse, times(inverse, pieces)
 
 
 def first_kernel(even, odd, inverse_out, weight_out):
@@ -193,8 +229,9 @@
     loads = jnp.concatenate(
         [ref[b, rows - n : rows] for b in range(even.shape[0]) for ref in (even, odd)], axis=1
     )
-    gram = contract(loads, loads, ((1,), (1,)))
-    inverse_out[...], weight_out[...] = weights(loads, gram, jnp.ones((1, 1), jnp.float32))
+    pieces = parts_of(loads)
+    gram = gram_of(pieces, pieces)
+    inverse_out[...], weight_out[...] = weights(pieces, gram, jnp.ones((1, 1), jnp.float32))
 
 
 def first_weights(even, odd, n):
@@ -202,9 +239,8 @@
     return call(first_kernel, [(n, n), (n, 2 * parts * width)], even, odd, name="first")
 
 
-def cross_of(weight, hi, mid, low):
-    n = weight.shape[0]
-    stacked = jnp.concatenate(split3(weight), axis=0)
+def cross_of(stacked, hi, mid, low):
+    n = stacked.shape[0] // 3
 
     def product(count, ref):
         return jnp.dot(stacked[: count * n], ref[...], preferred_element_type=jnp.float32)
@@ -218,39 +254,51 @@
     slots = refs[: 2 * parts]
     inverse0, weight0, map_hi, map_lo = refs[2 * parts : 2 * parts + 4]
     block_out, noise_out, lat_out, hi, mid, low, held = refs[2 * parts + 4 :]
-    width = slots[0].shape[0]
+    width = slots[0].shape[1]
     blocks = 2 * parts
     freqs = blocks * width
     n = weight0.shape[0]
     diagonal = identity(width)
     power = jnp.zeros((width, width), jnp.float32)
+
+    def place_block(i, j, block, mirror):
+        rows = pl.ds(pl.multiple_of(i * width, width), width)
+        cols = pl.ds(pl.multiple_of(j * width, width), width)
+        for dest, value in zip((hi, mid, low), split3(block)):
+            dest[rows, cols] = value
+        if mirror:
+            for dest, value in zip((hi, mid, low), split3(block.T)):
+                dest[cols, rows] = value
+
     for s, ref in enumerate(slots):
         i = row_block(place, s // parts, parts - s % parts, parts)
-        for j in range(parts + 1):
-            block = ref[:, j * width : (j + 1) * width]
-            at_row = pl.multiple_of(i * width, width)
-            at_col = pl.multiple_of(lax.rem(i + j, blocks) * width, width)
-            for dest, value in zip((hi, mid, low), split3(block)):
-                dest[pl.ds(at_row, width), pl.ds(at_col, width)] = value
-            if j == 0:
-                power = power + jnp.where(diagonal, block, 0.0)
-            elif j < parts:
-                for dest, value in zip((hi, mid, low), split3(block.T)):
-                    dest[pl.ds(at_col, width), pl.ds(at_row, width)] = value
+        for j in range(parts):
+            place_block(i, lax.rem(i + j, blocks), ref[j * width : (j + 1) * width], j > 0)
+        power = power + jnp.where(diagonal, ref[:width], 0.0)
+    upper = place[0] == 0
+    for k in range(parts):
+        m = lax.rem(place[1] + parts - k, parts)
+        ours, theirs = slots[k][parts * width :], slots[parts + k][parts * width :]
+        block = jnp.concatenate(
+            [jnp.where(upper, ours, theirs), jnp.where(upper, theirs, ours)], axis=0
+        )
+        place_block(m, m + parts, block, True)
     power = total(power)
 
     def step(_, state):
         inverse, weight, noise = state
-        cross = cross_of(weight, hi, mid, low)
-        second = contract(cross, weight, ((1,), (1,)))
-        scaled = pixel_total * noise * inverse + second
-        updated = thin(inverse_spd(scaled), cross, ((1,), (0,)))
+        stacked = parts_of(weight)
+        cross = cross_of(stacked, hi, mid, low)
+        pieces = parts_of(cross)
+        scaled = pixel_total * noise * inverse + gram_of(pieces, stacked)
+        updated = times(inverse_spd(scaled), pieces)
         held[...] = updated
-        gram = contract(updated, updated, ((1,), (1,)))
+        pieces = parts_of(updated)
+        gram = gram_of(pieces, pieces)
         noise = (power - 2.0 * total(updated * cross) + total(scaled * gram)) / (
             pixel_total * freqs
         )
-        return (*weights(updated, gram, noise), noise)
+        return (*weights(pieces, gram, noise), noise)
 
     state = (inverse0[...], weight0[...], jnp.ones((1, 1), jnp.float32))
     _, weight, noise = lax.fori_loop(0, ITERS, step, state)
@@ -350,11 +398,14 @@
     ranks = sx * sy // 2
     groups = [[s * sy + t for s in range(c, sx, 2) for t in range(sy)] for c in range(2)]
     shape = piece.shape
-    pieces = piece.reshape(ranks, -1, shape[1])
-    pieces = lax.all_to_all(pieces, ("sx", "sy"), 0, 0, axis_index_groups=groups)
-    owned = jnp.sum(pieces, axis=0)
+    pieces = piece.reshape(-1, 2, shape[1])
     pieces = lax.all_to_all(
-        jnp.broadcast_to(owned[None], pieces.shape), ("sx", "sy"), 0, 0, axis_index_groups=groups
+        pieces, ("sx", "sy"), 0, 0, axis_index_groups=groups, tiled=True
+    )
+    owned = jnp.sum(pieces.reshape(ranks, -1, 2, shape[1]), axis=0)
+    pieces = jnp.broadcast_to(owned[None], (ranks, *owned.shape)).reshape(pieces.shape)
+    pieces = lax.all_to_all(
+        pieces, ("sx", "sy"), 0, 0, axis_index_groups=groups, tiled=True
     )
     piece = pieces.reshape(shape)
     mine = [piece] + [shifted(piece, k) for k in range(1, af)]

time: 190 us -> 175 us (0.921)
  Pallas kernels: 48.6 us -> 37 us
  waiting for transfers between devices: 55.3 us -> 53.1 us
    pallas_call x9, Pallas kernels: 48.6 us -> 37 us  [call(): pl.pallas_call(kernel, out_shape=outs, in_specs=specs, out_specs=[fast] *...]
    ppermute x9, waiting for transfers between devices: 28 us -> 26 us  [shifted(): return lax.ppermute(block, 'af', [(i, (i + k) % af) for i in range(af)])]
  transfers between devices with their start and end apart: 24 -> 24, of which waited for: 14 -> 13; matrix products, arithmetic and copies ran while one was open for 0% -> 0% of each run, Pallas kernels for 8% -> 8%
where the time goes in v3:
time: 175 us; the launch traced here: 174 us
  waiting for transfers between devices  53.1 us (30%)
  starting transfers between devices  39.9 us (23%)
  blocking collectives  38 us (22%)
  Pallas kernels  37 us (21%)
  other arithmetic  2.52 us (1%)
  between operations  2.05 us (1%)
    all_to_all x2, blocking collectives, body(): lax.all_to_all(pieces, ('sx', 'sy'), 0, 0, axis_index_groups=groups, tile...  38 us
    pallas_call x9, Pallas kernels, call(): pl.pallas_call(kernel, out_shape=outs, in_specs=specs, out_specs=[fast] *...  37 us
    ppermute x9, waiting for transfers between devices, shifted(): return lax.ppermute(block, 'af', [(i, (i + k) % af) for i in range(af)])  26 us
    all_to_all x2, waiting for transfers between devices, body(): traded.append(lax.all_to_all(spectra, 'af', 0, 0))  14.2 us
    ppermute x4, starting transfers between devices, halos(): low = lax.ppermute(block, axis, [(i, i + 1) for i in range(count - 1)])  12.3 us
    ppermute x9, starting transfers between devices, shifted(): return lax.ppermute(block, 'af', [(i, (i + k) % af) for i in range(af)])  11.2 us
    ppermute x4, starting transfers between devices, halos(): high = lax.ppermute(block, axis, [(i + 1, i) for i in range(count - 1)])  8.86 us
    ppermute x4, waiting for transfers between devices, halos(): low = lax.ppermute(block, axis, [(i, i + 1) for i in range(count - 1)])  8.09 us
  transfers between devices with their start and end apart: 24, of which 13 were waited for; matrix products, arithmetic and copies ran while one was open for 0% of the time, Pallas kernels for 8%

profile of v3, /device:TPU:32, one launch (start us, length us, event | category | flops | bytes accessed | tf_op | source)
XLA Modules:
  0.0 174.3 jit_solution(6221186366172763418)
XLA Ops:
  4.1 3.1 %collective-permute-start.4 = (f32[32,32,128]{2,1,0:T(8,128)S(1)}, f32[32,32,128]{2,1,0:T(8,128)S(1)}, u32[]{:S(2)}, u32[]{:S(2)}) collective-permute-start(f32[32,32,128]{2,1,0:T(8,128)S(1)} %get-tuple-element.28.own), channel_id=1, source_target_pairs={{0,32},{32,64},{64,96},{96,128},{128,160},{160,192},{192,224},{1,3... | collective-permute-start | bytes 1572872 | tf_op jit(solution)/shard_map/ppermute | solution.py:368
  8.5 3.7 %collective-permute-start = (f32[32,32,128]{2,1,0:T(8,128)S(1)}, f32[32,32,128]{2,1,0:T(8,128)S(1)}, u32[]{:S(2)}, u32[]{:S(2)}) collective-permute-start(f32[32,32,128]{2,1,0:T(8,128)S(1)} %get-tuple-element.29.own), channel_id=1, source_target_pairs={{0,32},{32,64},{64,96},{96,128},{128,160},{160,192},{192,224},{1,3... | collective-permute-start | bytes 1572872 | tf_op jit(solution)/shard_map/ppermute | solution.py:368
  12.3 2.4 %beam.6 = f32[4,8,32,128]{3,2,1,0:T(8,128)S(1)} custom-call(f32[32,32,128]{2,1,0:T(8,128)S(1)} %collective-permute-done.4.low, f32[32,32,128]{2,1,0:T(8,128)S(1)} %get-tuple-element.28.own, f32[32,32,128]{2,1,0:T(8,128)S(1)} %collective-permute-done.5.high, f32[65,256]{1,0:T(8,128)S(1)} %bitcast.43), custom_call_target="tpu_custom_call" | custom-call | tf_op jit(solution)/shard_map/beam/pallas_call | solution.py:30
  14.7 3.2 %collective-permute-start.7 = (f32[32,32,128]{2,1,0:T(8,128)S(1)}, f32[32,32,128]{2,1,0:T(8,128)S(1)}, u32[]{:S(2)}, u32[]{:S(2)}) collective-permute-start(f32[32,32,128]{2,1,0:T(8,128)S(1)} %bitcast.32), channel_id=1, source_target_pairs={{4,0},{8,4},{12,8},{16,12},{20,16},{24,20},{28,24},{5,1},{9,5},{13... | collective-permute-start | bytes 1572872 | tf_op jit(solution)/shard_map/ppermute | solution.py:369
  17.8 2.8 %collective-permute-start.6 = (f32[32,32,128]{2,1,0:T(8,128)S(1)}, f32[32,32,128]{2,1,0:T(8,128)S(1)}, u32[]{:S(2)}, u32[]{:S(2)}) collective-permute-start(f32[32,32,128]{2,1,0:T(8,128)S(1)} %bitcast.33), channel_id=1, source_target_pairs={{0,4},{4,8},{8,12},{12,16},{16,20},{20,24},{24,28},{1,5},{5,9},{9,... | collective-permute-start | bytes 1572872 | tf_op jit(solution)/shard_map/ppermute | solution.py:368
  20.7 2.3 %beam.4 = f32[4,8,32,128]{3,2,1,0:T(8,128)S(1)} custom-call(f32[32,32,128]{2,1,0:T(8,128)S(1)} %collective-permute-done.low, f32[32,32,128]{2,1,0:T(8,128)S(1)} %get-tuple-element.29.own, f32[32,32,128]{2,1,0:T(8,128)S(1)} %collective-permute-done.1.high, f32[65,256]{1,0:T(8,128)S(1)} %bitcast.44), custom_call_target="tpu_custom_call" | custom-call | tf_op jit(solution)/shard_map/beam/pallas_call | solution.py:30
  23.0 3.1 %collective-permute-start.3 = (f32[32,32,128]{2,1,0:T(8,128)S(1)}, f32[32,32,128]{2,1,0:T(8,128)S(1)}, u32[]{:S(2)}, u32[]{:S(2)}) collective-permute-start(f32[32,32,128]{2,1,0:T(8,128)S(1)} %bitcast.35), channel_id=1, source_target_pairs={{4,0},{8,4},{12,8},{16,12},{20,16},{24,20},{28,24},{5,1},{9,5},{13... | collective-permute-start | bytes 1572872 | tf_op jit(solution)/shard_map/ppermute | solution.py:369
  26.1 2.8 %collective-permute-start.2 = (f32[32,32,128]{2,1,0:T(8,128)S(1)}, f32[32,32,128]{2,1,0:T(8,128)S(1)}, u32[]{:S(2)}, u32[]{:S(2)}) collective-permute-start(f32[32,32,128]{2,1,0:T(8,128)S(1)} %bitcast.36), channel_id=1, source_target_pairs={{0,4},{4,8},{8,12},{12,16},{16,20},{20,24},{24,28},{1,5},{5,9},{9,... | collective-permute-start | bytes 1572872 | tf_op jit(solution)/shard_map/ppermute | solution.py:368
  30.1 4.0 %collective-permute-done.6.low = f32[32,32,128]{2,1,0:T(8,128)S(1)} collective-permute-done((f32[32,32,128]{2,1,0:T(8,128)S(1)}, f32[32,32,128]{2,1,0:T(8,128)S(1)}, u32[]{:S(2)}, u32[]{:S(2)}) %collective-permute-start.6) | collective-permute-done | bytes 524320 | tf_op jit(solution)/shard_map/ppermute | solution.py:368
  34.1 3.2 %beam.7 = f32[4,9,32,128]{3,2,1,0:T(8,128)} custom-call(f32[32,32,128]{2,1,0:T(8,128)S(1)} %collective-permute-done.6.low, f32[32,32,128]{2,1,0:T(8,128)S(1)} %bitcast.34, f32[32,32,128]{2,1,0:T(8,128)S(1)} %collective-permute-done.7.high, f32[65,256]{1,0:T(8,128)S(1)} %bitcast.45, f32[32,256]{1,0:T(8,128)S(1)} %bitcast.47), custom_call_target="tpu_custom_call" | custom-call | tf_op jit(solution)/shard_map/beam/pallas_call | solution.py:30
  37.3 3.5 %all-to-all-start.1 = ((f32[4,288,128]{2,1,0:T(8,128)}), f32[4,288,128]{2,1,0:T(8,128)S(1)}, u32[]{:S(2)}, u32[]{:S(2)}) async-start(f32[4,288,128]{2,1,0:T(8,128)} %bitcast.8.refs_6_), calls=%async_computation.1 | async-start | bytes 1179648 | tf_op jit(solution)/shard_map/all_to_all | solution.py:388
  41.3 4.0 %collective-permute-done.2.low = f32[32,32,128]{2,1,0:T(8,128)S(1)} collective-permute-done((f32[32,32,128]{2,1,0:T(8,128)S(1)}, f32[32,32,128]{2,1,0:T(8,128)S(1)}, u32[]{:S(2)}, u32[]{:S(2)}) %collective-permute-start.2) | collective-permute-done | bytes 524320 | tf_op jit(solution)/shard_map/ppermute | solution.py:368
  45.3 3.1 %beam.5 = f32[4,9,32,128]{3,2,1,0:T(8,128)} custom-call(f32[32,32,128]{2,1,0:T(8,128)S(1)} %collective-permute-done.2.low, f32[32,32,128]{2,1,0:T(8,128)S(1)} %bitcast.37, f32[32,32,128]{2,1,0:T(8,128)S(1)} %collective-permute-done.3.high, f32[65,256]{1,0:T(8,128)S(1)} %bitcast.46, f32[32,256]{1,0:T(8,128)S(1)} %bitcast.48), custom_call_target="tpu_custom_call" | custom-call | tf_op jit(solution)/shard_map/beam/pallas_call | solution.py:30
  48.5 3.6 %all-to-all-done.1.refs_1_.odd = f32[4,288,128]{2,1,0:T(8,128)S(1)} async-done(((f32[4,288,128]{2,1,0:T(8,128)}), f32[4,288,128]{2,1,0:T(8,128)S(1)}, u32[]{:S(2)}, u32[]{:S(2)}) %all-to-all-start.1) | async-done | bytes 589856 | tf_op jit(solution)/shard_map/all_to_all | solution.py:388
  52.1 3.5 %all-to-all-start = ((f32[4,288,128]{2,1,0:T(8,128)}), f32[4,288,128]{2,1,0:T(8,128)S(1)}, u32[]{:S(2)}, u32[]{:S(2)}) async-start(f32[4,288,128]{2,1,0:T(8,128)} %bitcast.6.refs_5_), calls=%async_computation | async-start | bytes 1179648 | tf_op jit(solution)/shard_map/all_to_all | solution.py:388
  55.7 10.6 %all-to-all-done.refs_0_.even = f32[4,288,128]{2,1,0:T(8,128)S(1)} async-done(((f32[4,288,128]{2,1,0:T(8,128)}), f32[4,288,128]{2,1,0:T(8,128)S(1)}, u32[]{:S(2)}, u32[]{:S(2)}) %all-to-all-start) | async-done | bytes 589856 | tf_op jit(solution)/shard_map/all_to_all | solution.py:388
  66.3 1.5 moments.2
  71.6 2.7 %collective-permute-start.11 = (f32[576,128]{1,0:T(8,128)S(1)}, f32[576,128]{1,0:T(8,128)S(1)}, u32[]{:S(2)}, u32[]{:S(2)}) collective-permute-start(f32[576,128]{1,0:T(8,128)S(1)} %get-tuple-element.26), channel_id=1, source_target_pairs={{0,3},{1,0},{2,1},{3,2},{4,7},{5,4},{6,5},{7,6},{8,11},{9,8},{10,9... | collective-permute-start | bytes 884744 | tf_op jit(solution)/shard_map/ppermute | solution.py:373
  74.3 1.6 first.1
  75.9 11.7 %collective-permute-done.9 = f32[576,128]{1,0:T(8,128)S(1)} collective-permute-done((f32[576,128]{1,0:T(8,128)S(1)}, f32[576,128]{1,0:T(8,128)S(1)}, u32[]{:S(2)}, u32[]{:S(2)}) %collective-permute-start.9) | collective-permute-done | bytes 294944 | tf_op jit(solution)/shard_map/ppermute | solution.py:373
  87.7 22.2 %all_to_all.20 = f32[288,2,128]{2,1,0:T(2,128)S(1)} all-to-all(f32[288,2,128]{2,1,0:T(2,128)S(1)} %bitcast.51), channel_id=1, replica_groups={{0,4,8,12,16,20,24,28,64,68,72,76,80,84,88,92,128,132,136,140,144,148,1..., dimensions={0} | all-to-all | bytes 589824 | tf_op jit(solution)/shard_map/all_to_all | solution.py:402
  110.0 15.8 %all_to_all.21 = f32[288,2,128]{2,1,0:T(2,128)S(1)} all-to-all(f32[288,2,128]{2,1,0:T(2,128)S(1)} %bitcast.50), channel_id=1, replica_groups={{0,4,8,12,16,20,24,28,64,68,72,76,80,84,88,92,128,132,136,140,144,148,1..., dimensions={0} | all-to-all | bytes 589824 | tf_op jit(solution)/shard_map/all_to_all | solution.py:407
  125.8 2.3 %collective-permute-start.14 = (f32[576,128]{1,0:T(8,128)S(1)}, f32[576,128]{1,0:T(8,128)S(1)}, u32[]{:S(2)}, u32[]{:S(2)}) collective-permute-start(f32[576,128]{1,0:T(8,128)S(1)} %bitcast.38), channel_id=1, source_target_pairs={{0,3},{1,0},{2,1},{3,2},{4,7},{5,4},{6,5},{7,6},{8,11},{9,8},{10,9... | collective-permute-start | bytes 884744 | tf_op jit(solution)/shard_map/ppermute | solution.py:373
  128.2 1.6 collective-permute-start.13
  129.8 8.0 %collective-permute-done.14.refs_3_ = f32[576,128]{1,0:T(8,128)S(1)} collective-permute-done((f32[576,128]{1,0:T(8,128)S(1)}, f32[576,128]{1,0:T(8,128)S(1)}, u32[]{:S(2)}, u32[]{:S(2)}) %collective-permute-start.14) | collective-permute-done | bytes 294944 | tf_op jit(solution)/shard_map/ppermute | solution.py:373
  138.3 1.8 %collective-permute-done.12.refs_1_ = f32[576,128]{1,0:T(8,128)S(1)} collective-permute-done((f32[576,128]{1,0:T(8,128)S(1)}, f32[576,128]{1,0:T(8,128)S(1)}, u32[]{:S(2)}, u32[]{:S(2)}) %collective-permute-start.12) | collective-permute-done | bytes 294944 | tf_op jit(solution)/shard_map/ppermute | solution.py:373
  140.1 1.6 collective-permute-done.16.refs_5_
  141.7 19.8 %fit.1 = (f32[32,256]{1,0:T(8,128)S(1)}, f32[1,1]{1,0:T(1,128)S(1)}, f32[32,256]{1,0:T(8,128)S(1)}) custom-call(s32[2]{0:T(128)S(1)} %pad_add_fusion.place, f32[576,128]{1,0:T(8,128)S(1)} %bitcast.42, f32[576,128]{1,0:T(8,128)S(1)} %collective-permute-done.12.refs_1_, f32[576,128]{1,0:T(8,128)S(1)} %collective-permute-done.13.refs_2_, ...), custom_call_target="tpu_custom_call" | custom-call | tf_op jit(solution)/shard_map/fit/pallas_call | solution.py:30
  161.5 2.2 %collective-permute-start.21 = (f32[32,256]{1,0:T(8,128)S(1)}, f32[32,256]{1,0:T(8,128)S(1)}, u32[]{:S(2)}, u32[]{:S(2)}) collective-permute-start(f32[32,256]{1,0:T(8,128)S(1)} %get-tuple-element.22.refs_0_), channel_id=1, source_target_pairs={{0,3},{1,0},{2,1},{3,2},{4,7},{5,4},{6,5},{7,6},{8,11},{9,8},{10,9... | collective-permute-start | bytes 98312 | tf_op jit(solution)/shard_map/ppermute | solution.py:373
  163.8 1.7 collective-permute-start.20
  166.2 3.1 %collective-permute-done.20.refs_2_ = f32[32,256]{1,0:T(8,128)S(1)} collective-permute-done((f32[32,256]{1,0:T(8,128)S(1)}, f32[32,256]{1,0:T(8,128)S(1)}, u32[]{:S(2)}, u32[]{:S(2)}) %collective-permute-start.20) | collective-permute-done | bytes 32800 | tf_op jit(solution)/shard_map/ppermute | solution.py:373
  170.6 1.6 clean.1
  (43 shorter events, 14.1 us)
Async XLA Ops:
  0.6 11.6 %copy-start = (f32[256,65]{0,1:T(8,128)S(1)}, f32[256,65]{0,1:T(8,128)}, u32[]{:S(2)}) copy-start(f32[256,65]{0,1:T(8,128)} %param.7) | copy-start | bytes 199684
  2.8 9.4 %collective-permute-start.5 = (f32[32,32,128]{2,1,0:T(8,128)S(1)}, f32[32,32,128]{2,1,0:T(8,128)S(1)}, u32[]{:S(2)}, u32[]{:S(2)}) collective-permute-start(f32[32,32,128]{2,1,0:T(8,128)S(1)} %get-tuple-element.28.own), channel_id=1, source_target_pairs={{32,0},{64,32},{96,64},{128,96},{160,128},{192,160},{224,192},{33,... | collective-permute-start | bytes 1572872 | tf_op jit(solution)/shard_map/ppermute | solution.py:369
  4.1 8.1 %collective-permute-start.4 = (f32[32,32,128]{2,1,0:T(8,128)S(1)}, f32[32,32,128]{2,1,0:T(8,128)S(1)}, u32[]{:S(2)}, u32[]{:S(2)}) collective-permute-start(f32[32,32,128]{2,1,0:T(8,128)S(1)} %get-tuple-element.28.own), channel_id=1, source_target_pairs={{0,32},{32,64},{64,96},{96,128},{128,160},{160,192},{192,224},{1,3... | collective-permute-start | bytes 1572872 | tf_op jit(solution)/shard_map/ppermute | solution.py:368
  7.2 13.5 %collective-permute-start.1 = (f32[32,32,128]{2,1,0:T(8,128)S(1)}, f32[32,32,128]{2,1,0:T(8,128)S(1)}, u32[]{:S(2)}, u32[]{:S(2)}) collective-permute-start(f32[32,32,128]{2,1,0:T(8,128)S(1)} %get-tuple-element.29.own), channel_id=1, source_target_pairs={{32,0},{64,32},{96,64},{128,96},{160,128},{192,160},{224,192},{33,... | collective-permute-start | bytes 1572872 | tf_op jit(solution)/shard_map/ppermute | solution.py:369
  8.5 12.2 %collective-permute-start = (f32[32,32,128]{2,1,0:T(8,128)S(1)}, f32[32,32,128]{2,1,0:T(8,128)S(1)}, u32[]{:S(2)}, u32[]{:S(2)}) collective-permute-start(f32[32,32,128]{2,1,0:T(8,128)S(1)} %get-tuple-element.29.own), channel_id=1, source_target_pairs={{0,32},{32,64},{64,96},{96,128},{128,160},{160,192},{192,224},{1,3... | collective-permute-start | bytes 1572872 | tf_op jit(solution)/shard_map/ppermute | solution.py:368
  14.6 19.5 %copy-start.1 = (f32[256,65]{0,1:T(8,128)S(1)}, f32[256,65]{0,1:T(8,128)}, u32[]{:S(2)}) copy-start(f32[256,65]{0,1:T(8,128)} %param.8) | copy-start | bytes 199684
  14.6 19.5 %copy-start.2 = (f32[256,32]{0,1:T(8,128)S(1)}, f32[256,32]{0,1:T(8,128)}, u32[]{:S(2)}) copy-start(f32[256,32]{0,1:T(8,128)} %param.9) | copy-start | bytes 98308
  14.7 15.4 %collective-permute-start.7 = (f32[32,32,128]{2,1,0:T(8,128)S(1)}, f32[32,32,128]{2,1,0:T(8,128)S(1)}, u32[]{:S(2)}, u32[]{:S(2)}) collective-permute-start(f32[32,32,128]{2,1,0:T(8,128)S(1)} %bitcast.32), channel_id=1, source_target_pairs={{4,0},{8,4},{12,8},{16,12},{20,16},{24,20},{28,24},{5,1},{9,5},{13... | collective-permute-start | bytes 1572872 | tf_op jit(solution)/shard_map/ppermute | solution.py:369
  17.8 16.3 %collective-permute-start.6 = (f32[32,32,128]{2,1,0:T(8,128)S(1)}, f32[32,32,128]{2,1,0:T(8,128)S(1)}, u32[]{:S(2)}, u32[]{:S(2)}) collective-permute-start(f32[32,32,128]{2,1,0:T(8,128)S(1)} %bitcast.33), channel_id=1, source_target_pairs={{0,4},{4,8},{8,12},{12,16},{16,20},{20,24},{24,28},{1,5},{5,9},{9,... | collective-permute-start | bytes 1572872 | tf_op jit(solution)/shard_map/ppermute | solution.py:368
  23.0 18.3 %collective-permute-start.3 = (f32[32,32,128]{2,1,0:T(8,128)S(1)}, f32[32,32,128]{2,1,0:T(8,128)S(1)}, u32[]{:S(2)}, u32[]{:S(2)}) collective-permute-start(f32[32,32,128]{2,1,0:T(8,128)S(1)} %bitcast.35), channel_id=1, source_target_pairs={{4,0},{8,4},{12,8},{16,12},{20,16},{24,20},{28,24},{5,1},{9,5},{13... | collective-permute-start | bytes 1572872 | tf_op jit(solution)/shard_map/ppermute | solution.py:369
  26.1 19.2 %collective-permute-start.2 = (f32[32,32,128]{2,1,0:T(8,128)S(1)}, f32[32,32,128]{2,1,0:T(8,128)S(1)}, u32[]{:S(2)}, u32[]{:S(2)}) collective-permute-start(f32[32,32,128]{2,1,0:T(8,128)S(1)} %bitcast.36), channel_id=1, source_target_pairs={{0,4},{4,8},{8,12},{12,16},{16,20},{20,24},{24,28},{1,5},{5,9},{9,... | collective-permute-start | bytes 1572872 | tf_op jit(solution)/shard_map/ppermute | solution.py:368
  37.3 14.8 %all-to-all-start.1 = ((f32[4,288,128]{2,1,0:T(8,128)}), f32[4,288,128]{2,1,0:T(8,128)S(1)}, u32[]{:S(2)}, u32[]{:S(2)}) async-start(f32[4,288,128]{2,1,0:T(8,128)} %bitcast.8.refs_6_), calls=%async_computation.1 | async-start | bytes 1179648 | tf_op jit(solution)/shard_map/all_to_all | solution.py:388
  52.1 14.2 %all-to-all-start = ((f32[4,288,128]{2,1,0:T(8,128)}), f32[4,288,128]{2,1,0:T(8,128)S(1)}, u32[]{:S(2)}, u32[]{:S(2)}) async-start(f32[4,288,128]{2,1,0:T(8,128)} %bitcast.6.refs_5_), calls=%async_computation | async-start | bytes 1179648 | tf_op jit(solution)/shard_map/all_to_all | solution.py:388
  67.8 2.9 %collective-permute-start.8 = (f32[4,576,128]{2,1,0:T(8,128)S(1)}, f32[4,576,128]{2,1,0:T(8,128)S(1)}, u32[]{:S(2)}, u32[]{:S(2)}) collective-permute-start(f32[4,576,128]{2,1,0:T(8,128)S(1)} %get-tuple-element.16), channel_id=1, source_target_pairs={{0,32},{32,0},{64,96},{96,64},{128,160},{160,128},{192,224},{224,1... | collective-permute-start | bytes 3538952 | tf_op jit(solution)/shard_map/ppermute | solution.py:376
  70.9 16.7 %collective-permute-start.9 = (f32[576,128]{1,0:T(8,128)S(1)}, f32[576,128]{1,0:T(8,128)S(1)}, u32[]{:S(2)}, u32[]{:S(2)}) collective-permute-start(f32[576,128]{1,0:T(8,128)S(1)} %get-tuple-element.25), channel_id=1, source_target_pairs={{0,1},{1,2},{2,3},{3,0},{4,5},{5,6},{6,7},{7,4},{8,9},{9,10},{10,1... | collective-permute-start | bytes 884744 | tf_op jit(solution)/shard_map/ppermute | solution.py:373
  71.6 16.0 %collective-permute-start.11 = (f32[576,128]{1,0:T(8,128)S(1)}, f32[576,128]{1,0:T(8,128)S(1)}, u32[]{:S(2)}, u32[]{:S(2)}) collective-permute-start(f32[576,128]{1,0:T(8,128)S(1)} %get-tuple-element.26), channel_id=1, source_target_pairs={{0,3},{1,0},{2,1},{3,2},{4,7},{5,4},{6,5},{7,6},{8,11},{9,8},{10,9... | collective-permute-start | bytes 884744 | tf_op jit(solution)/shard_map/ppermute | solution.py:373
  74.3 13.3 %collective-permute-start.10 = (f32[576,128]{1,0:T(8,128)S(1)}, f32[576,128]{1,0:T(8,128)S(1)}, u32[]{:S(2)}, u32[]{:S(2)}) collective-permute-start(f32[576,128]{1,0:T(8,128)S(1)} %get-tuple-element.27), channel_id=1, source_target_pairs={{0,2},{1,3},{2,0},{3,1},{4,6},{5,7},{6,4},{7,5},{8,10},{9,11},{10,... | collective-permute-start | bytes 884744 | tf_op jit(solution)/shard_map/ppermute | solution.py:373
  125.8 12.0 %collective-permute-start.14 = (f32[576,128]{1,0:T(8,128)S(1)}, f32[576,128]{1,0:T(8,128)S(1)}, u32[]{:S(2)}, u32[]{:S(2)}) collective-permute-start(f32[576,128]{1,0:T(8,128)S(1)} %bitcast.38), channel_id=1, source_target_pairs={{0,3},{1,0},{2,1},{3,2},{4,7},{5,4},{6,5},{7,6},{8,11},{9,8},{10,9... | collective-permute-start | bytes 884744 | tf_op jit(solution)/shard_map/ppermute | solution.py:373
  128.2 9.6 %collective-permute-start.13 = (f32[576,128]{1,0:T(8,128)S(1)}, f32[576,128]{1,0:T(8,128)S(1)}, u32[]{:S(2)}, u32[]{:S(2)}) collective-permute-start(f32[576,128]{1,0:T(8,128)S(1)} %bitcast.39), channel_id=1, source_target_pairs={{0,2},{1,3},{2,0},{3,1},{4,6},{5,7},{6,4},{7,5},{8,10},{9,11},{10,... | collective-permute-start | bytes 884744 | tf_op jit(solution)/shard_map/ppermute | solution.py:373
  129.8 10.4 %collective-permute-start.12 = (f32[576,128]{1,0:T(8,128)S(1)}, f32[576,128]{1,0:T(8,128)S(1)}, u32[]{:S(2)}, u32[]{:S(2)}) collective-permute-start(f32[576,128]{1,0:T(8,128)S(1)} %bitcast.40), channel_id=1, source_target_pairs={{0,1},{1,2},{2,3},{3,0},{4,5},{5,6},{6,7},{7,4},{8,9},{9,10},{10,1... | collective-permute-start | bytes 884744 | tf_op jit(solution)/shard_map/ppermute | solution.py:373
  129.8 10.4 %collective-permute-start.15 = (f32[576,128]{1,0:T(8,128)S(1)}, f32[576,128]{1,0:T(8,128)S(1)}, u32[]{:S(2)}, u32[]{:S(2)}) collective-permute-start(f32[576,128]{1,0:T(8,128)S(1)} %bitcast.41), channel_id=1, source_target_pairs={{0,32},{32,0},{64,96},{96,64},{128,160},{160,128},{192,224},{224,1... | collective-permute-start | bytes 884744 | tf_op jit(solution)/shard_map/ppermute | solution.py:376
  137.8 2.3 %collective-permute-start.18 = (f32[576,128]{1,0:T(8,128)S(1)}, f32[576,128]{1,0:T(8,128)S(1)}, u32[]{:S(2)}, u32[]{:S(2)}) collective-permute-start(f32[576,128]{1,0:T(8,128)S(1)} %collective-permute-done.14.refs_3_), channel_id=1, source_target_pairs={{0,32},{32,0},{64,96},{96,64},{128,160},{160,128},{192,224},{224,1... | collective-permute-start | bytes 884744 | tf_op jit(solution)/shard_map/ppermute | solution.py:376
  137.8 2.3 %collective-permute-start.17 = (f32[576,128]{1,0:T(8,128)S(1)}, f32[576,128]{1,0:T(8,128)S(1)}, u32[]{:S(2)}, u32[]{:S(2)}) collective-permute-start(f32[576,128]{1,0:T(8,128)S(1)} %collective-permute-done.13.refs_2_), channel_id=1, source_target_pairs={{0,32},{32,0},{64,96},{96,64},{128,160},{160,128},{192,224},{224,1... | collective-permute-start | bytes 884744 | tf_op jit(solution)/shard_map/ppermute | solution.py:376
  140.1 1.6 collective-permute-start.16
  161.5 4.6 %collective-permute-start.21 = (f32[32,256]{1,0:T(8,128)S(1)}, f32[32,256]{1,0:T(8,128)S(1)}, u32[]{:S(2)}, u32[]{:S(2)}) collective-permute-start(f32[32,256]{1,0:T(8,128)S(1)} %get-tuple-element.22.refs_0_), channel_id=1, source_target_pairs={{0,3},{1,0},{2,1},{3,2},{4,7},{5,4},{6,5},{7,6},{8,11},{9,8},{10,9... | collective-permute-start | bytes 98312 | tf_op jit(solution)/shard_map/ppermute | solution.py:373
  163.8 5.5 %collective-permute-start.20 = (f32[32,256]{1,0:T(8,128)S(1)}, f32[32,256]{1,0:T(8,128)S(1)}, u32[]{:S(2)}, u32[]{:S(2)}) collective-permute-start(f32[32,256]{1,0:T(8,128)S(1)} %get-tuple-element.22.refs_0_), channel_id=1, source_target_pairs={{0,2},{1,3},{2,0},{3,1},{4,6},{5,7},{6,4},{7,5},{8,10},{9,11},{10,... | collective-permute-start | bytes 98312 | tf_op jit(solution)/shard_map/ppermute | solution.py:373
  165.5 5.1 %collective-permute-start.19 = (f32[32,256]{1,0:T(8,128)S(1)}, f32[32,256]{1,0:T(8,128)S(1)}, u32[]{:S(2)}, u32[]{:S(2)}) collective-permute-start(f32[32,256]{1,0:T(8,128)S(1)} %get-tuple-element.22.refs_0_), channel_id=1, source_target_pairs={{0,1},{1,2},{2,3},{3,0},{4,5},{5,6},{6,7},{7,4},{8,9},{9,10},{10,1... | collective-permute-start | bytes 98312 | tf_op jit(solution)/shard_map/ppermute | solution.py:373

commit v4 on v3

--- a/solution.py
+++ b/solution.py
@@ -14,16 +14,17 @@
 LIMIT = 32 << 20
 
 
-def call(kernel, out_shapes, *args, name, scratch=(), dtypes=None):
+def call(kernel, out_shapes, *args, name, scratch=(), dtypes=None, out_space=VM):
     dtypes = dtypes or [jnp.float32] * len(out_shapes)
     fast = pl.BlockSpec(memory_space=VM)
     specs = [
         pl.BlockSpec(memory_space=pltpu.SMEM) if x.dtype == jnp.int32 else fast for x in args
     ]
-    if INTERPRET:
+    if INTERPRET or out_space is not VM:
         outs = [jax.ShapeDtypeStruct(s, d) for s, d in zip(out_shapes, dtypes)]
     else:
         outs = [VM(s, d) for s, d in zip(out_shapes, dtypes)]
+    if not INTERPRET:
         args = [
             x if x.dtype == jnp.int32 else pltpu.with_memory_space_constraint(x, VM) for x in args
         ]
@@ -31,7 +32,7 @@
         kernel,
         out_shape=outs,
         in_specs=specs,
-        out_specs=[fast] * len(outs),
+        out_specs=[pl.BlockSpec(memory_space=out_space)] * len(outs),
         scratch_shapes=list(scratch),
         compiler_params=pltpu.CompilerParams(vmem_limit_bytes=LIMIT),
         interpret=INTERPRET,
@@ -62,44 +63,65 @@
     return lax.dot_general(a, b, (dims, ((), ())), preferred_element_type=jnp.float32)
 
 
-def beam_kernel(half, low, own, high, taps, *rest):
-    out = rest[-1]
-    length, wide, width = own.shape
+def strip(refs, taps, lanes, j, out):
+    length = refs[1].shape[0]
     count = taps.shape[0]
-    refs = (low, own, high)
-    lanes = slice(half * width, (half + 1) * width)
-
-    def strip(j, _):
-        at = pl.ds(pl.multiple_of(j * 8, 8), 8)
-        for block in range(length // 8):
-            acc = [None] * 8
-            held = {}
-            for k in range(count + 7):
-                row = block * 8 + k
-                value = refs[row // length][row % length, at, :]
-                if k < count:
-                    held[k] = jnp.broadcast_to(taps[k : k + 1, lanes], value.shape)
-                for i in range(8):
-                    t = k - i
-                    if 0 <= t < count:
-                        term = held[t] * value
-                        acc[i] = term if acc[i] is None else acc[i] + term
-            out[j, 0:8, block * 8 : block * 8 + 8, :] = jnp.swapaxes(jnp.stack(acc), 0, 1)
-        if len(rest) == 2:
-            for e in range(out.shape[1] - 8):
-                out[j, 8 + e] = rest[0][e * length : (e + 1) * length, lanes]
-
-    lax.fori_loop(0, wide // 8, strip, None)
-
-
-def beam(low, own, high, taps, half, loads=None):
+    at = pl.ds(pl.multiple_of(j * 8, 8), 8)
+    for block in range(length // 8):
+        acc = [None] * 8
+        held = {}
+        for k in range(count + 7):
+            row = block * 8 + k
+            value = refs[row // length][row % length, at, :]
+            if k < count:
+                held[k] = jnp.broadcast_to(taps[k : k + 1, lanes], value.shape)
+            for i in range(8):
+                t = k - i
+                if 0 <= t < count:
+                    term = held[t] * value
+                    acc[i] = term if acc[i] is None else acc[i] + term
+        out[0:8, block * 8 : block * 8 + 8, :] = jnp.swapaxes(jnp.stack(acc), 0, 1)
+
+
+def lanes_of(half, own):
+    return slice(half * own.shape[2], (half + 1) * own.shape[2])
+
+
+def beam_kernel(half, low, own, high, taps, out):
+    def one(j, _):
+        strip((low, own, high), taps, lanes_of(half, own), j, out.at[j])
+
+    lax.fori_loop(0, own.shape[1] // 8, one, None)
+
+
+def beam(low, own, high, taps, half):
     a, b, f = own.shape
     assert taps.shape[0] == 2 * a + 1
-    more = [] if loads is None else [loads]
-    extra = 0 if loads is None else loads.shape[0] // a
-    shape = (b // 8, 8 + extra, a, f)
     kernel = functools.partial(beam_kernel, half)
-    return call(kernel, [shape], low, own, high, taps, *more, name="beam")[0]
+    return call(kernel, [(b // 8, 8, a, f)], low, own, high, taps, name="beam")[0]
+
+
+def parted_kernel(half, place, low, own, high, taps, loads, *outs):
+    parts = len(outs)
+    length = own.shape[0]
+    lanes = lanes_of(half, own)
+    for k, out in enumerate(outs):
+        strip((low, own, high), taps, lanes, lax.rem(place[1] + k, parts), out)
+        for e in range(out.shape[0] - 8):
+            out[8 + e] = loads[e * length : (e + 1) * length, lanes]
+
+
+def parted_beam(place, low, own, high, taps, half, loads, parts):
+    a, b, f = own.shape
+    assert taps.shape[0] == 2 * a + 1 and b == 8 * parts
+    shape = (8 + loads.shape[0] // a, a, f)
+    kernel = functools.partial(parted_kernel, half)
+    outs = call(kernel, [shape] * parts, place, low, own, high, taps, loads, name="beam")
+    return [x.reshape(-1, f) for x in outs]
+
+
+def source(place, k, parts):
+    return lax.rem(place[1] + parts - k, parts)
 
 
 def row_block(place, c, k, parts):
@@ -107,12 +129,13 @@
 
 
 def moment_kernel(c, pixels, place, *refs):
-    if len(refs) == 5:
-        even, odd, out, hi, lo = refs
-        parts = even.shape[0]
-        for b in range(2 * parts):
-            value = (even, odd)[b % 2][b // 2, 0:pixels]
+    if len(refs) > 3:
+        out, hi, lo = refs[-3:]
+        parts = hi.shape[0] // 2
+        for s in range(2 * parts):
+            value = refs[s][0:pixels]
             top = value.astype(jnp.bfloat16)
+            b = 2 * source(place, s % parts, parts) + s // parts
             hi[b] = top
             lo[b] = (value - top.astype(jnp.float32)).astype(jnp.bfloat16)
     else:
@@ -143,13 +166,14 @@
         )
 
 
-def moments(place, even, odd, pixels):
-    parts, _, width = even.shape
+def moments(place, slots, pixels):
+    width = slots[0].shape[1]
+    parts = len(slots) // 2
     shape = (parts, width * parts + width // 2, width)
     halves = (2 * parts, pixels, width)
     half = jnp.bfloat16
     theirs, hi, lo = call(
-        functools.partial(moment_kernel, 1, pixels), [shape, halves, halves], place, even, odd,
+        functools.partial(moment_kernel, 1, pixels), [shape, halves, halves], place, *slots,
         name="moments", dtypes=[jnp.float32, half, half],
     )
     ours = call(functools.partial(moment_kernel, 0, pixels), [shape], place, hi, lo, name="moments")
@@ -223,37 +247,36 @@
     return inverse, times(inverse, pieces)
 
 
-def first_kernel(even, odd, inverse_out, weight_out):
+def first_kernel(place, *refs):
+    slots, (inverse_out, weight_out, loads) = refs[:-3], refs[-3:]
+    parts = len(slots) // 2
     n = weight_out.shape[0]
-    rows = even.shape[1]
-    loads = jnp.concatenate(
-        [ref[b, rows - n : rows] for b in range(even.shape[0]) for ref in (even, odd)], axis=1
-    )
-    pieces = parts_of(loads)
+    rows, width = slots[0].shape
+    for s, ref in enumerate(slots):
+        b = 2 * source(place, s % parts, parts) + s // parts
+        loads[:, pl.ds(pl.multiple_of(b * width, width), width)] = ref[rows - n : rows]
+    pieces = parts_of(loads[...])
     gram = gram_of(pieces, pieces)
     inverse_out[...], weight_out[...] = weights(pieces, gram, jnp.ones((1, 1), jnp.float32))
 
 
-def first_weights(even, odd, n):
-    parts, _, width = even.shape
-    return call(first_kernel, [(n, n), (n, 2 * parts * width)], even, odd, name="first")
-
-
-def cross_of(stacked, hi, mid, low):
+def first_weights(place, slots, n):
+    shape = (n, len(slots) * slots[0].shape[1])
+    scratch = [VM(shape, jnp.float32)]
+    return call(first_kernel, [(n, n), shape], place, *slots, name="first", scratch=scratch)
+
+
+def cross_of(stacked, hi, lo):
     n = stacked.shape[0] // 3
-
-    def product(count, ref):
-        return jnp.dot(stacked[: count * n], ref[...], preferred_element_type=jnp.float32)
-
-    top, middle, last = product(3, hi), product(2, mid), product(1, low)
-    small = top[2 * n :] + middle[n:] + last
-    return top[:n] + (top[n : 2 * n] + middle[:n] + small)
+    top = jnp.dot(stacked, hi[...], preferred_element_type=jnp.float32)
+    low = jnp.dot(stacked[: 2 * n], lo[...], preferred_element_type=jnp.float32)
+    return top[:n] + (top[n : 2 * n] + low[:n] + (top[2 * n :] + low[n:]))
 
 
 def fit_kernel(pixel_total, parts, place, *refs):
     slots = refs[: 2 * parts]
     inverse0, weight0, map_hi, map_lo = refs[2 * parts : 2 * parts + 4]
-    block_out, noise_out, lat_out, hi, mid, low, held = refs[2 * parts + 4 :]
+    block_out, noise_out, lat_out, hi, lo, held = refs[2 * parts + 4 :]
     width = slots[0].shape[1]
     blocks = 2 * parts
     freqs = blocks * width
@@ -264,11 +287,11 @@
     def place_block(i, j, block, mirror):
         rows = pl.ds(pl.multiple_of(i * width, width), width)
         cols = pl.ds(pl.multiple_of(j * width, width), width)
-        for dest, value in zip((hi, mid, low), split3(block)):
-            dest[rows, cols] = value
+        top, rest, _ = split3(block)
+        hi[rows, cols], lo[rows, cols] = top, rest
         if mirror:
-            for dest, value in zip((hi, mid, low), split3(block.T)):
-                dest[cols, rows] = value
+            top, rest, _ = split3(block.T)
+            hi[cols, rows], lo[cols, rows] = top, rest
 
     for s, ref in enumerate(slots):
         i = row_block(place, s // parts, parts - s % parts, parts)
@@ -288,7 +311,7 @@
     def step(_, state):
         inverse, weight, noise = state
         stacked = parts_of(weight)
-        cross = cross_of(stacked, hi, mid, low)
+        cross = cross_of(stacked, hi, lo)
         pieces = parts_of(cross)
         scaled = pixel_total * noise * inverse + gram_of(pieces, stacked)
         updated = times(inverse_spd(scaled), pieces)
@@ -330,28 +353,39 @@
         [(n, freqs // parts), (1, 1), (n, hi.shape[1])],
         place, *slots, inverse0, weight0, hi, lo,
         name="fit",
-        scratch=[VM((freqs, freqs), jnp.bfloat16)] * 3 + [VM((n, freqs), jnp.float32)],
+        scratch=[VM((freqs, freqs), jnp.bfloat16)] * 2 + [VM((n, freqs), jnp.float32)],
     )
 
 
 def clean_kernel(parts, place, *refs):
-    latents, loads, first, second, out = refs[:parts], *refs[parts:]
-    width = first.shape[2]
+    latents, loads, slots = refs[:parts], refs[parts], refs[parts + 1 : 3 * parts + 1]
+    out, held, sems = refs[3 * parts + 1 :]
+    width = slots[0].shape[1]
     rows = latents[0].shape[1]
+    copies = []
     for k in range(parts):
-        at = lax.rem(place[1] + parts - k, parts)
         model = thin(latents[k][...], loads[...], ((0,), (0,)))
-        here = pl.ds(pl.multiple_of(at * rows, rows), rows)
-        out[here, 0:width] = first[at, 0:rows] - model[:, 0:width]
-        out[here, width:] = second[at, 0:rows] - model[:, width:]
-
-
-def clean(place, first, second, latents, loads):
-    parts, _, width = first.shape
+        for h in range(2):
+            lanes = slice(h * width, (h + 1) * width)
+            held[k, :, lanes] = slots[h * parts + (parts - k) % parts][0:rows] - model[:, lanes]
+        here = pl.ds(pl.multiple_of(source(place, k, parts) * rows, rows), rows)
+        copies.append(pltpu.make_async_copy(held.at[k], out.at[here], sems.at[k]))
+        copies[-1].start()
+    for copy in copies:
+        copy.wait()
+
+
+def clean(place, slots, latents, loads):
+    parts = len(latents)
     rows = latents[0].shape[1]
-    kernel = functools.partial(clean_kernel, parts)
-    shape = (parts * rows, 2 * width)
-    return call(kernel, [shape], place, *latents, loads, first, second, name="clean")[0]
+    wide = 2 * slots[0].shape[1]
+    return call(
+        functools.partial(clean_kernel, parts), [(parts * rows, wide)],
+        place, *latents, loads, *slots,
+        name="clean",
+        scratch=[VM((parts, rows, wide), jnp.float32), pltpu.SemaphoreType.DMA((parts,))],
+        out_space=pl.ANY,
+    )[0]
 
 
 def body(sky_maps, validity, row_taps, column_taps, init_loadings):
@@ -382,15 +416,13 @@
         smoothed = beam(around[h][0], masked[h], around[h][1], row_taps.T, h)
         smoothed = smoothed.reshape(cols_here, rows_here, width)
         low, high = halos(smoothed, "sy", sy)
-        spectra = beam(low, smoothed, high, column_taps.T, h, init_loadings.T)
-        spectra = spectra.reshape(af, pixels + n, width)
-        beamed.append(spectra)
-        traded.append(lax.all_to_all(spectra, "af", 0, 0))
-    even, odd = traded
-
-    theirs, partial, hi, lo = moments(place, even, odd, pixels)
+        slots = parted_beam(place, low, smoothed, high, column_taps.T, h, init_loadings.T, af)
+        beamed += slots
+        traded += slots[:1] + [shifted(slots[k], k) for k in range(1, af)]
+
+    theirs, partial, hi, lo = moments(place, traded, pixels)
     partial = partial + swapped(theirs)
-    inverse0, weight0 = first_weights(even, odd, n)
+    inverse0, weight0 = first_weights(place, traded, n)
     piece = partial[0]
     for k in range(1, af):
         piece = piece + shifted(partial[k], k)
@@ -415,7 +447,7 @@
         place, mine + other, inverse0, weight0, hi, lo, float(pixels_here * sx * sy)
     )
     latents = [latent] + [shifted(latent, k) for k in range(1, af)]
-    cleaned = clean(place, beamed[0], beamed[1], latents, loads_here)
+    cleaned = clean(place, beamed, latents, loads_here)
     return cleaned.reshape(rows_here, cols_here, freqs_here), loads_here.T, noise.reshape(())
 
 

time: 175 us -> 172 us (0.983)
  waiting for transfers between devices: 53.1 us -> 34.4 us
  starting transfers between devices: 39.9 us -> 49.7 us
  blocking collectives: 38 us -> 46.3 us
    all_to_all x2 -> x0, waiting for transfers between devices: 14.2 us -> none  [body(): traded.append(lax.all_to_all(spectra, 'af', 0, 0))]
    ppermute x9 -> x15, starting transfers between devices: 11.2 us -> 24.8 us  [shifted(): return lax.ppermute(block, 'af', [(i, (i + k) % af) for i in range(af)])]
    all_to_all x2, blocking collectives: 38 us -> 46.3 us  [body(): lax.all_to_all(pieces, ('sx', 'sy'), 0, 0, axis_index_groups=groups, tile...]
    all_to_all x2 -> x0, starting transfers between devices: 6.95 us -> none  [body(): traded.append(lax.all_to_all(spectra, 'af', 0, 0))]
    ppermute x4, waiting for transfers between devices: 8.09 us -> 2.07 us  [halos(): low = lax.ppermute(block, axis, [(i, i + 1) for i in range(count - 1)])]
    ppermute x5, starting transfers between devices: 0.61 us -> 4.28 us  [swapped(): return lax.ppermute(block, 'sx', [(i, i ^ 1) for i in range(sx)])]
    ppermute x9 -> x15, waiting for transfers between devices: 26 us -> 29.6 us  [shifted(): return lax.ppermute(block, 'af', [(i, (i + k) % af) for i in range(af)])]
    ppermute x4, starting transfers between devices: 8.86 us -> 6.78 us  [halos(): high = lax.ppermute(block, axis, [(i + 1, i) for i in range(count - 1)])]
  transfers between devices with their start and end apart: 24 -> 28, of which waited for: 13 -> 15; matrix products, arithmetic and copies ran while one was open for 0% -> 0% of each run, Pallas kernels for 8% -> 8%
where the time goes in v4:
time: 172 us
  starting transfers between devices  49.7 us (29%)
  blocking collectives  46.3 us (27%)
  Pallas kernels  35.3 us (21%)
  waiting for transfers between devices  34.4 us (20%)
  other arithmetic  2.56 us (1%)
  between operations  2.06 us (1%)
    all_to_all x2, blocking collectives, body(): lax.all_to_all(pieces, ('sx', 'sy'), 0, 0, axis_index_groups=groups, tile...  46.3 us
    pallas_call x9, Pallas kernels, call(): pl.pallas_call(kernel, out_shape=outs, in_specs=specs, out_specs=[pl.Bloc...  35.3 us
    ppermute x15, waiting for transfers between devices, shifted(): return lax.ppermute(block, 'af', [(i, (i + k) % af) for i in range(af)])  29.6 us
    ppermute x15, starting transfers between devices, shifted(): return lax.ppermute(block, 'af', [(i, (i + k) % af) for i in range(af)])  24.8 us
    ppermute x4, starting transfers between devices, halos(): low = lax.ppermute(block, axis, [(i, i + 1) for i in range(count - 1)])  13.8 us
    ppermute x4, starting transfers between devices, halos(): high = lax.ppermute(block, axis, [(i + 1, i) for i in range(count - 1)])  6.78 us
    ppermute x5, starting transfers between devices, swapped(): return lax.ppermute(block, 'sx', [(i, i ^ 1) for i in range(sx)])  4.28 us
  transfers between devices with their start and end apart: 28, of which 15 were waited for; matrix products, arithmetic and copies ran while one was open for 0% of the time, Pallas kernels for 8%

profile of v4, /device:TPU:32, one launch (start us, length us, event | category | flops | bytes accessed | tf_op | source)
XLA Modules:
  0.0 171.7 jit_solution(18418156299585126530)
XLA Ops:
  2.8 1.8 %collective-permute-start.7 = (f32[32,32,128]{2,1,0:T(8,128)S(1)}, f32[32,32,128]{2,1,0:T(8,128)S(1)}, u32[]{:S(2)}, u32[]{:S(2)}) collective-permute-start(f32[32,32,128]{2,1,0:T(8,128)S(1)} %get-tuple-element.44.own), channel_id=1, source_target_pairs={{0,32},{32,64},{64,96},{96,128},{128,160},{160,192},{192,224},{1,3... | collective-permute-start | bytes 1572872 | tf_op jit(solution)/shard_map/ppermute | solution.py:402
  5.9 4.4 %collective-permute-start = (f32[32,32,128]{2,1,0:T(8,128)S(1)}, f32[32,32,128]{2,1,0:T(8,128)S(1)}, u32[]{:S(2)}, u32[]{:S(2)}) collective-permute-start(f32[32,32,128]{2,1,0:T(8,128)S(1)} %get-tuple-element.45.own), channel_id=1, source_target_pairs={{0,32},{32,64},{64,96},{96,128},{128,160},{160,192},{192,224},{1,3... | collective-permute-start | bytes 1572872 | tf_op jit(solution)/shard_map/ppermute | solution.py:402
  11.6 2.4 %beam.6 = f32[4,8,32,128]{3,2,1,0:T(8,128)S(1)} custom-call(f32[32,32,128]{2,1,0:T(8,128)S(1)} %collective-permute-done.7.low, f32[32,32,128]{2,1,0:T(8,128)S(1)} %get-tuple-element.44.own, f32[32,32,128]{2,1,0:T(8,128)S(1)} %collective-permute-done.8.high, f32[65,256]{1,0:T(8,128)S(1)} %bitcast.54), custom_call_target="tpu_custom_call" | custom-call | tf_op jit(solution)/shard_map/beam/pallas_call | solution.py:31
  14.0 2.1 %collective-permute-start.10 = (f32[32,32,128]{2,1,0:T(8,128)S(1)}, f32[32,32,128]{2,1,0:T(8,128)S(1)}, u32[]{:S(2)}, u32[]{:S(2)}) collective-permute-start(f32[32,32,128]{2,1,0:T(8,128)S(1)} %bitcast.40), channel_id=1, source_target_pairs={{4,0},{8,4},{12,8},{16,12},{20,16},{24,20},{28,24},{5,1},{9,5},{13... | collective-permute-start | bytes 1572872 | tf_op jit(solution)/shard_map/ppermute | solution.py:403
  16.2 3.8 %collective-permute-start.9 = (f32[32,32,128]{2,1,0:T(8,128)S(1)}, f32[32,32,128]{2,1,0:T(8,128)S(1)}, u32[]{:S(2)}, u32[]{:S(2)}) collective-permute-start(f32[32,32,128]{2,1,0:T(8,128)S(1)} %bitcast.41), channel_id=1, source_target_pairs={{0,4},{4,8},{8,12},{12,16},{16,20},{20,24},{24,28},{1,5},{5,9},{9,... | collective-permute-start | bytes 1572872 | tf_op jit(solution)/shard_map/ppermute | solution.py:402
  20.0 2.3 %beam.4 = f32[4,8,32,128]{3,2,1,0:T(8,128)S(1)} custom-call(f32[32,32,128]{2,1,0:T(8,128)S(1)} %collective-permute-done.low, f32[32,32,128]{2,1,0:T(8,128)S(1)} %get-tuple-element.45.own, f32[32,32,128]{2,1,0:T(8,128)S(1)} %collective-permute-done.1.high, f32[65,256]{1,0:T(8,128)S(1)} %bitcast.55), custom_call_target="tpu_custom_call" | custom-call | tf_op jit(solution)/shard_map/beam/pallas_call | solution.py:31
  22.4 3.8 %collective-permute-start.2 = (f32[32,32,128]{2,1,0:T(8,128)S(1)}, f32[32,32,128]{2,1,0:T(8,128)S(1)}, u32[]{:S(2)}, u32[]{:S(2)}) collective-permute-start(f32[32,32,128]{2,1,0:T(8,128)S(1)} %bitcast.37), channel_id=1, source_target_pairs={{0,4},{4,8},{8,12},{12,16},{16,20},{20,24},{24,28},{1,5},{5,9},{9,... | collective-permute-start | bytes 1572872 | tf_op jit(solution)/shard_map/ppermute | solution.py:402
  26.2 2.0 %collective-permute-start.3 = (f32[32,32,128]{2,1,0:T(8,128)S(1)}, f32[32,32,128]{2,1,0:T(8,128)S(1)}, u32[]{:S(2)}, u32[]{:S(2)}) collective-permute-start(f32[32,32,128]{2,1,0:T(8,128)S(1)} %bitcast.38), channel_id=1, source_target_pairs={{4,0},{8,4},{12,8},{16,12},{20,16},{24,20},{28,24},{5,1},{9,5},{13... | collective-permute-start | bytes 1572872 | tf_op jit(solution)/shard_map/ppermute | solution.py:403
  29.4 2.9 %beam.7 = (f32[9,32,128]{2,1,0:T(8,128)S(1)}, f32[9,32,128]{2,1,0:T(8,128)S(1)}, f32[9,32,128]{2,1,0:T(8,128)S(1)}, f32[9,32,128]{2,1,0:T(8,128)S(1)}) custom-call(s32[2]{0:T(128)S(1)} %pad_add_fusion.place, f32[32,32,128]{2,1,0:T(8,128)S(1)} %collective-permute-done.9.low, f32[32,32,128]{2,1,0:T(8,128)S(1)} %bitcast.42, ...), custom_call_target="tpu_custom_call" | custom-call | tf_op jit(solution)/shard_map/beam/pallas_call | solution.py:31
  33.9 2.7 %collective-permute-start.12 = (f32[288,128]{1,0:T(8,128)S(1)}, f32[288,128]{1,0:T(8,128)S(1)}, u32[]{:S(2)}, u32[]{:S(2)}) collective-permute-start(f32[288,128]{1,0:T(8,128)S(1)} %bitcast.60), channel_id=1, source_target_pairs={{0,2},{1,3},{2,0},{3,1},{4,6},{5,7},{6,4},{7,5},{8,10},{9,11},{10,... | collective-permute-start | bytes 442376 | tf_op jit(solution)/shard_map/ppermute | solution.py:407
  38.1 1.8 %collective-permute-done.2.low = f32[32,32,128]{2,1,0:T(8,128)S(1)} collective-permute-done((f32[32,32,128]{2,1,0:T(8,128)S(1)}, f32[32,32,128]{2,1,0:T(8,128)S(1)}, u32[]{:S(2)}, u32[]{:S(2)}) %collective-permute-start.2) | collective-permute-done | bytes 524320 | tf_op jit(solution)/shard_map/ppermute | solution.py:402
  40.0 2.9 %beam.5 = (f32[9,32,128]{2,1,0:T(8,128)S(1)}, f32[9,32,128]{2,1,0:T(8,128)S(1)}, f32[9,32,128]{2,1,0:T(8,128)S(1)}, f32[9,32,128]{2,1,0:T(8,128)S(1)}) custom-call(s32[2]{0:T(128)S(1)} %pad_add_fusion.place, f32[32,32,128]{2,1,0:T(8,128)S(1)} %collective-permute-done.2.low, f32[32,32,128]{2,1,0:T(8,128)S(1)} %bitcast.39, ...), custom_call_target="tpu_custom_call" | custom-call | tf_op jit(solution)/shard_map/beam/pallas_call | solution.py:31
  42.9 1.6 collective-permute-start.4
  44.5 2.7 %collective-permute-start.5 = (f32[288,128]{1,0:T(8,128)S(1)}, f32[288,128]{1,0:T(8,128)S(1)}, u32[]{:S(2)}, u32[]{:S(2)}) collective-permute-start(f32[288,128]{1,0:T(8,128)S(1)} %bitcast.66), channel_id=1, source_target_pairs={{0,2},{1,3},{2,0},{3,1},{4,6},{5,7},{6,4},{7,5},{8,10},{9,11},{10,... | collective-permute-start | bytes 442376 | tf_op jit(solution)/shard_map/ppermute | solution.py:407
  48.6 1.9 %collective-permute-done.4.refs_1_ = f32[288,128]{1,0:T(8,128)S(1)} collective-permute-done((f32[288,128]{1,0:T(8,128)S(1)}, f32[288,128]{1,0:T(8,128)S(1)}, u32[]{:S(2)}, u32[]{:S(2)}) %collective-permute-start.4) | collective-permute-done | bytes 147488 | tf_op jit(solution)/shard_map/ppermute | solution.py:407
  50.5 2.0 %collective-permute-done.5.refs_2_ = f32[288,128]{1,0:T(8,128)S(1)} collective-permute-done((f32[288,128]{1,0:T(8,128)S(1)}, f32[288,128]{1,0:T(8,128)S(1)}, u32[]{:S(2)}, u32[]{:S(2)}) %collective-permute-start.5) | collective-permute-done | bytes 147488 | tf_op jit(solution)/shard_map/ppermute | solution.py:407
  52.5 1.6 moments.2
  54.1 3.8 %collective-permute-start.14 = (f32[4,576,128]{2,1,0:T(8,128)S(1)}, f32[4,576,128]{2,1,0:T(8,128)S(1)}, u32[]{:S(2)}, u32[]{:S(2)}) collective-permute-start(f32[4,576,128]{2,1,0:T(8,128)S(1)} %get-tuple-element.32), channel_id=1, source_target_pairs={{0,32},{32,0},{64,96},{96,64},{128,160},{160,128},{192,224},{224,1... | collective-permute-start | bytes 3538952 | tf_op jit(solution)/shard_map/ppermute | solution.py:410
  61.6 3.0 %collective-permute-start.16 = (f32[576,128]{1,0:T(8,128)S(1)}, f32[576,128]{1,0:T(8,128)S(1)}, u32[]{:S(2)}, u32[]{:S(2)}) collective-permute-start(f32[576,128]{1,0:T(8,128)S(1)} %get-tuple-element.43), channel_id=1, source_target_pairs={{0,2},{1,3},{2,0},{3,1},{4,6},{5,7},{6,4},{7,5},{8,10},{9,11},{10,... | collective-permute-start | bytes 884744 | tf_op jit(solution)/shard_map/ppermute | solution.py:407
  64.9 2.2 %first.1 = (f32[32,32]{1,0:T(8,128)S(1)}, f32[32,1024]{1,0:T(8,128)S(1)}) custom-call(s32[2]{0:T(128)S(1)} %pad_add_fusion.place, f32[288,128]{1,0:T(8,128)S(1)} %bitcast.47, f32[288,128]{1,0:T(8,128)S(1)} %collective-permute-done.4.refs_1_, f32[288,128]{1,0:T(8,128)S(1)} %collective-permute-done.5.refs_2_, f32[288,128]{1,0:T(8,128)S(1)} %collective-permute-done.6.refs_3_, ...), custom_call_target="tpu_custom_call" | custom-call | tf_op jit(solution)/shard_map/first/pallas_call | solution.py:31
  67.0 4.1 %collective-permute-done.15 = f32[576,128]{1,0:T(8,128)S(1)} collective-permute-done((f32[576,128]{1,0:T(8,128)S(1)}, f32[576,128]{1,0:T(8,128)S(1)}, u32[]{:S(2)}, u32[]{:S(2)}) %collective-permute-start.15) | collective-permute-done | bytes 294944 | tf_op jit(solution)/shard_map/ppermute | solution.py:407
  71.1 7.1 %collective-permute-done.16 = f32[576,128]{1,0:T(8,128)S(1)} collective-permute-done((f32[576,128]{1,0:T(8,128)S(1)}, f32[576,128]{1,0:T(8,128)S(1)}, u32[]{:S(2)}, u32[]{:S(2)}) %collective-permute-start.16) | collective-permute-done | bytes 294944 | tf_op jit(solution)/shard_map/ppermute | solution.py:407
  78.3 30.1 %all_to_all.10 = f32[288,2,128]{2,1,0:T(2,128)S(1)} all-to-all(f32[288,2,128]{2,1,0:T(2,128)S(1)} %bitcast.74), channel_id=1, replica_groups={{0,4,8,12,16,20,24,28,64,68,72,76,80,84,88,92,128,132,136,140,144,148,1..., dimensions={0} | all-to-all | bytes 589824 | tf_op jit(solution)/shard_map/all_to_all | solution.py:434
  108.6 16.1 %all_to_all.11 = f32[288,2,128]{2,1,0:T(2,128)S(1)} all-to-all(f32[288,2,128]{2,1,0:T(2,128)S(1)} %bitcast.73), channel_id=1, replica_groups={{0,4,8,12,16,20,24,28,64,68,72,76,80,84,88,92,128,132,136,140,144,148,1..., dimensions={0} | all-to-all | bytes 589824 | tf_op jit(solution)/shard_map/all_to_all | solution.py:439
  124.7 2.9 %collective-permute-start.18 = (f32[576,128]{1,0:T(8,128)S(1)}, f32[576,128]{1,0:T(8,128)S(1)}, u32[]{:S(2)}, u32[]{:S(2)}) collective-permute-start(f32[576,128]{1,0:T(8,128)S(1)} %bitcast.49), channel_id=1, source_target_pairs={{0,1},{1,2},{2,3},{3,0},{4,5},{5,6},{6,7},{7,4},{8,9},{9,10},{10,1... | collective-permute-start | bytes 884744 | tf_op jit(solution)/shard_map/ppermute | solution.py:407
  127.6 2.8 %collective-permute-start.19 = (f32[576,128]{1,0:T(8,128)S(1)}, f32[576,128]{1,0:T(8,128)S(1)}, u32[]{:S(2)}, u32[]{:S(2)}) collective-permute-start(f32[576,128]{1,0:T(8,128)S(1)} %bitcast.50), channel_id=1, source_target_pairs={{0,2},{1,3},{2,0},{3,1},{4,6},{5,7},{6,4},{7,5},{8,10},{9,11},{10,... | collective-permute-start | bytes 884744 | tf_op jit(solution)/shard_map/ppermute | solution.py:407
  130.5 5.5 %collective-permute-done.18.refs_1_ = f32[576,128]{1,0:T(8,128)S(1)} collective-permute-done((f32[576,128]{1,0:T(8,128)S(1)}, f32[576,128]{1,0:T(8,128)S(1)}, u32[]{:S(2)}, u32[]{:S(2)}) %collective-permute-start.18) | collective-permute-done | bytes 294944 | tf_op jit(solution)/shard_map/ppermute | solution.py:407
  135.9 5.9 %collective-permute-done.19.refs_2_ = f32[576,128]{1,0:T(8,128)S(1)} collective-permute-done((f32[576,128]{1,0:T(8,128)S(1)}, f32[576,128]{1,0:T(8,128)S(1)}, u32[]{:S(2)}, u32[]{:S(2)}) %collective-permute-start.19) | collective-permute-done | bytes 294944 | tf_op jit(solution)/shard_map/ppermute | solution.py:407
  143.8 17.8 %fit.1 = (f32[32,256]{1,0:T(8,128)S(1)}, f32[1,1]{1,0:T(1,128)S(1)}, f32[32,256]{1,0:T(8,128)S(1)}) custom-call(s32[2]{0:T(128)S(1)} %pad_add_fusion.place, f32[576,128]{1,0:T(8,128)S(1)} %bitcast.53, f32[576,128]{1,0:T(8,128)S(1)} %collective-permute-done.18.refs_1_, f32[576,128]{1,0:T(8,128)S(1)} %collective-permute-done.19.refs_2_, ...), custom_call_target="tpu_custom_call" | custom-call | tf_op jit(solution)/shard_map/fit/pallas_call | solution.py:31
  161.7 3.2 %collective-permute-start.26 = (f32[32,256]{1,0:T(8,128)S(1)}, f32[32,256]{1,0:T(8,128)S(1)}, u32[]{:S(2)}, u32[]{:S(2)}) collective-permute-start(f32[32,256]{1,0:T(8,128)S(1)} %get-tuple-element.38.refs_0_), channel_id=1, source_target_pairs={{0,2},{1,3},{2,0},{3,1},{4,6},{5,7},{6,4},{7,5},{8,10},{9,11},{10,... | collective-permute-start | bytes 98312 | tf_op jit(solution)/shard_map/ppermute | solution.py:407
  167.2 1.6 collective-permute-done.27.refs_3_
  168.8 1.8 %clean.1 = f32[1024,256]{1,0:T(8,128)} custom-call(s32[2]{0:T(128)S(1)} %pad_add_fusion.place, f32[32,256]{1,0:T(8,128)S(1)} %get-tuple-element.38.refs_0_, f32[32,256]{1,0:T(8,128)S(1)} %collective-permute-done.25.refs_1_, f32[32,256]{1,0:T(8,128)S(1)} %collective-permute-done.26.refs_2_, f32[32,256]{1,0:T(8,128)S(1)} %collective-permute-done.27.refs_3_, ...), custom_call_target="tpu_custom_call" | custom-call | tf_op jit(solution)/shard_map/clean/pallas_call | solution.py:31
  (62 shorter events, 19.2 us)
Async XLA Ops:
  2.8 8.8 %collective-permute-start.7 = (f32[32,32,128]{2,1,0:T(8,128)S(1)}, f32[32,32,128]{2,1,0:T(8,128)S(1)}, u32[]{:S(2)}, u32[]{:S(2)}) collective-permute-start(f32[32,32,128]{2,1,0:T(8,128)S(1)} %get-tuple-element.44.own), channel_id=1, source_target_pairs={{0,32},{32,64},{64,96},{96,128},{128,160},{160,192},{192,224},{1,3... | collective-permute-start | bytes 1572872 | tf_op jit(solution)/shard_map/ppermute | solution.py:402
  4.6 7.0 %collective-permute-start.8 = (f32[32,32,128]{2,1,0:T(8,128)S(1)}, f32[32,32,128]{2,1,0:T(8,128)S(1)}, u32[]{:S(2)}, u32[]{:S(2)}) collective-permute-start(f32[32,32,128]{2,1,0:T(8,128)S(1)} %get-tuple-element.44.own), channel_id=1, source_target_pairs={{32,0},{64,32},{96,64},{128,96},{160,128},{192,160},{224,192},{33,... | collective-permute-start | bytes 1572872 | tf_op jit(solution)/shard_map/ppermute | solution.py:403
  5.9 14.1 %collective-permute-start = (f32[32,32,128]{2,1,0:T(8,128)S(1)}, f32[32,32,128]{2,1,0:T(8,128)S(1)}, u32[]{:S(2)}, u32[]{:S(2)}) collective-permute-start(f32[32,32,128]{2,1,0:T(8,128)S(1)} %get-tuple-element.45.own), channel_id=1, source_target_pairs={{0,32},{32,64},{64,96},{96,128},{128,160},{160,192},{192,224},{1,3... | collective-permute-start | bytes 1572872 | tf_op jit(solution)/shard_map/ppermute | solution.py:402
  10.3 9.7 %collective-permute-start.1 = (f32[32,32,128]{2,1,0:T(8,128)S(1)}, f32[32,32,128]{2,1,0:T(8,128)S(1)}, u32[]{:S(2)}, u32[]{:S(2)}) collective-permute-start(f32[32,32,128]{2,1,0:T(8,128)S(1)} %get-tuple-element.45.own), channel_id=1, source_target_pairs={{32,0},{64,32},{96,64},{128,96},{160,128},{192,160},{224,192},{33,... | collective-permute-start | bytes 1572872 | tf_op jit(solution)/shard_map/ppermute | solution.py:403
  14.0 14.3 %collective-permute-start.10 = (f32[32,32,128]{2,1,0:T(8,128)S(1)}, f32[32,32,128]{2,1,0:T(8,128)S(1)}, u32[]{:S(2)}, u32[]{:S(2)}) collective-permute-start(f32[32,32,128]{2,1,0:T(8,128)S(1)} %bitcast.40), channel_id=1, source_target_pairs={{4,0},{8,4},{12,8},{16,12},{20,16},{24,20},{28,24},{5,1},{9,5},{13... | collective-permute-start | bytes 1572872 | tf_op jit(solution)/shard_map/ppermute | solution.py:403
  16.2 12.5 %collective-permute-start.9 = (f32[32,32,128]{2,1,0:T(8,128)S(1)}, f32[32,32,128]{2,1,0:T(8,128)S(1)}, u32[]{:S(2)}, u32[]{:S(2)}) collective-permute-start(f32[32,32,128]{2,1,0:T(8,128)S(1)} %bitcast.41), channel_id=1, source_target_pairs={{0,4},{4,8},{8,12},{12,16},{16,20},{20,24},{24,28},{1,5},{5,9},{9,... | collective-permute-start | bytes 1572872 | tf_op jit(solution)/shard_map/ppermute | solution.py:402
  22.4 17.5 %collective-permute-start.2 = (f32[32,32,128]{2,1,0:T(8,128)S(1)}, f32[32,32,128]{2,1,0:T(8,128)S(1)}, u32[]{:S(2)}, u32[]{:S(2)}) collective-permute-start(f32[32,32,128]{2,1,0:T(8,128)S(1)} %bitcast.37), channel_id=1, source_target_pairs={{0,4},{4,8},{8,12},{12,16},{16,20},{20,24},{24,28},{1,5},{5,9},{9,... | collective-permute-start | bytes 1572872 | tf_op jit(solution)/shard_map/ppermute | solution.py:402
  26.2 13.9 %collective-permute-start.3 = (f32[32,32,128]{2,1,0:T(8,128)S(1)}, f32[32,32,128]{2,1,0:T(8,128)S(1)}, u32[]{:S(2)}, u32[]{:S(2)}) collective-permute-start(f32[32,32,128]{2,1,0:T(8,128)S(1)} %bitcast.38), channel_id=1, source_target_pairs={{4,0},{8,4},{12,8},{16,12},{20,16},{24,20},{28,24},{5,1},{9,5},{13... | collective-permute-start | bytes 1572872 | tf_op jit(solution)/shard_map/ppermute | solution.py:403
  32.3 21.8 %copy-start.4 = (f32[9,32,128]{2,1,0:T(8,128)}, f32[9,32,128]{2,1,0:T(8,128)S(1)}, u32[]{:S(2)}) copy-start(f32[9,32,128]{2,1,0:T(8,128)S(1)} %get-tuple-element.28) | copy-start | bytes 442372
  32.4 14.9 %collective-permute-start.11 = (f32[288,128]{1,0:T(8,128)S(1)}, f32[288,128]{1,0:T(8,128)S(1)}, u32[]{:S(2)}, u32[]{:S(2)}) collective-permute-start(f32[288,128]{1,0:T(8,128)S(1)} %bitcast.58), channel_id=1, source_target_pairs={{0,1},{1,2},{2,3},{3,0},{4,5},{5,6},{6,7},{7,4},{8,9},{9,10},{10,1... | collective-permute-start | bytes 442376 | tf_op jit(solution)/shard_map/ppermute | solution.py:407
  33.9 14.7 %collective-permute-start.12 = (f32[288,128]{1,0:T(8,128)S(1)}, f32[288,128]{1,0:T(8,128)S(1)}, u32[]{:S(2)}, u32[]{:S(2)}) collective-permute-start(f32[288,128]{1,0:T(8,128)S(1)} %bitcast.60), channel_id=1, source_target_pairs={{0,2},{1,3},{2,0},{3,1},{4,6},{5,7},{6,4},{7,5},{8,10},{9,11},{10,... | collective-permute-start | bytes 442376 | tf_op jit(solution)/shard_map/ppermute | solution.py:407
  36.6 12.0 %collective-permute-start.13 = (f32[288,128]{1,0:T(8,128)S(1)}, f32[288,128]{1,0:T(8,128)S(1)}, u32[]{:S(2)}, u32[]{:S(2)}) collective-permute-start(f32[288,128]{1,0:T(8,128)S(1)} %bitcast.62), channel_id=1, source_target_pairs={{0,3},{1,0},{2,1},{3,2},{4,7},{5,4},{6,5},{7,6},{8,11},{9,8},{10,9... | collective-permute-start | bytes 442376 | tf_op jit(solution)/shard_map/ppermute | solution.py:407
  42.9 7.6 %collective-permute-start.4 = (f32[288,128]{1,0:T(8,128)S(1)}, f32[288,128]{1,0:T(8,128)S(1)}, u32[]{:S(2)}, u32[]{:S(2)}) collective-permute-start(f32[288,128]{1,0:T(8,128)S(1)} %bitcast.64), channel_id=1, source_target_pairs={{0,1},{1,2},{2,3},{3,0},{4,5},{5,6},{6,7},{7,4},{8,9},{9,10},{10,1... | collective-permute-start | bytes 442376 | tf_op jit(solution)/shard_map/ppermute | solution.py:407
  44.5 8.0 %collective-permute-start.5 = (f32[288,128]{1,0:T(8,128)S(1)}, f32[288,128]{1,0:T(8,128)S(1)}, u32[]{:S(2)}, u32[]{:S(2)}) collective-permute-start(f32[288,128]{1,0:T(8,128)S(1)} %bitcast.66), channel_id=1, source_target_pairs={{0,2},{1,3},{2,0},{3,1},{4,6},{5,7},{6,4},{7,5},{8,10},{9,11},{10,... | collective-permute-start | bytes 442376 | tf_op jit(solution)/shard_map/ppermute | solution.py:407
  47.2 5.3 %collective-permute-start.6 = (f32[288,128]{1,0:T(8,128)S(1)}, f32[288,128]{1,0:T(8,128)S(1)}, u32[]{:S(2)}, u32[]{:S(2)}) collective-permute-start(f32[288,128]{1,0:T(8,128)S(1)} %bitcast.68), channel_id=1, source_target_pairs={{0,3},{1,0},{2,1},{3,2},{4,7},{5,4},{6,5},{7,6},{8,11},{9,8},{10,9... | collective-permute-start | bytes 442376 | tf_op jit(solution)/shard_map/ppermute | solution.py:407
  54.1 6.2 %collective-permute-start.14 = (f32[4,576,128]{2,1,0:T(8,128)S(1)}, f32[4,576,128]{2,1,0:T(8,128)S(1)}, u32[]{:S(2)}, u32[]{:S(2)}) collective-permute-start(f32[4,576,128]{2,1,0:T(8,128)S(1)} %get-tuple-element.32), channel_id=1, source_target_pairs={{0,32},{32,0},{64,96},{96,64},{128,160},{160,128},{192,224},{224,1... | collective-permute-start | bytes 3538952 | tf_op jit(solution)/shard_map/ppermute | solution.py:410
  60.5 10.6 %collective-permute-start.15 = (f32[576,128]{1,0:T(8,128)S(1)}, f32[576,128]{1,0:T(8,128)S(1)}, u32[]{:S(2)}, u32[]{:S(2)}) collective-permute-start(f32[576,128]{1,0:T(8,128)S(1)} %get-tuple-element.41), channel_id=1, source_target_pairs={{0,1},{1,2},{2,3},{3,0},{4,5},{5,6},{6,7},{7,4},{8,9},{9,10},{10,1... | collective-permute-start | bytes 884744 | tf_op jit(solution)/shard_map/ppermute | solution.py:407
  61.6 16.6 %collective-permute-start.16 = (f32[576,128]{1,0:T(8,128)S(1)}, f32[576,128]{1,0:T(8,128)S(1)}, u32[]{:S(2)}, u32[]{:S(2)}) collective-permute-start(f32[576,128]{1,0:T(8,128)S(1)} %get-tuple-element.43), channel_id=1, source_target_pairs={{0,2},{1,3},{2,0},{3,1},{4,6},{5,7},{6,4},{7,5},{8,10},{9,11},{10,... | collective-permute-start | bytes 884744 | tf_op jit(solution)/shard_map/ppermute | solution.py:407
  64.6 13.6 %collective-permute-start.17 = (f32[576,128]{1,0:T(8,128)S(1)}, f32[576,128]{1,0:T(8,128)S(1)}, u32[]{:S(2)}, u32[]{:S(2)}) collective-permute-start(f32[576,128]{1,0:T(8,128)S(1)} %get-tuple-element.42), channel_id=1, source_target_pairs={{0,3},{1,0},{2,1},{3,2},{4,7},{5,4},{6,5},{7,6},{8,11},{9,8},{10,9... | collective-permute-start | bytes 884744 | tf_op jit(solution)/shard_map/ppermute | solution.py:407
  124.7 44.1 %copy-start.3 = (f32[9,32,128]{2,1,0:T(8,128)S(1)}, f32[9,32,128]{2,1,0:T(8,128)}, u32[]{:S(2)}) copy-start(f32[9,32,128]{2,1,0:T(8,128)} %copy-done.2) | copy-start | bytes 442372
  124.7 44.1 %copy-start.5 = (f32[9,32,128]{2,1,0:T(8,128)S(1)}, f32[9,32,128]{2,1,0:T(8,128)}, u32[]{:S(2)}) copy-start(f32[9,32,128]{2,1,0:T(8,128)} %copy-done.4) | copy-start | bytes 442372
  124.7 44.1 %copy-start.7 = (f32[9,32,128]{2,1,0:T(8,128)S(1)}, f32[9,32,128]{2,1,0:T(8,128)}, u32[]{:S(2)}) copy-start(f32[9,32,128]{2,1,0:T(8,128)} %copy-done.6) | copy-start | bytes 442372
  124.7 11.2 %collective-permute-start.18 = (f32[576,128]{1,0:T(8,128)S(1)}, f32[576,128]{1,0:T(8,128)S(1)}, u32[]{:S(2)}, u32[]{:S(2)}) collective-permute-start(f32[576,128]{1,0:T(8,128)S(1)} %bitcast.49), channel_id=1, source_target_pairs={{0,1},{1,2},{2,3},{3,0},{4,5},{5,6},{6,7},{7,4},{8,9},{9,10},{10,1... | collective-permute-start | bytes 884744 | tf_op jit(solution)/shard_map/ppermute | solution.py:407
  127.6 14.2 %collective-permute-start.19 = (f32[576,128]{1,0:T(8,128)S(1)}, f32[576,128]{1,0:T(8,128)S(1)}, u32[]{:S(2)}, u32[]{:S(2)}) collective-permute-start(f32[576,128]{1,0:T(8,128)S(1)} %bitcast.50), channel_id=1, source_target_pairs={{0,2},{1,3},{2,0},{3,1},{4,6},{5,7},{6,4},{7,5},{8,10},{9,11},{10,... | collective-permute-start | bytes 884744 | tf_op jit(solution)/shard_map/ppermute | solution.py:407
  130.5 11.4 %collective-permute-start.20 = (f32[576,128]{1,0:T(8,128)S(1)}, f32[576,128]{1,0:T(8,128)S(1)}, u32[]{:S(2)}, u32[]{:S(2)}) collective-permute-start(f32[576,128]{1,0:T(8,128)S(1)} %bitcast.51), channel_id=1, source_target_pairs={{0,3},{1,0},{2,1},{3,2},{4,7},{5,4},{6,5},{7,6},{8,11},{9,8},{10,9... | collective-permute-start | bytes 884744 | tf_op jit(solution)/shard_map/ppermute | solution.py:407
  130.5 11.9 %collective-permute-start.21 = (f32[576,128]{1,0:T(8,128)S(1)}, f32[576,128]{1,0:T(8,128)S(1)}, u32[]{:S(2)}, u32[]{:S(2)}) collective-permute-start(f32[576,128]{1,0:T(8,128)S(1)} %bitcast.52), channel_id=1, source_target_pairs={{0,32},{32,0},{64,96},{96,64},{128,160},{160,128},{192,224},{224,1... | collective-permute-start | bytes 884744 | tf_op jit(solution)/shard_map/ppermute | solution.py:410
  135.9 6.4 %collective-permute-start.22 = (f32[576,128]{1,0:T(8,128)S(1)}, f32[576,128]{1,0:T(8,128)S(1)}, u32[]{:S(2)}, u32[]{:S(2)}) collective-permute-start(f32[576,128]{1,0:T(8,128)S(1)} %collective-permute-done.18.refs_1_), channel_id=1, source_target_pairs={{0,32},{32,0},{64,96},{96,64},{128,160},{160,128},{192,224},{224,1... | collective-permute-start | bytes 884744 | tf_op jit(solution)/shard_map/ppermute | solution.py:410
  141.8 1.6 collective-permute-start.23
  141.8 2.0 %collective-permute-start.24 = (f32[576,128]{1,0:T(8,128)S(1)}, f32[576,128]{1,0:T(8,128)S(1)}, u32[]{:S(2)}, u32[]{:S(2)}) collective-permute-start(f32[576,128]{1,0:T(8,128)S(1)} %collective-permute-done.20.refs_3_), channel_id=1, source_target_pairs={{0,32},{32,0},{64,96},{96,64},{128,160},{160,128},{192,224},{224,1... | collective-permute-start | bytes 884744 | tf_op jit(solution)/shard_map/ppermute | solution.py:410
  161.6 5.2 %collective-permute-start.25 = (f32[32,256]{1,0:T(8,128)S(1)}, f32[32,256]{1,0:T(8,128)S(1)}, u32[]{:S(2)}, u32[]{:S(2)}) collective-permute-start(f32[32,256]{1,0:T(8,128)S(1)} %get-tuple-element.38.refs_0_), channel_id=1, source_target_pairs={{0,1},{1,2},{2,3},{3,0},{4,5},{5,6},{6,7},{7,4},{8,9},{9,10},{10,1... | collective-permute-start | bytes 98312 | tf_op jit(solution)/shard_map/ppermute | solution.py:407
  161.7 5.5 %collective-permute-start.26 = (f32[32,256]{1,0:T(8,128)S(1)}, f32[32,256]{1,0:T(8,128)S(1)}, u32[]{:S(2)}, u32[]{:S(2)}) collective-permute-start(f32[32,256]{1,0:T(8,128)S(1)} %get-tuple-element.38.refs_0_), channel_id=1, source_target_pairs={{0,2},{1,3},{2,0},{3,1},{4,6},{5,7},{6,4},{7,5},{8,10},{9,11},{10,... | collective-permute-start | bytes 98312 | tf_op jit(solution)/shard_map/ppermute | solution.py:407
  164.9 3.9 %collective-permute-start.27 = (f32[32,256]{1,0:T(8,128)S(1)}, f32[32,256]{1,0:T(8,128)S(1)}, u32[]{:S(2)}, u32[]{:S(2)}) collective-permute-start(f32[32,256]{1,0:T(8,128)S(1)} %get-tuple-element.38.refs_0_), channel_id=1, source_target_pairs={{0,3},{1,0},{2,1},{3,2},{4,7},{5,4},{6,5},{7,6},{8,11},{9,8},{10,9... | collective-permute-start | bytes 98312 | tf_op jit(solution)/shard_map/ppermute | solution.py:407
  (5 other events, 68.3 us)

commit v5 on v4

--- a/solution.py
+++ b/solution.py
@@ -101,23 +101,20 @@
     return call(kernel, [(b // 8, 8, a, f)], low, own, high, taps, name="beam")[0]
 
 
-def parted_kernel(half, place, low, own, high, taps, loads, *outs):
-    parts = len(outs)
+def parted_kernel(half, k, parts, place, low, own, high, taps, loads, out):
     length = own.shape[0]
     lanes = lanes_of(half, own)
-    for k, out in enumerate(outs):
-        strip((low, own, high), taps, lanes, lax.rem(place[1] + k, parts), out)
-        for e in range(out.shape[0] - 8):
-            out[8 + e] = loads[e * length : (e + 1) * length, lanes]
-
-
-def parted_beam(place, low, own, high, taps, half, loads, parts):
+    strip((low, own, high), taps, lanes, lax.rem(place[1] + k, parts), out)
+    for e in range(out.shape[0] - 8):
+        out[8 + e] = loads[e * length : (e + 1) * length, lanes]
+
+
+def parted_beam(place, low, own, high, taps, half, loads, k, parts):
     a, b, f = own.shape
     assert taps.shape[0] == 2 * a + 1 and b == 8 * parts
     shape = (8 + loads.shape[0] // a, a, f)
-    kernel = functools.partial(parted_kernel, half)
-    outs = call(kernel, [shape] * parts, place, low, own, high, taps, loads, name="beam")
-    return [x.reshape(-1, f) for x in outs]
+    kernel = functools.partial(parted_kernel, half, k, parts)
+    return call(kernel, [shape], place, low, own, high, taps, loads, name="beam")[0].reshape(-1, f)
 
 
 def source(place, k, parts):
@@ -149,18 +146,18 @@
     for k in range(parts):
         i = row_block(place, c, k, parts)
         at = [lax.rem(i + j, blocks) for j in range(parts)]
-        left = jnp.concatenate([lo[i], hi[i], hi[i]], axis=0)
+        left = jnp.concatenate([lo[i], lo[i], hi[i], hi[i]], axis=0)
         high = jnp.concatenate([hi[b] for b in at], axis=1)
         low = jnp.concatenate([lo[b] for b in at], axis=1)
-        right = jnp.concatenate([high, low, high], axis=0)
+        right = jnp.concatenate([low, high, low, high], axis=0)
         block = lax.dot_general(left, right, dims, preferred_element_type=jnp.float32)
         for j in range(parts):
             out[k, j * width : (j + 1) * width, :] = block[:, j * width : (j + 1) * width]
         m = lax.rem(i, parts)
-        left = jnp.concatenate([lo[m], hi[m], hi[m]], axis=0)
+        left = jnp.concatenate([lo[m], lo[m], hi[m], hi[m]], axis=0)
         left = jnp.where(upper, left[:, :half], left[:, half:])
         m = m + parts
-        right = jnp.concatenate([hi[m], lo[m], hi[m]], axis=0)
+        right = jnp.concatenate([lo[m], hi[m], lo[m], hi[m]], axis=0)
         out[k, parts * width :, :] = lax.dot_general(
             left, right, dims, preferred_element_type=jnp.float32
         )
@@ -266,17 +263,21 @@
     return call(first_kernel, [(n, n), shape], place, *slots, name="first", scratch=scratch)
 
 
-def cross_of(stacked, hi, lo):
+def cross_of(stacked, hi, mid, low):
     n = stacked.shape[0] // 3
-    top = jnp.dot(stacked, hi[...], preferred_element_type=jnp.float32)
-    low = jnp.dot(stacked[: 2 * n], lo[...], preferred_element_type=jnp.float32)
-    return top[:n] + (top[n : 2 * n] + low[:n] + (top[2 * n :] + low[n:]))
+
+    def product(count, ref):
+        return jnp.dot(stacked[: count * n], ref[...], preferred_element_type=jnp.float32)
+
+    top, middle, last = product(3, hi), product(2, mid), product(1, low)
+    small = top[2 * n :] + middle[n:] + last
+    return top[:n] + (top[n : 2 * n] + middle[:n] + small)
 
 
 def fit_kernel(pixel_total, parts, place, *refs):
     slots = refs[: 2 * parts]
     inverse0, weight0, map_hi, map_lo = refs[2 * parts : 2 * parts + 4]
-    block_out, noise_out, lat_out, hi, lo, held = refs[2 * parts + 4 :]
+    block_out, noise_out, lat_out, hi, mid, low, held = refs[2 * parts + 4 :]
     width = slots[0].shape[1]
     blocks = 2 * parts
     freqs = blocks * width
@@ -287,11 +288,9 @@
     def place_block(i, j, block, mirror):
         rows = pl.ds(pl.multiple_of(i * width, width), width)
         cols = pl.ds(pl.multiple_of(j * width, width), width)
-        top, rest, _ = split3(block)
-        hi[rows, cols], lo[rows, cols] = top, rest
+        hi[rows, cols], mid[rows, cols], low[rows, cols] = split3(block)
         if mirror:
-            top, rest, _ = split3(block.T)
-            hi[cols, rows], lo[cols, rows] = top, rest
+            hi[cols, rows], mid[cols, rows], low[cols, rows] = split3(block.T)
 
     for s, ref in enumerate(slots):
         i = row_block(place, s // parts, parts - s % parts, parts)
@@ -311,7 +310,7 @@
     def step(_, state):
         inverse, weight, noise = state
         stacked = parts_of(weight)
-        cross = cross_of(stacked, hi, lo)
+        cross = cross_of(stacked, hi, mid, low)
         pieces = parts_of(cross)
         scaled = pixel_total * noise * inverse + gram_of(pieces, stacked)
         updated = times(inverse_spd(scaled), pieces)
@@ -353,7 +352,7 @@
         [(n, freqs // parts), (1, 1), (n, hi.shape[1])],
         place, *slots, inverse0, weight0, hi, lo,
         name="fit",
-        scratch=[VM((freqs, freqs), jnp.bfloat16)] * 2 + [VM((n, freqs), jnp.float32)],
+        scratch=[VM((freqs, freqs), jnp.bfloat16)] * 3 + [VM((n, freqs), jnp.float32)],
     )
 
 
@@ -416,9 +415,15 @@
         smoothed = beam(around[h][0], masked[h], around[h][1], row_taps.T, h)
         smoothed = smoothed.reshape(cols_here, rows_here, width)
         low, high = halos(smoothed, "sy", sy)
-        slots = parted_beam(place, low, smoothed, high, column_taps.T, h, init_loadings.T, af)
+        slots, here = [None] * af, [None] * af
+        for k in (*range(af // 2, af), *range(af // 2)):
+            operands = (low, smoothed, high)
+            slots[k] = parted_beam(
+                place, *operands, column_taps.T, h, init_loadings.T, k, af
+            )
+            here[k] = shifted(slots[k], k) if k > 0 else slots[k]
         beamed += slots
-        traded += slots[:1] + [shifted(slots[k], k) for k in range(1, af)]
+        traded += here
 
     theirs, partial, hi, lo = moments(place, traded, pixels)
     partial = partial + swapped(theirs)

time: 172 us -> 174 us (1.012)
  Pallas kernels: 35.3 us -> 40.9 us
  starting transfers between devices: 49.7 us -> 46 us
    pallas_call x9 -> x15, Pallas kernels: 35.3 us -> 40.9 us  [call(): pl.pallas_call(kernel, out_shape=outs, in_specs=specs, out_specs=[pl.Bloc...]
    ppermute x5, starting transfers between devices: 4.28 us -> 2.07 us  [swapped(): return lax.ppermute(block, 'sx', [(i, i ^ 1) for i in range(sx)])]
  transfers between devices with their start and end apart: 28 -> 28, of which waited for: 15 -> 14; matrix products, arithmetic and copies ran while one was open for 0% -> 0% of each run, Pallas kernels for 8% -> 10%
where the time goes in v5:
time: 174 us; the launch traced here: 173 us
  blocking collectives  46.6 us (27%)
  starting transfers between devices  46 us (26%)
  Pallas kernels  40.9 us (24%)
  waiting for transfers between devices  33.9 us (19%)
  other arithmetic  2.53 us (1%)
  between operations  2.21 us (1%)
    all_to_all x2, blocking collectives, body(): lax.all_to_all(pieces, ('sx', 'sy'), 0, 0, axis_index_groups=groups, tile...  46.6 us
    pallas_call x15, Pallas kernels, call(): pl.pallas_call(kernel, out_shape=outs, in_specs=specs, out_specs=[pl.Bloc...  40.9 us
    ppermute x15, waiting for transfers between devices, shifted(): return lax.ppermute(block, 'af', [(i, (i + k) % af) for i in range(af)])  28 us
    ppermute x15, starting transfers between devices, shifted(): return lax.ppermute(block, 'af', [(i, (i + k) % af) for i in range(af)])  23.4 us
    ppermute x4, starting transfers between devices, halos(): low = lax.ppermute(block, axis, [(i, i + 1) for i in range(count - 1)])  13.8 us
    ppermute x4, starting transfers between devices, halos(): high = lax.ppermute(block, axis, [(i + 1, i) for i in range(count - 1)])  6.78 us
  transfers between devices with their start and end apart: 28, of which 14 were waited for; matrix products, arithmetic and copies ran while one was open for 0% of the time, Pallas kernels for 10%

profile of v5, /device:TPU:32, one launch (start us, length us, event | category | flops | bytes accessed | tf_op | source)
XLA Modules:
  0.0 173.0 jit_solution(1756678602867215587)
XLA Ops:
  1.4 1.4 slice_multiply_fusion
  2.8 1.8 %collective-permute-start.7 = (f32[32,32,128]{2,1,0:T(8,128)S(1)}, f32[32,32,128]{2,1,0:T(8,128)S(1)}, u32[]{:S(2)}, u32[]{:S(2)}) collective-permute-start(f32[32,32,128]{2,1,0:T(8,128)S(1)} %get-tuple-element.28.own), channel_id=1, source_target_pairs={{0,32},{32,64},{64,96},{96,128},{128,160},{160,192},{192,224},{1,3... | collective-permute-start | bytes 1572872 | tf_op jit(solution)/shard_map/ppermute | solution.py:401
  4.6 1.3 collective-permute-start.8
  5.9 4.4 %collective-permute-start = (f32[32,32,128]{2,1,0:T(8,128)S(1)}, f32[32,32,128]{2,1,0:T(8,128)S(1)}, u32[]{:S(2)}, u32[]{:S(2)}) collective-permute-start(f32[32,32,128]{2,1,0:T(8,128)S(1)} %get-tuple-element.29.own), channel_id=1, source_target_pairs={{0,32},{32,64},{64,96},{96,128},{128,160},{160,192},{192,224},{1,3... | collective-permute-start | bytes 1572872 | tf_op jit(solution)/shard_map/ppermute | solution.py:401
  10.3 1.3 collective-permute-start.1
  11.6 2.4 %beam.15 = f32[4,8,32,128]{3,2,1,0:T(8,128)S(1)} custom-call(f32[32,32,128]{2,1,0:T(8,128)S(1)} %collective-permute-done.7.low, f32[32,32,128]{2,1,0:T(8,128)S(1)} %get-tuple-element.28.own, f32[32,32,128]{2,1,0:T(8,128)S(1)} %collective-permute-done.8.high, f32[65,256]{1,0:T(8,128)S(1)} %bitcast.88), custom_call_target="tpu_custom_call" | custom-call | tf_op jit(solution)/shard_map/beam/pallas_call | solution.py:31
  14.0 2.1 %collective-permute-start.10 = (f32[32,32,128]{2,1,0:T(8,128)S(1)}, f32[32,32,128]{2,1,0:T(8,128)S(1)}, u32[]{:S(2)}, u32[]{:S(2)}) collective-permute-start(f32[32,32,128]{2,1,0:T(8,128)S(1)} %bitcast.37), channel_id=1, source_target_pairs={{4,0},{8,4},{12,8},{16,12},{20,16},{24,20},{28,24},{5,1},{9,5},{13... | collective-permute-start | bytes 1572872 | tf_op jit(solution)/shard_map/ppermute | solution.py:402
  16.2 3.8 %collective-permute-start.9 = (f32[32,32,128]{2,1,0:T(8,128)S(1)}, f32[32,32,128]{2,1,0:T(8,128)S(1)}, u32[]{:S(2)}, u32[]{:S(2)}) collective-permute-start(f32[32,32,128]{2,1,0:T(8,128)S(1)} %bitcast.38), channel_id=1, source_target_pairs={{0,4},{4,8},{8,12},{12,16},{16,20},{20,24},{24,28},{1,5},{5,9},{9,... | collective-permute-start | bytes 1572872 | tf_op jit(solution)/shard_map/ppermute | solution.py:401
  20.0 2.3 %beam.10 = f32[4,8,32,128]{3,2,1,0:T(8,128)S(1)} custom-call(f32[32,32,128]{2,1,0:T(8,128)S(1)} %collective-permute-done.low, f32[32,32,128]{2,1,0:T(8,128)S(1)} %get-tuple-element.29.own, f32[32,32,128]{2,1,0:T(8,128)S(1)} %collective-permute-done.1.high, f32[65,256]{1,0:T(8,128)S(1)} %bitcast.89), custom_call_target="tpu_custom_call" | custom-call | tf_op jit(solution)/shard_map/beam/pallas_call | solution.py:31
  22.4 3.8 %collective-permute-start.2 = (f32[32,32,128]{2,1,0:T(8,128)S(1)}, f32[32,32,128]{2,1,0:T(8,128)S(1)}, u32[]{:S(2)}, u32[]{:S(2)}) collective-permute-start(f32[32,32,128]{2,1,0:T(8,128)S(1)} %bitcast.43), channel_id=1, source_target_pairs={{0,4},{4,8},{8,12},{12,16},{16,20},{20,24},{24,28},{1,5},{5,9},{9,... | collective-permute-start | bytes 1572872 | tf_op jit(solution)/shard_map/ppermute | solution.py:401
  26.2 2.0 %collective-permute-start.3 = (f32[32,32,128]{2,1,0:T(8,128)S(1)}, f32[32,32,128]{2,1,0:T(8,128)S(1)}, u32[]{:S(2)}, u32[]{:S(2)}) collective-permute-start(f32[32,32,128]{2,1,0:T(8,128)S(1)} %bitcast.44), channel_id=1, source_target_pairs={{4,0},{8,4},{12,8},{16,12},{20,16},{24,20},{28,24},{5,1},{9,5},{13... | collective-permute-start | bytes 1572872 | tf_op jit(solution)/shard_map/ppermute | solution.py:402
  29.8 2.8 %collective-permute-start.13 = (f32[288,128]{1,0:T(8,128)S(1)}, f32[288,128]{1,0:T(8,128)S(1)}, u32[]{:S(2)}, u32[]{:S(2)}) collective-permute-start(f32[288,128]{1,0:T(8,128)S(1)} %bitcast.76), channel_id=1, source_target_pairs={{0,3},{1,0},{2,1},{3,2},{4,7},{5,4},{6,5},{7,6},{8,11},{9,8},{10,9... | collective-permute-start | bytes 442376 | tf_op jit(solution)/shard_map/ppermute | solution.py:406
  36.8 3.1 %collective-permute-done.2.low = f32[32,32,128]{2,1,0:T(8,128)S(1)} collective-permute-done((f32[32,32,128]{2,1,0:T(8,128)S(1)}, f32[32,32,128]{2,1,0:T(8,128)S(1)}, u32[]{:S(2)}, u32[]{:S(2)}) %collective-permute-start.2) | collective-permute-done | bytes 524320 | tf_op jit(solution)/shard_map/ppermute | solution.py:401
  41.2 2.9 %collective-permute-start.6 = (f32[288,128]{1,0:T(8,128)S(1)}, f32[288,128]{1,0:T(8,128)S(1)}, u32[]{:S(2)}, u32[]{:S(2)}) collective-permute-start(f32[288,128]{1,0:T(8,128)S(1)} %bitcast.82), channel_id=1, source_target_pairs={{0,3},{1,0},{2,1},{3,2},{4,7},{5,4},{6,5},{7,6},{8,11},{9,8},{10,9... | collective-permute-start | bytes 442376 | tf_op jit(solution)/shard_map/ppermute | solution.py:406
  52.0 3.4 %collective-permute-done.4.refs_1_ = f32[288,128]{1,0:T(8,128)S(1)} collective-permute-done((f32[288,128]{1,0:T(8,128)S(1)}, f32[288,128]{1,0:T(8,128)S(1)}, u32[]{:S(2)}, u32[]{:S(2)}) %collective-permute-start.4) | collective-permute-done | bytes 147488 | tf_op jit(solution)/shard_map/ppermute | solution.py:406
  55.4 1.7 moments.2
  57.1 1.6 collective-permute-start.14
  58.7 1.6 moments.3
  61.4 1.7 collective-permute-start.16
  63.1 2.4 %collective-permute-start.17 = (f32[576,128]{1,0:T(8,128)S(1)}, f32[576,128]{1,0:T(8,128)S(1)}, u32[]{:S(2)}, u32[]{:S(2)}) collective-permute-start(f32[576,128]{1,0:T(8,128)S(1)} %get-tuple-element.26), channel_id=1, source_target_pairs={{0,3},{1,0},{2,1},{3,2},{4,7},{5,4},{6,5},{7,6},{8,11},{9,8},{10,9... | collective-permute-start | bytes 884744 | tf_op jit(solution)/shard_map/ppermute | solution.py:406
  65.6 2.2 %first.1 = (f32[32,32]{1,0:T(8,128)S(1)}, f32[32,1024]{1,0:T(8,128)S(1)}) custom-call(s32[2]{0:T(128)S(1)} %pad_add_fusion.place, f32[288,128]{1,0:T(8,128)S(1)} %bitcast.61, f32[288,128]{1,0:T(8,128)S(1)} %collective-permute-done.4.refs_1_, f32[288,128]{1,0:T(8,128)S(1)} %collective-permute-done.5.refs_2_, f32[288,128]{1,0:T(8,128)S(1)} %collective-permute-done.6.refs_3_, ...), custom_call_target="tpu_custom_call" | custom-call | tf_op jit(solution)/shard_map/first/pallas_call | solution.py:31
  67.8 10.5 %collective-permute-done.15 = f32[576,128]{1,0:T(8,128)S(1)} collective-permute-done((f32[576,128]{1,0:T(8,128)S(1)}, f32[576,128]{1,0:T(8,128)S(1)}, u32[]{:S(2)}, u32[]{:S(2)}) %collective-permute-start.15) | collective-permute-done | bytes 294944 | tf_op jit(solution)/shard_map/ppermute | solution.py:406
  78.9 30.6 %all_to_all.10 = f32[288,2,128]{2,1,0:T(2,128)S(1)} all-to-all(f32[288,2,128]{2,1,0:T(2,128)S(1)} %bitcast.92), channel_id=1, replica_groups={{0,4,8,12,16,20,24,28,64,68,72,76,80,84,88,92,128,132,136,140,144,148,1..., dimensions={0} | all-to-all | bytes 589824 | tf_op jit(solution)/shard_map/all_to_all | solution.py:439
  109.7 16.1 %all_to_all.11 = f32[288,2,128]{2,1,0:T(2,128)S(1)} all-to-all(f32[288,2,128]{2,1,0:T(2,128)S(1)} %bitcast.91), channel_id=1, replica_groups={{0,4,8,12,16,20,24,28,64,68,72,76,80,84,88,92,128,132,136,140,144,148,1..., dimensions={0} | all-to-all | bytes 589824 | tf_op jit(solution)/shard_map/all_to_all | solution.py:444
  125.8 2.1 %collective-permute-start.18 = (f32[576,128]{1,0:T(8,128)S(1)}, f32[576,128]{1,0:T(8,128)S(1)}, u32[]{:S(2)}, u32[]{:S(2)}) collective-permute-start(f32[576,128]{1,0:T(8,128)S(1)} %bitcast.71), channel_id=1, source_target_pairs={{0,1},{1,2},{2,3},{3,0},{4,5},{5,6},{6,7},{7,4},{8,9},{9,10},{10,1... | collective-permute-start | bytes 884744 | tf_op jit(solution)/shard_map/ppermute | solution.py:406
  127.8 2.7 %collective-permute-start.19 = (f32[576,128]{1,0:T(8,128)S(1)}, f32[576,128]{1,0:T(8,128)S(1)}, u32[]{:S(2)}, u32[]{:S(2)}) collective-permute-start(f32[576,128]{1,0:T(8,128)S(1)} %bitcast.72), channel_id=1, source_target_pairs={{0,2},{1,3},{2,0},{3,1},{4,6},{5,7},{6,4},{7,5},{8,10},{9,11},{10,... | collective-permute-start | bytes 884744 | tf_op jit(solution)/shard_map/ppermute | solution.py:406
  130.6 6.0 %collective-permute-done.18.refs_1_ = f32[576,128]{1,0:T(8,128)S(1)} collective-permute-done((f32[576,128]{1,0:T(8,128)S(1)}, f32[576,128]{1,0:T(8,128)S(1)}, u32[]{:S(2)}, u32[]{:S(2)}) %collective-permute-start.18) | collective-permute-done | bytes 294944 | tf_op jit(solution)/shard_map/ppermute | solution.py:406
  136.6 4.4 %collective-permute-done.19.refs_2_ = f32[576,128]{1,0:T(8,128)S(1)} collective-permute-done((f32[576,128]{1,0:T(8,128)S(1)}, f32[576,128]{1,0:T(8,128)S(1)}, u32[]{:S(2)}, u32[]{:S(2)}) %collective-permute-start.19) | collective-permute-done | bytes 294944 | tf_op jit(solution)/shard_map/ppermute | solution.py:406
  143.0 19.8 %fit.1 = (f32[32,256]{1,0:T(8,128)S(1)}, f32[1,1]{1,0:T(1,128)S(1)}, f32[32,256]{1,0:T(8,128)S(1)}) custom-call(s32[2]{0:T(128)S(1)} %pad_add_fusion.place, f32[576,128]{1,0:T(8,128)S(1)} %bitcast.75, f32[576,128]{1,0:T(8,128)S(1)} %collective-permute-done.18.refs_1_, f32[576,128]{1,0:T(8,128)S(1)} %collective-permute-done.19.refs_2_, ...), custom_call_target="tpu_custom_call" | custom-call | tf_op jit(solution)/shard_map/fit/pallas_call | solution.py:31
  164.0 2.2 %collective-permute-start.26 = (f32[32,256]{1,0:T(8,128)S(1)}, f32[32,256]{1,0:T(8,128)S(1)}, u32[]{:S(2)}, u32[]{:S(2)}) collective-permute-start(f32[32,256]{1,0:T(8,128)S(1)} %get-tuple-element.22.refs_0_), channel_id=1, source_target_pairs={{0,2},{1,3},{2,0},{3,1},{4,6},{5,7},{6,4},{7,5},{8,10},{9,11},{10,... | collective-permute-start | bytes 98312 | tf_op jit(solution)/shard_map/ppermute | solution.py:406
  166.1 1.5 collective-permute-start.27
  170.1 1.8 %clean.1 = f32[1024,256]{1,0:T(8,128)} custom-call(s32[2]{0:T(128)S(1)} %pad_add_fusion.place, f32[32,256]{1,0:T(8,128)S(1)} %get-tuple-element.22.refs_0_, f32[32,256]{1,0:T(8,128)S(1)} %collective-permute-done.25.refs_1_, f32[32,256]{1,0:T(8,128)S(1)} %collective-permute-done.26.refs_2_, f32[32,256]{1,0:T(8,128)S(1)} %collective-permute-done.27.refs_3_, ...), custom_call_target="tpu_custom_call" | custom-call | tf_op jit(solution)/shard_map/clean/pallas_call | solution.py:31
  (76 shorter events, 23.2 us)
Async XLA Ops:
  2.8 8.8 %collective-permute-start.7 = (f32[32,32,128]{2,1,0:T(8,128)S(1)}, f32[32,32,128]{2,1,0:T(8,128)S(1)}, u32[]{:S(2)}, u32[]{:S(2)}) collective-permute-start(f32[32,32,128]{2,1,0:T(8,128)S(1)} %get-tuple-element.28.own), channel_id=1, source_target_pairs={{0,32},{32,64},{64,96},{96,128},{128,160},{160,192},{192,224},{1,3... | collective-permute-start | bytes 1572872 | tf_op jit(solution)/shard_map/ppermute | solution.py:401
  4.6 7.0 %collective-permute-start.8 = (f32[32,32,128]{2,1,0:T(8,128)S(1)}, f32[32,32,128]{2,1,0:T(8,128)S(1)}, u32[]{:S(2)}, u32[]{:S(2)}) collective-permute-start(f32[32,32,128]{2,1,0:T(8,128)S(1)} %get-tuple-element.28.own), channel_id=1, source_target_pairs={{32,0},{64,32},{96,64},{128,96},{160,128},{192,160},{224,192},{33,... | collective-permute-start | bytes 1572872 | tf_op jit(solution)/shard_map/ppermute | solution.py:402
  5.9 14.1 %collective-permute-start = (f32[32,32,128]{2,1,0:T(8,128)S(1)}, f32[32,32,128]{2,1,0:T(8,128)S(1)}, u32[]{:S(2)}, u32[]{:S(2)}) collective-permute-start(f32[32,32,128]{2,1,0:T(8,128)S(1)} %get-tuple-element.29.own), channel_id=1, source_target_pairs={{0,32},{32,64},{64,96},{96,128},{128,160},{160,192},{192,224},{1,3... | collective-permute-start | bytes 1572872 | tf_op jit(solution)/shard_map/ppermute | solution.py:401
  10.3 9.7 %collective-permute-start.1 = (f32[32,32,128]{2,1,0:T(8,128)S(1)}, f32[32,32,128]{2,1,0:T(8,128)S(1)}, u32[]{:S(2)}, u32[]{:S(2)}) collective-permute-start(f32[32,32,128]{2,1,0:T(8,128)S(1)} %get-tuple-element.29.own), channel_id=1, source_target_pairs={{32,0},{64,32},{96,64},{128,96},{160,128},{192,160},{224,192},{33,... | collective-permute-start | bytes 1572872 | tf_op jit(solution)/shard_map/ppermute | solution.py:402
  14.0 14.3 %collective-permute-start.10 = (f32[32,32,128]{2,1,0:T(8,128)S(1)}, f32[32,32,128]{2,1,0:T(8,128)S(1)}, u32[]{:S(2)}, u32[]{:S(2)}) collective-permute-start(f32[32,32,128]{2,1,0:T(8,128)S(1)} %bitcast.37), channel_id=1, source_target_pairs={{4,0},{8,4},{12,8},{16,12},{20,16},{24,20},{28,24},{5,1},{9,5},{13... | collective-permute-start | bytes 1572872 | tf_op jit(solution)/shard_map/ppermute | solution.py:402
  16.2 12.5 %collective-permute-start.9 = (f32[32,32,128]{2,1,0:T(8,128)S(1)}, f32[32,32,128]{2,1,0:T(8,128)S(1)}, u32[]{:S(2)}, u32[]{:S(2)}) collective-permute-start(f32[32,32,128]{2,1,0:T(8,128)S(1)} %bitcast.38), channel_id=1, source_target_pairs={{0,4},{4,8},{8,12},{12,16},{16,20},{20,24},{24,28},{1,5},{5,9},{9,... | collective-permute-start | bytes 1572872 | tf_op jit(solution)/shard_map/ppermute | solution.py:401
  22.4 17.5 %collective-permute-start.2 = (f32[32,32,128]{2,1,0:T(8,128)S(1)}, f32[32,32,128]{2,1,0:T(8,128)S(1)}, u32[]{:S(2)}, u32[]{:S(2)}) collective-permute-start(f32[32,32,128]{2,1,0:T(8,128)S(1)} %bitcast.43), channel_id=1, source_target_pairs={{0,4},{4,8},{8,12},{12,16},{16,20},{20,24},{24,28},{1,5},{5,9},{9,... | collective-permute-start | bytes 1572872 | tf_op jit(solution)/shard_map/ppermute | solution.py:401
  26.2 13.9 %collective-permute-start.3 = (f32[32,32,128]{2,1,0:T(8,128)S(1)}, f32[32,32,128]{2,1,0:T(8,128)S(1)}, u32[]{:S(2)}, u32[]{:S(2)}) collective-permute-start(f32[32,32,128]{2,1,0:T(8,128)S(1)} %bitcast.44), channel_id=1, source_target_pairs={{4,0},{8,4},{12,8},{16,12},{20,16},{24,20},{28,24},{5,1},{9,5},{13... | collective-permute-start | bytes 1572872 | tf_op jit(solution)/shard_map/ppermute | solution.py:402
  29.8 17.4 %collective-permute-start.13 = (f32[288,128]{1,0:T(8,128)S(1)}, f32[288,128]{1,0:T(8,128)S(1)}, u32[]{:S(2)}, u32[]{:S(2)}) collective-permute-start(f32[288,128]{1,0:T(8,128)S(1)} %bitcast.76), channel_id=1, source_target_pairs={{0,3},{1,0},{2,1},{3,2},{4,7},{5,4},{6,5},{7,6},{8,11},{9,8},{10,9... | collective-permute-start | bytes 442376 | tf_op jit(solution)/shard_map/ppermute | solution.py:406
  33.7 16.9 %collective-permute-start.12 = (f32[288,128]{1,0:T(8,128)S(1)}, f32[288,128]{1,0:T(8,128)S(1)}, u32[]{:S(2)}, u32[]{:S(2)}) collective-permute-start(f32[288,128]{1,0:T(8,128)S(1)} %bitcast.78), channel_id=1, source_target_pairs={{0,2},{1,3},{2,0},{3,1},{4,6},{5,7},{6,4},{7,5},{8,10},{9,11},{10,... | collective-permute-start | bytes 442376 | tf_op jit(solution)/shard_map/ppermute | solution.py:406
  35.8 14.9 %collective-permute-start.11 = (f32[288,128]{1,0:T(8,128)S(1)}, f32[288,128]{1,0:T(8,128)S(1)}, u32[]{:S(2)}, u32[]{:S(2)}) collective-permute-start(f32[288,128]{1,0:T(8,128)S(1)} %bitcast.80), channel_id=1, source_target_pairs={{0,1},{1,2},{2,3},{3,0},{4,5},{5,6},{6,7},{7,4},{8,9},{9,10},{10,1... | collective-permute-start | bytes 442376 | tf_op jit(solution)/shard_map/ppermute | solution.py:406
  41.2 9.5 %collective-permute-start.6 = (f32[288,128]{1,0:T(8,128)S(1)}, f32[288,128]{1,0:T(8,128)S(1)}, u32[]{:S(2)}, u32[]{:S(2)}) collective-permute-start(f32[288,128]{1,0:T(8,128)S(1)} %bitcast.82), channel_id=1, source_target_pairs={{0,3},{1,0},{2,1},{3,2},{4,7},{5,4},{6,5},{7,6},{8,11},{9,8},{10,9... | collective-permute-start | bytes 442376 | tf_op jit(solution)/shard_map/ppermute | solution.py:406
  45.2 6.7 %collective-permute-start.5 = (f32[288,128]{1,0:T(8,128)S(1)}, f32[288,128]{1,0:T(8,128)S(1)}, u32[]{:S(2)}, u32[]{:S(2)}) collective-permute-start(f32[288,128]{1,0:T(8,128)S(1)} %bitcast.84), channel_id=1, source_target_pairs={{0,2},{1,3},{2,0},{3,1},{4,6},{5,7},{6,4},{7,5},{8,10},{9,11},{10,... | collective-permute-start | bytes 442376 | tf_op jit(solution)/shard_map/ppermute | solution.py:406
  47.2 8.2 %collective-permute-start.4 = (f32[288,128]{1,0:T(8,128)S(1)}, f32[288,128]{1,0:T(8,128)S(1)}, u32[]{:S(2)}, u32[]{:S(2)}) collective-permute-start(f32[288,128]{1,0:T(8,128)S(1)} %bitcast.86), channel_id=1, source_target_pairs={{0,1},{1,2},{2,3},{3,0},{4,5},{5,6},{6,7},{7,4},{8,9},{9,10},{10,1... | collective-permute-start | bytes 442376 | tf_op jit(solution)/shard_map/ppermute | solution.py:406
  57.1 4.0 %collective-permute-start.14 = (f32[4,576,128]{2,1,0:T(8,128)S(1)}, f32[4,576,128]{2,1,0:T(8,128)S(1)}, u32[]{:S(2)}, u32[]{:S(2)}) collective-permute-start(f32[4,576,128]{2,1,0:T(8,128)S(1)} %get-tuple-element.16), channel_id=1, source_target_pairs={{0,32},{32,0},{64,96},{96,64},{128,160},{160,128},{192,224},{224,1... | collective-permute-start | bytes 3538952 | tf_op jit(solution)/shard_map/ppermute | solution.py:409
  61.4 16.9 %collective-permute-start.15 = (f32[576,128]{1,0:T(8,128)S(1)}, f32[576,128]{1,0:T(8,128)S(1)}, u32[]{:S(2)}, u32[]{:S(2)}) collective-permute-start(f32[576,128]{1,0:T(8,128)S(1)} %get-tuple-element.25), channel_id=1, source_target_pairs={{0,1},{1,2},{2,3},{3,0},{4,5},{5,6},{6,7},{7,4},{8,9},{9,10},{10,1... | collective-permute-start | bytes 884744 | tf_op jit(solution)/shard_map/ppermute | solution.py:406
  61.4 16.8 %collective-permute-start.16 = (f32[576,128]{1,0:T(8,128)S(1)}, f32[576,128]{1,0:T(8,128)S(1)}, u32[]{:S(2)}, u32[]{:S(2)}) collective-permute-start(f32[576,128]{1,0:T(8,128)S(1)} %get-tuple-element.27), channel_id=1, source_target_pairs={{0,2},{1,3},{2,0},{3,1},{4,6},{5,7},{6,4},{7,5},{8,10},{9,11},{10,... | collective-permute-start | bytes 884744 | tf_op jit(solution)/shard_map/ppermute | solution.py:406
  63.1 15.7 %collective-permute-start.17 = (f32[576,128]{1,0:T(8,128)S(1)}, f32[576,128]{1,0:T(8,128)S(1)}, u32[]{:S(2)}, u32[]{:S(2)}) collective-permute-start(f32[576,128]{1,0:T(8,128)S(1)} %get-tuple-element.26), channel_id=1, source_target_pairs={{0,3},{1,0},{2,1},{3,2},{4,7},{5,4},{6,5},{7,6},{8,11},{9,8},{10,9... | collective-permute-start | bytes 884744 | tf_op jit(solution)/shard_map/ppermute | solution.py:406
  125.8 44.3 %copy-start.5 = (f32[9,32,128]{2,1,0:T(8,128)S(1)}, f32[9,32,128]{2,1,0:T(8,128)}, u32[]{:S(2)}) copy-start(f32[9,32,128]{2,1,0:T(8,128)} %copy-done.4) | copy-start | bytes 442372
  125.8 44.3 %copy-start.7 = (f32[9,32,128]{2,1,0:T(8,128)S(1)}, f32[9,32,128]{2,1,0:T(8,128)}, u32[]{:S(2)}) copy-start(f32[9,32,128]{2,1,0:T(8,128)} %copy-done.6) | copy-start | bytes 442372
  125.8 44.3 %copy-start.9 = (f32[9,32,128]{2,1,0:T(8,128)S(1)}, f32[9,32,128]{2,1,0:T(8,128)}, u32[]{:S(2)}) copy-start(f32[9,32,128]{2,1,0:T(8,128)} %copy-done.8) | copy-start | bytes 442372
  125.8 44.3 %copy-start.11 = (f32[9,32,128]{2,1,0:T(8,128)S(1)}, f32[9,32,128]{2,1,0:T(8,128)}, u32[]{:S(2)}) copy-start(f32[9,32,128]{2,1,0:T(8,128)} %copy-done.10) | copy-start | bytes 442372
  125.8 10.8 %collective-permute-start.18 = (f32[576,128]{1,0:T(8,128)S(1)}, f32[576,128]{1,0:T(8,128)S(1)}, u32[]{:S(2)}, u32[]{:S(2)}) collective-permute-start(f32[576,128]{1,0:T(8,128)S(1)} %bitcast.71), channel_id=1, source_target_pairs={{0,1},{1,2},{2,3},{3,0},{4,5},{5,6},{6,7},{7,4},{8,9},{9,10},{10,1... | collective-permute-start | bytes 884744 | tf_op jit(solution)/shard_map/ppermute | solution.py:406
  127.8 13.2 %collective-permute-start.19 = (f32[576,128]{1,0:T(8,128)S(1)}, f32[576,128]{1,0:T(8,128)S(1)}, u32[]{:S(2)}, u32[]{:S(2)}) collective-permute-start(f32[576,128]{1,0:T(8,128)S(1)} %bitcast.72), channel_id=1, source_target_pairs={{0,2},{1,3},{2,0},{3,1},{4,6},{5,7},{6,4},{7,5},{8,10},{9,11},{10,... | collective-permute-start | bytes 884744 | tf_op jit(solution)/shard_map/ppermute | solution.py:406
  130.5 10.5 %collective-permute-start.20 = (f32[576,128]{1,0:T(8,128)S(1)}, f32[576,128]{1,0:T(8,128)S(1)}, u32[]{:S(2)}, u32[]{:S(2)}) collective-permute-start(f32[576,128]{1,0:T(8,128)S(1)} %bitcast.73), channel_id=1, source_target_pairs={{0,3},{1,0},{2,1},{3,2},{4,7},{5,4},{6,5},{7,6},{8,11},{9,8},{10,9... | collective-permute-start | bytes 884744 | tf_op jit(solution)/shard_map/ppermute | solution.py:406
  130.6 10.9 %collective-permute-start.21 = (f32[576,128]{1,0:T(8,128)S(1)}, f32[576,128]{1,0:T(8,128)S(1)}, u32[]{:S(2)}, u32[]{:S(2)}) collective-permute-start(f32[576,128]{1,0:T(8,128)S(1)} %bitcast.74), channel_id=1, source_target_pairs={{0,32},{32,0},{64,96},{96,64},{128,160},{160,128},{192,224},{224,1... | collective-permute-start | bytes 884744 | tf_op jit(solution)/shard_map/ppermute | solution.py:409
  136.6 5.0 %collective-permute-start.22 = (f32[576,128]{1,0:T(8,128)S(1)}, f32[576,128]{1,0:T(8,128)S(1)}, u32[]{:S(2)}, u32[]{:S(2)}) collective-permute-start(f32[576,128]{1,0:T(8,128)S(1)} %collective-permute-done.18.refs_1_), channel_id=1, source_target_pairs={{0,32},{32,0},{64,96},{96,64},{128,160},{160,128},{192,224},{224,1... | collective-permute-start | bytes 884744 | tf_op jit(solution)/shard_map/ppermute | solution.py:409
  141.0 1.6 collective-permute-start.23
  141.0 2.0 %collective-permute-start.24 = (f32[576,128]{1,0:T(8,128)S(1)}, f32[576,128]{1,0:T(8,128)S(1)}, u32[]{:S(2)}, u32[]{:S(2)}) collective-permute-start(f32[576,128]{1,0:T(8,128)S(1)} %collective-permute-done.20.refs_3_), channel_id=1, source_target_pairs={{0,32},{32,0},{64,96},{96,64},{128,160},{160,128},{192,224},{224,1... | collective-permute-start | bytes 884744 | tf_op jit(solution)/shard_map/ppermute | solution.py:409
  162.9 5.4 %collective-permute-start.25 = (f32[32,256]{1,0:T(8,128)S(1)}, f32[32,256]{1,0:T(8,128)S(1)}, u32[]{:S(2)}, u32[]{:S(2)}) collective-permute-start(f32[32,256]{1,0:T(8,128)S(1)} %get-tuple-element.22.refs_0_), channel_id=1, source_target_pairs={{0,1},{1,2},{2,3},{3,0},{4,5},{5,6},{6,7},{7,4},{8,9},{9,10},{10,1... | collective-permute-start | bytes 98312 | tf_op jit(solution)/shard_map/ppermute | solution.py:406
  164.0 5.4 %collective-permute-start.26 = (f32[32,256]{1,0:T(8,128)S(1)}, f32[32,256]{1,0:T(8,128)S(1)}, u32[]{:S(2)}, u32[]{:S(2)}) collective-permute-start(f32[32,256]{1,0:T(8,128)S(1)} %get-tuple-element.22.refs_0_), channel_id=1, source_target_pairs={{0,2},{1,3},{2,0},{3,1},{4,6},{5,7},{6,4},{7,5},{8,10},{9,11},{10,... | collective-permute-start | bytes 98312 | tf_op jit(solution)/shard_map/ppermute | solution.py:406
  166.1 3.9 %collective-permute-start.27 = (f32[32,256]{1,0:T(8,128)S(1)}, f32[32,256]{1,0:T(8,128)S(1)}, u32[]{:S(2)}, u32[]{:S(2)}) collective-permute-start(f32[32,256]{1,0:T(8,128)S(1)} %get-tuple-element.22.refs_0_), channel_id=1, source_target_pairs={{0,3},{1,0},{2,1},{3,2},{4,7},{5,4},{6,5},{7,6},{8,11},{9,8},{10,9... | collective-permute-start | bytes 98312 | tf_op jit(solution)/shard_map/ppermute | solution.py:406
  (9 other events, 115.2 us)

commit v6 on v5

--- a/solution.py
+++ b/solution.py
@@ -239,28 +239,8 @@
     return jnp.dot(left, right, preferred_element_type=jnp.float32)
 
 
-def weights(pieces, gram, noise):
-    inverse = inverse_spd(gram + jnp.where(identity(gram.shape[0]), noise, 0.0))
-    return inverse, times(inverse, pieces)
-
-
-def first_kernel(place, *refs):
-    slots, (inverse_out, weight_out, loads) = refs[:-3], refs[-3:]
-    parts = len(slots) // 2
-    n = weight_out.shape[0]
-    rows, width = slots[0].shape
-    for s, ref in enumerate(slots):
-        b = 2 * source(place, s % parts, parts) + s // parts
-        loads[:, pl.ds(pl.multiple_of(b * width, width), width)] = ref[rows - n : rows]
-    pieces = parts_of(loads[...])
-    gram = gram_of(pieces, pieces)
-    inverse_out[...], weight_out[...] = weights(pieces, gram, jnp.ones((1, 1), jnp.float32))
-
-
-def first_weights(place, slots, n):
-    shape = (n, len(slots) * slots[0].shape[1])
-    scratch = [VM(shape, jnp.float32)]
-    return call(first_kernel, [(n, n), shape], place, *slots, name="first", scratch=scratch)
+def regularized(gram, noise):
+    return inverse_spd(gram + jnp.where(identity(gram.shape[0]), noise, 0.0))
 
 
 def cross_of(stacked, hi, mid, low):
@@ -275,13 +255,13 @@
 
 
 def fit_kernel(pixel_total, parts, place, *refs):
-    slots = refs[: 2 * parts]
-    inverse0, weight0, map_hi, map_lo = refs[2 * parts : 2 * parts + 4]
-    block_out, noise_out, lat_out, hi, mid, low, held = refs[2 * parts + 4 :]
+    slots, maps = refs[: 2 * parts], refs[2 * parts : 4 * parts]
+    map_hi, map_lo = refs[4 * parts : 4 * parts + 2]
+    block_out, noise_out, lat_out, hi, mid, low, held = refs[4 * parts + 2 :]
     width = slots[0].shape[1]
     blocks = 2 * parts
     freqs = blocks * width
-    n = weight0.shape[0]
+    n = held.shape[0]
     diagonal = identity(width)
     power = jnp.zeros((width, width), jnp.float32)
 
@@ -307,12 +287,20 @@
         place_block(m, m + parts, block, True)
     power = total(power)
 
+    for p, ref in enumerate(maps):
+        b = 2 * source(place, p % parts, parts) + p // parts
+        rows = ref.shape[0]
+        held[:, pl.ds(pl.multiple_of(b * width, width), width)] = ref[rows - n : rows]
+
     def step(_, state):
-        inverse, weight, noise = state
-        stacked = parts_of(weight)
-        cross = cross_of(stacked, hi, mid, low)
+        gram, noise = state
+        pieces = parts_of(held[...])
+        raw = cross_of(pieces, hi, mid, low)
+        inverse = regularized(gram, noise)
+        weight = parts_of(times(inverse, pieces))
+        cross = times(inverse, parts_of(raw))
         pieces = parts_of(cross)
-        scaled = pixel_total * noise * inverse + gram_of(pieces, stacked)
+        scaled = pixel_total * noise * inverse + gram_of(pieces, weight)
         updated = times(inverse_spd(scaled), pieces)
         held[...] = updated
         pieces = parts_of(updated)
@@ -320,10 +308,12 @@
         noise = (power - 2.0 * total(updated * cross) + total(scaled * gram)) / (
             pixel_total * freqs
         )
-        return (*weights(pieces, gram, noise), noise)
-
-    state = (inverse0[...], weight0[...], jnp.ones((1, 1), jnp.float32))
-    _, weight, noise = lax.fori_loop(0, ITERS, step, state)
+        return gram, noise
+
+    pieces = parts_of(held[...])
+    state = (gram_of(pieces, pieces), jnp.ones((1, 1), jnp.float32))
+    gram, noise = lax.fori_loop(0, ITERS, step, state)
+    weight = times(regularized(gram, noise), parts_of(held[...]))
     noise_out[...] = noise
     here = block_out.shape[1]
     block_out[...] = held[:, pl.ds(pl.multiple_of(place[1] * here, here), here)]
@@ -344,13 +334,13 @@
     lat_out[...] = latent
 
 
-def fit(place, slots, inverse0, weight0, hi, lo, pixel_total):
-    n, freqs = weight0.shape
-    parts = hi.shape[0] // 2
+def fit(place, slots, maps, hi, lo, n, pixel_total):
+    blocks, pixels, width = hi.shape
+    freqs = blocks * width
     return call(
-        functools.partial(fit_kernel, pixel_total, parts),
-        [(n, freqs // parts), (1, 1), (n, hi.shape[1])],
-        place, *slots, inverse0, weight0, hi, lo,
+        functools.partial(fit_kernel, pixel_total, blocks // 2),
+        [(n, 2 * width), (1, 1), (n, pixels)],
+        place, *slots, *maps, hi, lo,
         name="fit",
         scratch=[VM((freqs, freqs), jnp.bfloat16)] * 3 + [VM((n, freqs), jnp.float32)],
     )
@@ -427,11 +417,9 @@
 
     theirs, partial, hi, lo = moments(place, traded, pixels)
     partial = partial + swapped(theirs)
-    inverse0, weight0 = first_weights(place, traded, n)
     piece = partial[0]
     for k in range(1, af):
         piece = piece + shifted(partial[k], k)
-    piece, inverse0, weight0 = lax.optimization_barrier((piece, inverse0, weight0))
     ranks = sx * sy // 2
     groups = [[s * sy + t for s in range(c, sx, 2) for t in range(sy)] for c in range(2)]
     shape = piece.shape
@@ -449,7 +437,7 @@
     other = [swapped(x) for x in mine]
 
     loads_here, noise, latent = fit(
-        place, mine + other, inverse0, weight0, hi, lo, float(pixels_here * sx * sy)
+        place, mine + other, traded, hi, lo, n, float(pixels_here * sx * sy)
     )
     latents = [latent] + [shifted(latent, k) for k in range(1, af)]
     cleaned = clean(place, beamed, latents, loads_here)

time: 174 us -> 171 us (0.983)
  Pallas kernels: 40.9 us -> 35.9 us
  waiting for transfers between devices: 33.9 us -> 36.1 us
    pallas_call x15 -> x14, Pallas kernels: 40.9 us -> 35.9 us  [call(): pl.pallas_call(kernel, out_shape=outs, in_specs=specs, out_specs=[pl.Bloc...]
    ppermute x15, waiting for transfers between devices: 28 us -> 30.2 us  [shifted(): return lax.ppermute(block, 'af', [(i, (i + k) % af) for i in range(af)])]
  transfers between devices with their start and end apart: 28 -> 28, of which waited for: 14 -> 14; matrix products, arithmetic and copies ran while one was open for 0% -> 0% of each run, Pallas kernels for 10% -> 9%
where the time goes in v6:
time: 171 us
  blocking collectives  46.7 us (27%)
  starting transfers between devices  46 us (27%)
  waiting for transfers between devices  36.1 us (21%)
  Pallas kernels  35.9 us (21%)
  other arithmetic  2.56 us (1%)
  between operations  2.35 us (1%)
    all_to_all x2, blocking collectives, body(): lax.all_to_all(pieces, ('sx', 'sy'), 0, 0, axis_index_groups=groups, tile...  46.7 us
    pallas_call x14, Pallas kernels, call(): pl.pallas_call(kernel, out_shape=outs, in_specs=specs, out_specs=[pl.Bloc...  35.9 us
    ppermute x15, waiting for transfers between devices, shifted(): return lax.ppermute(block, 'af', [(i, (i + k) % af) for i in range(af)])  30.2 us
    ppermute x15, starting transfers between devices, shifted(): return lax.ppermute(block, 'af', [(i, (i + k) % af) for i in range(af)])  23.4 us
    ppermute x4, starting transfers between devices, halos(): low = lax.ppermute(block, axis, [(i, i + 1) for i in range(count - 1)])  13.8 us
    ppermute x4, starting transfers between devices, halos(): high = lax.ppermute(block, axis, [(i + 1, i) for i in range(count - 1)])  6.78 us
  transfers between devices with their start and end apart: 28, of which 14 were waited for; matrix products, arithmetic and copies ran while one was open for 0% of the time, Pallas kernels for 9%

profile of v6, /device:TPU:32, one launch (start us, length us, event | category | flops | bytes accessed | tf_op | source)
XLA Modules:
  0.0 170.5 jit_solution(4965796428480029023)
XLA Ops:
  1.4 1.4 slice_multiply_fusion
  2.8 1.8 %collective-permute-start.7 = (f32[32,32,128]{2,1,0:T(8,128)S(1)}, f32[32,32,128]{2,1,0:T(8,128)S(1)}, u32[]{:S(2)}, u32[]{:S(2)}) collective-permute-start(f32[32,32,128]{2,1,0:T(8,128)S(1)} %get-tuple-element.18.own), channel_id=1, source_target_pairs={{0,32},{32,64},{64,96},{96,128},{128,160},{160,192},{192,224},{1,3... | collective-permute-start | bytes 1572872 | tf_op jit(solution)/shard_map/ppermute | solution.py:391
  4.6 1.3 collective-permute-start.8
  5.9 4.4 %collective-permute-start = (f32[32,32,128]{2,1,0:T(8,128)S(1)}, f32[32,32,128]{2,1,0:T(8,128)S(1)}, u32[]{:S(2)}, u32[]{:S(2)}) collective-permute-start(f32[32,32,128]{2,1,0:T(8,128)S(1)} %get-tuple-element.19.own), channel_id=1, source_target_pairs={{0,32},{32,64},{64,96},{96,128},{128,160},{160,192},{192,224},{1,3... | collective-permute-start | bytes 1572872 | tf_op jit(solution)/shard_map/ppermute | solution.py:391
  10.3 1.3 collective-permute-start.1
  11.6 2.4 %beam.15 = f32[4,8,32,128]{3,2,1,0:T(8,128)S(1)} custom-call(f32[32,32,128]{2,1,0:T(8,128)S(1)} %collective-permute-done.7.low, f32[32,32,128]{2,1,0:T(8,128)S(1)} %get-tuple-element.18.own, f32[32,32,128]{2,1,0:T(8,128)S(1)} %collective-permute-done.8.high, f32[65,256]{1,0:T(8,128)S(1)} %bitcast.88), custom_call_target="tpu_custom_call" | custom-call | tf_op jit(solution)/shard_map/beam/pallas_call | solution.py:31
  14.0 2.1 %collective-permute-start.10 = (f32[32,32,128]{2,1,0:T(8,128)S(1)}, f32[32,32,128]{2,1,0:T(8,128)S(1)}, u32[]{:S(2)}, u32[]{:S(2)}) collective-permute-start(f32[32,32,128]{2,1,0:T(8,128)S(1)} %bitcast.37), channel_id=1, source_target_pairs={{4,0},{8,4},{12,8},{16,12},{20,16},{24,20},{28,24},{5,1},{9,5},{13... | collective-permute-start | bytes 1572872 | tf_op jit(solution)/shard_map/ppermute | solution.py:392
  16.2 3.8 %collective-permute-start.9 = (f32[32,32,128]{2,1,0:T(8,128)S(1)}, f32[32,32,128]{2,1,0:T(8,128)S(1)}, u32[]{:S(2)}, u32[]{:S(2)}) collective-permute-start(f32[32,32,128]{2,1,0:T(8,128)S(1)} %bitcast.38), channel_id=1, source_target_pairs={{0,4},{4,8},{8,12},{12,16},{16,20},{20,24},{24,28},{1,5},{5,9},{9,... | collective-permute-start | bytes 1572872 | tf_op jit(solution)/shard_map/ppermute | solution.py:391
  20.0 2.3 %beam.10 = f32[4,8,32,128]{3,2,1,0:T(8,128)S(1)} custom-call(f32[32,32,128]{2,1,0:T(8,128)S(1)} %collective-permute-done.low, f32[32,32,128]{2,1,0:T(8,128)S(1)} %get-tuple-element.19.own, f32[32,32,128]{2,1,0:T(8,128)S(1)} %collective-permute-done.1.high, f32[65,256]{1,0:T(8,128)S(1)} %bitcast.89), custom_call_target="tpu_custom_call" | custom-call | tf_op jit(solution)/shard_map/beam/pallas_call | solution.py:31
  22.4 3.8 %collective-permute-start.2 = (f32[32,32,128]{2,1,0:T(8,128)S(1)}, f32[32,32,128]{2,1,0:T(8,128)S(1)}, u32[]{:S(2)}, u32[]{:S(2)}) collective-permute-start(f32[32,32,128]{2,1,0:T(8,128)S(1)} %bitcast.43), channel_id=1, source_target_pairs={{0,4},{4,8},{8,12},{12,16},{16,20},{20,24},{24,28},{1,5},{5,9},{9,... | collective-permute-start | bytes 1572872 | tf_op jit(solution)/shard_map/ppermute | solution.py:391
  26.2 2.0 %collective-permute-start.3 = (f32[32,32,128]{2,1,0:T(8,128)S(1)}, f32[32,32,128]{2,1,0:T(8,128)S(1)}, u32[]{:S(2)}, u32[]{:S(2)}) collective-permute-start(f32[32,32,128]{2,1,0:T(8,128)S(1)} %bitcast.44), channel_id=1, source_target_pairs={{4,0},{8,4},{12,8},{16,12},{20,16},{24,20},{28,24},{5,1},{9,5},{13... | collective-permute-start | bytes 1572872 | tf_op jit(solution)/shard_map/ppermute | solution.py:392
  29.8 2.8 %collective-permute-start.13 = (f32[288,128]{1,0:T(8,128)S(1)}, f32[288,128]{1,0:T(8,128)S(1)}, u32[]{:S(2)}, u32[]{:S(2)}) collective-permute-start(f32[288,128]{1,0:T(8,128)S(1)} %bitcast.76), channel_id=1, source_target_pairs={{0,3},{1,0},{2,1},{3,2},{4,7},{5,4},{6,5},{7,6},{8,11},{9,8},{10,9... | collective-permute-start | bytes 442376 | tf_op jit(solution)/shard_map/ppermute | solution.py:396
  36.8 3.1 %collective-permute-done.2.low = f32[32,32,128]{2,1,0:T(8,128)S(1)} collective-permute-done((f32[32,32,128]{2,1,0:T(8,128)S(1)}, f32[32,32,128]{2,1,0:T(8,128)S(1)}, u32[]{:S(2)}, u32[]{:S(2)}) %collective-permute-start.2) | collective-permute-done | bytes 524320 | tf_op jit(solution)/shard_map/ppermute | solution.py:391
  41.2 2.9 %collective-permute-start.6 = (f32[288,128]{1,0:T(8,128)S(1)}, f32[288,128]{1,0:T(8,128)S(1)}, u32[]{:S(2)}, u32[]{:S(2)}) collective-permute-start(f32[288,128]{1,0:T(8,128)S(1)} %bitcast.82), channel_id=1, source_target_pairs={{0,3},{1,0},{2,1},{3,2},{4,7},{5,4},{6,5},{7,6},{8,11},{9,8},{10,9... | collective-permute-start | bytes 442376 | tf_op jit(solution)/shard_map/ppermute | solution.py:396
  50.7 1.2 collective-permute-done.5.refs_2_.refs_10_
  52.0 3.4 %collective-permute-done.4.refs_1_.refs_9_ = f32[288,128]{1,0:T(8,128)S(1)} collective-permute-done((f32[288,128]{1,0:T(8,128)S(1)}, f32[288,128]{1,0:T(8,128)S(1)}, u32[]{:S(2)}, u32[]{:S(2)}) %collective-permute-start.4) | collective-permute-done | bytes 147488 | tf_op jit(solution)/shard_map/ppermute | solution.py:396
  55.4 1.7 moments.2
  57.1 1.6 collective-permute-start.14
  58.7 1.6 moments.3
  61.5 1.7 collective-permute-start.16
  63.2 2.4 %collective-permute-start.17 = (f32[576,128]{1,0:T(8,128)S(1)}, f32[576,128]{1,0:T(8,128)S(1)}, u32[]{:S(2)}, u32[]{:S(2)}) collective-permute-start(f32[576,128]{1,0:T(8,128)S(1)} %get-tuple-element.16), channel_id=1, source_target_pairs={{0,3},{1,0},{2,1},{3,2},{4,7},{5,4},{6,5},{7,6},{8,11},{9,8},{10,9... | collective-permute-start | bytes 884744 | tf_op jit(solution)/shard_map/ppermute | solution.py:396
  65.6 12.7 %collective-permute-done.15 = f32[576,128]{1,0:T(8,128)S(1)} collective-permute-done((f32[576,128]{1,0:T(8,128)S(1)}, f32[576,128]{1,0:T(8,128)S(1)}, u32[]{:S(2)}, u32[]{:S(2)}) %collective-permute-start.15) | collective-permute-done | bytes 294944 | tf_op jit(solution)/shard_map/ppermute | solution.py:396
  79.0 30.7 %all_to_all.10 = f32[288,2,128]{2,1,0:T(2,128)S(1)} all-to-all(f32[288,2,128]{2,1,0:T(2,128)S(1)} %bitcast.92), channel_id=1, replica_groups={{0,4,8,12,16,20,24,28,64,68,72,76,80,84,88,92,128,132,136,140,144,148,1..., dimensions={0} | all-to-all | bytes 589824 | tf_op jit(solution)/shard_map/all_to_all | solution.py:427
  109.9 16.1 %all_to_all.11 = f32[288,2,128]{2,1,0:T(2,128)S(1)} all-to-all(f32[288,2,128]{2,1,0:T(2,128)S(1)} %bitcast.91), channel_id=1, replica_groups={{0,4,8,12,16,20,24,28,64,68,72,76,80,84,88,92,128,132,136,140,144,148,1..., dimensions={0} | all-to-all | bytes 589824 | tf_op jit(solution)/shard_map/all_to_all | solution.py:432
  126.0 2.1 %collective-permute-start.18 = (f32[576,128]{1,0:T(8,128)S(1)}, f32[576,128]{1,0:T(8,128)S(1)}, u32[]{:S(2)}, u32[]{:S(2)}) collective-permute-start(f32[576,128]{1,0:T(8,128)S(1)} %bitcast.71), channel_id=1, source_target_pairs={{0,1},{1,2},{2,3},{3,0},{4,5},{5,6},{6,7},{7,4},{8,9},{9,10},{10,1... | collective-permute-start | bytes 884744 | tf_op jit(solution)/shard_map/ppermute | solution.py:396
  128.1 2.7 %collective-permute-start.19 = (f32[576,128]{1,0:T(8,128)S(1)}, f32[576,128]{1,0:T(8,128)S(1)}, u32[]{:S(2)}, u32[]{:S(2)}) collective-permute-start(f32[576,128]{1,0:T(8,128)S(1)} %bitcast.72), channel_id=1, source_target_pairs={{0,2},{1,3},{2,0},{3,1},{4,6},{5,7},{6,4},{7,5},{8,10},{9,11},{10,... | collective-permute-start | bytes 884744 | tf_op jit(solution)/shard_map/ppermute | solution.py:396
  130.9 6.0 %collective-permute-done.18.refs_1_ = f32[576,128]{1,0:T(8,128)S(1)} collective-permute-done((f32[576,128]{1,0:T(8,128)S(1)}, f32[576,128]{1,0:T(8,128)S(1)}, u32[]{:S(2)}, u32[]{:S(2)}) %collective-permute-start.18) | collective-permute-done | bytes 294944 | tf_op jit(solution)/shard_map/ppermute | solution.py:396
  136.8 4.4 %collective-permute-done.19.refs_2_ = f32[576,128]{1,0:T(8,128)S(1)} collective-permute-done((f32[576,128]{1,0:T(8,128)S(1)}, f32[576,128]{1,0:T(8,128)S(1)}, u32[]{:S(2)}, u32[]{:S(2)}) %collective-permute-start.19) | collective-permute-done | bytes 294944 | tf_op jit(solution)/shard_map/ppermute | solution.py:396
  143.3 17.1 %fit.1 = (f32[32,256]{1,0:T(8,128)S(1)}, f32[1,1]{1,0:T(1,128)S(1)}, f32[32,256]{1,0:T(8,128)S(1)}) custom-call(s32[2]{0:T(128)S(1)} %pad_add_fusion.place, f32[576,128]{1,0:T(8,128)S(1)} %bitcast.75, f32[576,128]{1,0:T(8,128)S(1)} %collective-permute-done.18.refs_1_, f32[576,128]{1,0:T(8,128)S(1)} %collective-permute-done.19.refs_2_, ...), custom_call_target="tpu_custom_call" | custom-call | tf_op jit(solution)/shard_map/fit/pallas_call | solution.py:31
  161.4 2.2 %collective-permute-start.26 = (f32[32,256]{1,0:T(8,128)S(1)}, f32[32,256]{1,0:T(8,128)S(1)}, u32[]{:S(2)}, u32[]{:S(2)}) collective-permute-start(f32[32,256]{1,0:T(8,128)S(1)} %get-tuple-element.12.refs_0_), channel_id=1, source_target_pairs={{0,2},{1,3},{2,0},{3,1},{4,6},{5,7},{6,4},{7,5},{8,10},{9,11},{10,... | collective-permute-start | bytes 98312 | tf_op jit(solution)/shard_map/ppermute | solution.py:396
  163.7 1.5 collective-permute-start.27
  167.6 1.8 %clean.1 = f32[1024,256]{1,0:T(8,128)} custom-call(s32[2]{0:T(128)S(1)} %pad_add_fusion.place, f32[32,256]{1,0:T(8,128)S(1)} %get-tuple-element.12.refs_0_, f32[32,256]{1,0:T(8,128)S(1)} %collective-permute-done.25.refs_1_, f32[32,256]{1,0:T(8,128)S(1)} %collective-permute-done.26.refs_2_, f32[32,256]{1,0:T(8,128)S(1)} %collective-permute-done.27.refs_3_, ...), custom_call_target="tpu_custom_call" | custom-call | tf_op jit(solution)/shard_map/clean/pallas_call | solution.py:31
  (99 shorter events, 22.0 us)
Async XLA Ops:
  2.8 8.8 %collective-permute-start.7 = (f32[32,32,128]{2,1,0:T(8,128)S(1)}, f32[32,32,128]{2,1,0:T(8,128)S(1)}, u32[]{:S(2)}, u32[]{:S(2)}) collective-permute-start(f32[32,32,128]{2,1,0:T(8,128)S(1)} %get-tuple-element.18.own), channel_id=1, source_target_pairs={{0,32},{32,64},{64,96},{96,128},{128,160},{160,192},{192,224},{1,3... | collective-permute-start | bytes 1572872 | tf_op jit(solution)/shard_map/ppermute | solution.py:391
  4.6 7.0 %collective-permute-start.8 = (f32[32,32,128]{2,1,0:T(8,128)S(1)}, f32[32,32,128]{2,1,0:T(8,128)S(1)}, u32[]{:S(2)}, u32[]{:S(2)}) collective-permute-start(f32[32,32,128]{2,1,0:T(8,128)S(1)} %get-tuple-element.18.own), channel_id=1, source_target_pairs={{32,0},{64,32},{96,64},{128,96},{160,128},{192,160},{224,192},{33,... | collective-permute-start | bytes 1572872 | tf_op jit(solution)/shard_map/ppermute | solution.py:392
  5.9 14.1 %collective-permute-start = (f32[32,32,128]{2,1,0:T(8,128)S(1)}, f32[32,32,128]{2,1,0:T(8,128)S(1)}, u32[]{:S(2)}, u32[]{:S(2)}) collective-permute-start(f32[32,32,128]{2,1,0:T(8,128)S(1)} %get-tuple-element.19.own), channel_id=1, source_target_pairs={{0,32},{32,64},{64,96},{96,128},{128,160},{160,192},{192,224},{1,3... | collective-permute-start | bytes 1572872 | tf_op jit(solution)/shard_map/ppermute | solution.py:391
  10.3 9.7 %collective-permute-start.1 = (f32[32,32,128]{2,1,0:T(8,128)S(1)}, f32[32,32,128]{2,1,0:T(8,128)S(1)}, u32[]{:S(2)}, u32[]{:S(2)}) collective-permute-start(f32[32,32,128]{2,1,0:T(8,128)S(1)} %get-tuple-element.19.own), channel_id=1, source_target_pairs={{32,0},{64,32},{96,64},{128,96},{160,128},{192,160},{224,192},{33,... | collective-permute-start | bytes 1572872 | tf_op jit(solution)/shard_map/ppermute | solution.py:392
  14.0 14.3 %collective-permute-start.10 = (f32[32,32,128]{2,1,0:T(8,128)S(1)}, f32[32,32,128]{2,1,0:T(8,128)S(1)}, u32[]{:S(2)}, u32[]{:S(2)}) collective-permute-start(f32[32,32,128]{2,1,0:T(8,128)S(1)} %bitcast.37), channel_id=1, source_target_pairs={{4,0},{8,4},{12,8},{16,12},{20,16},{24,20},{28,24},{5,1},{9,5},{13... | collective-permute-start | bytes 1572872 | tf_op jit(solution)/shard_map/ppermute | solution.py:392
  16.2 12.5 %collective-permute-start.9 = (f32[32,32,128]{2,1,0:T(8,128)S(1)}, f32[32,32,128]{2,1,0:T(8,128)S(1)}, u32[]{:S(2)}, u32[]{:S(2)}) collective-permute-start(f32[32,32,128]{2,1,0:T(8,128)S(1)} %bitcast.38), channel_id=1, source_target_pairs={{0,4},{4,8},{8,12},{12,16},{16,20},{20,24},{24,28},{1,5},{5,9},{9,... | collective-permute-start | bytes 1572872 | tf_op jit(solution)/shard_map/ppermute | solution.py:391
  22.4 17.5 %collective-permute-start.2 = (f32[32,32,128]{2,1,0:T(8,128)S(1)}, f32[32,32,128]{2,1,0:T(8,128)S(1)}, u32[]{:S(2)}, u32[]{:S(2)}) collective-permute-start(f32[32,32,128]{2,1,0:T(8,128)S(1)} %bitcast.43), channel_id=1, source_target_pairs={{0,4},{4,8},{8,12},{12,16},{16,20},{20,24},{24,28},{1,5},{5,9},{9,... | collective-permute-start | bytes 1572872 | tf_op jit(solution)/shard_map/ppermute | solution.py:391
  26.2 13.9 %collective-permute-start.3 = (f32[32,32,128]{2,1,0:T(8,128)S(1)}, f32[32,32,128]{2,1,0:T(8,128)S(1)}, u32[]{:S(2)}, u32[]{:S(2)}) collective-permute-start(f32[32,32,128]{2,1,0:T(8,128)S(1)} %bitcast.44), channel_id=1, source_target_pairs={{4,0},{8,4},{12,8},{16,12},{20,16},{24,20},{28,24},{5,1},{9,5},{13... | collective-permute-start | bytes 1572872 | tf_op jit(solution)/shard_map/ppermute | solution.py:392
  29.8 17.4 %collective-permute-start.13 = (f32[288,128]{1,0:T(8,128)S(1)}, f32[288,128]{1,0:T(8,128)S(1)}, u32[]{:S(2)}, u32[]{:S(2)}) collective-permute-start(f32[288,128]{1,0:T(8,128)S(1)} %bitcast.76), channel_id=1, source_target_pairs={{0,3},{1,0},{2,1},{3,2},{4,7},{5,4},{6,5},{7,6},{8,11},{9,8},{10,9... | collective-permute-start | bytes 442376 | tf_op jit(solution)/shard_map/ppermute | solution.py:396
  33.8 16.9 %collective-permute-start.12 = (f32[288,128]{1,0:T(8,128)S(1)}, f32[288,128]{1,0:T(8,128)S(1)}, u32[]{:S(2)}, u32[]{:S(2)}) collective-permute-start(f32[288,128]{1,0:T(8,128)S(1)} %bitcast.78), channel_id=1, source_target_pairs={{0,2},{1,3},{2,0},{3,1},{4,6},{5,7},{6,4},{7,5},{8,10},{9,11},{10,... | collective-permute-start | bytes 442376 | tf_op jit(solution)/shard_map/ppermute | solution.py:396
  35.8 14.9 %collective-permute-start.11 = (f32[288,128]{1,0:T(8,128)S(1)}, f32[288,128]{1,0:T(8,128)S(1)}, u32[]{:S(2)}, u32[]{:S(2)}) collective-permute-start(f32[288,128]{1,0:T(8,128)S(1)} %bitcast.80), channel_id=1, source_target_pairs={{0,1},{1,2},{2,3},{3,0},{4,5},{5,6},{6,7},{7,4},{8,9},{9,10},{10,1... | collective-permute-start | bytes 442376 | tf_op jit(solution)/shard_map/ppermute | solution.py:396
  41.2 9.5 %collective-permute-start.6 = (f32[288,128]{1,0:T(8,128)S(1)}, f32[288,128]{1,0:T(8,128)S(1)}, u32[]{:S(2)}, u32[]{:S(2)}) collective-permute-start(f32[288,128]{1,0:T(8,128)S(1)} %bitcast.82), channel_id=1, source_target_pairs={{0,3},{1,0},{2,1},{3,2},{4,7},{5,4},{6,5},{7,6},{8,11},{9,8},{10,9... | collective-permute-start | bytes 442376 | tf_op jit(solution)/shard_map/ppermute | solution.py:396
  45.2 6.7 %collective-permute-start.5 = (f32[288,128]{1,0:T(8,128)S(1)}, f32[288,128]{1,0:T(8,128)S(1)}, u32[]{:S(2)}, u32[]{:S(2)}) collective-permute-start(f32[288,128]{1,0:T(8,128)S(1)} %bitcast.84), channel_id=1, source_target_pairs={{0,2},{1,3},{2,0},{3,1},{4,6},{5,7},{6,4},{7,5},{8,10},{9,11},{10,... | collective-permute-start | bytes 442376 | tf_op jit(solution)/shard_map/ppermute | solution.py:396
  47.2 8.2 %collective-permute-start.4 = (f32[288,128]{1,0:T(8,128)S(1)}, f32[288,128]{1,0:T(8,128)S(1)}, u32[]{:S(2)}, u32[]{:S(2)}) collective-permute-start(f32[288,128]{1,0:T(8,128)S(1)} %bitcast.86), channel_id=1, source_target_pairs={{0,1},{1,2},{2,3},{3,0},{4,5},{5,6},{6,7},{7,4},{8,9},{9,10},{10,1... | collective-permute-start | bytes 442376 | tf_op jit(solution)/shard_map/ppermute | solution.py:396
  57.1 4.1 %collective-permute-start.14 = (f32[4,576,128]{2,1,0:T(8,128)S(1)}, f32[4,576,128]{2,1,0:T(8,128)S(1)}, u32[]{:S(2)}, u32[]{:S(2)}) collective-permute-start(f32[4,576,128]{2,1,0:T(8,128)S(1)} %get-tuple-element.11), channel_id=1, source_target_pairs={{0,32},{32,0},{64,96},{96,64},{128,160},{160,128},{192,224},{224,1... | collective-permute-start | bytes 3538952 | tf_op jit(solution)/shard_map/ppermute | solution.py:399
  61.4 16.9 %collective-permute-start.15 = (f32[576,128]{1,0:T(8,128)S(1)}, f32[576,128]{1,0:T(8,128)S(1)}, u32[]{:S(2)}, u32[]{:S(2)}) collective-permute-start(f32[576,128]{1,0:T(8,128)S(1)} %get-tuple-element.15), channel_id=1, source_target_pairs={{0,1},{1,2},{2,3},{3,0},{4,5},{5,6},{6,7},{7,4},{8,9},{9,10},{10,1... | collective-permute-start | bytes 884744 | tf_op jit(solution)/shard_map/ppermute | solution.py:396
  61.5 16.8 %collective-permute-start.16 = (f32[576,128]{1,0:T(8,128)S(1)}, f32[576,128]{1,0:T(8,128)S(1)}, u32[]{:S(2)}, u32[]{:S(2)}) collective-permute-start(f32[576,128]{1,0:T(8,128)S(1)} %get-tuple-element.17), channel_id=1, source_target_pairs={{0,2},{1,3},{2,0},{3,1},{4,6},{5,7},{6,4},{7,5},{8,10},{9,11},{10,... | collective-permute-start | bytes 884744 | tf_op jit(solution)/shard_map/ppermute | solution.py:396
  63.2 15.7 %collective-permute-start.17 = (f32[576,128]{1,0:T(8,128)S(1)}, f32[576,128]{1,0:T(8,128)S(1)}, u32[]{:S(2)}, u32[]{:S(2)}) collective-permute-start(f32[576,128]{1,0:T(8,128)S(1)} %get-tuple-element.16), channel_id=1, source_target_pairs={{0,3},{1,0},{2,1},{3,2},{4,7},{5,4},{6,5},{7,6},{8,11},{9,8},{10,9... | collective-permute-start | bytes 884744 | tf_op jit(solution)/shard_map/ppermute | solution.py:396
  79.0 64.3 %copy-start.3 = (f32[288,128]{1,0:T(8,128)S(1)}, f32[288,128]{1,0:T(8,128)}, u32[]{:S(2)}) copy-start(f32[288,128]{1,0:T(8,128)} %copy-done.2) | copy-start | bytes 442372
  79.0 64.3 %copy-start.5 = (f32[288,128]{1,0:T(8,128)S(1)}, f32[288,128]{1,0:T(8,128)}, u32[]{:S(2)}) copy-start(f32[288,128]{1,0:T(8,128)} %copy-done.4) | copy-start | bytes 442372
  79.0 64.2 %copy-start.7 = (f32[288,128]{1,0:T(8,128)S(1)}, f32[288,128]{1,0:T(8,128)}, u32[]{:S(2)}) copy-start(f32[288,128]{1,0:T(8,128)} %copy-done.6) | copy-start | bytes 442372
  79.0 64.2 %copy-start.9 = (f32[288,128]{1,0:T(8,128)S(1)}, f32[288,128]{1,0:T(8,128)}, u32[]{:S(2)}) copy-start(f32[288,128]{1,0:T(8,128)} %copy-done.8) | copy-start | bytes 442372
  126.0 10.8 %collective-permute-start.18 = (f32[576,128]{1,0:T(8,128)S(1)}, f32[576,128]{1,0:T(8,128)S(1)}, u32[]{:S(2)}, u32[]{:S(2)}) collective-permute-start(f32[576,128]{1,0:T(8,128)S(1)} %bitcast.71), channel_id=1, source_target_pairs={{0,1},{1,2},{2,3},{3,0},{4,5},{5,6},{6,7},{7,4},{8,9},{9,10},{10,1... | collective-permute-start | bytes 884744 | tf_op jit(solution)/shard_map/ppermute | solution.py:396
  128.1 13.2 %collective-permute-start.19 = (f32[576,128]{1,0:T(8,128)S(1)}, f32[576,128]{1,0:T(8,128)S(1)}, u32[]{:S(2)}, u32[]{:S(2)}) collective-permute-start(f32[576,128]{1,0:T(8,128)S(1)} %bitcast.72), channel_id=1, source_target_pairs={{0,2},{1,3},{2,0},{3,1},{4,6},{5,7},{6,4},{7,5},{8,10},{9,11},{10,... | collective-permute-start | bytes 884744 | tf_op jit(solution)/shard_map/ppermute | solution.py:396
  130.8 10.5 %collective-permute-start.20 = (f32[576,128]{1,0:T(8,128)S(1)}, f32[576,128]{1,0:T(8,128)S(1)}, u32[]{:S(2)}, u32[]{:S(2)}) collective-permute-start(f32[576,128]{1,0:T(8,128)S(1)} %bitcast.73), channel_id=1, source_target_pairs={{0,3},{1,0},{2,1},{3,2},{4,7},{5,4},{6,5},{7,6},{8,11},{9,8},{10,9... | collective-permute-start | bytes 884744 | tf_op jit(solution)/shard_map/ppermute | solution.py:396
  130.8 10.9 %collective-permute-start.21 = (f32[576,128]{1,0:T(8,128)S(1)}, f32[576,128]{1,0:T(8,128)S(1)}, u32[]{:S(2)}, u32[]{:S(2)}) collective-permute-start(f32[576,128]{1,0:T(8,128)S(1)} %bitcast.74), channel_id=1, source_target_pairs={{0,32},{32,0},{64,96},{96,64},{128,160},{160,128},{192,224},{224,1... | collective-permute-start | bytes 884744 | tf_op jit(solution)/shard_map/ppermute | solution.py:399
  136.8 5.0 %collective-permute-start.22 = (f32[576,128]{1,0:T(8,128)S(1)}, f32[576,128]{1,0:T(8,128)S(1)}, u32[]{:S(2)}, u32[]{:S(2)}) collective-permute-start(f32[576,128]{1,0:T(8,128)S(1)} %collective-permute-done.18.refs_1_), channel_id=1, source_target_pairs={{0,32},{32,0},{64,96},{96,64},{128,160},{160,128},{192,224},{224,1... | collective-permute-start | bytes 884744 | tf_op jit(solution)/shard_map/ppermute | solution.py:399
  141.2 1.6 collective-permute-start.23
  141.2 2.0 %collective-permute-start.24 = (f32[576,128]{1,0:T(8,128)S(1)}, f32[576,128]{1,0:T(8,128)S(1)}, u32[]{:S(2)}, u32[]{:S(2)}) collective-permute-start(f32[576,128]{1,0:T(8,128)S(1)} %collective-permute-done.20.refs_3_), channel_id=1, source_target_pairs={{0,32},{32,0},{64,96},{96,64},{128,160},{160,128},{192,224},{224,1... | collective-permute-start | bytes 884744 | tf_op jit(solution)/shard_map/ppermute | solution.py:399
  160.4 5.4 %collective-permute-start.25 = (f32[32,256]{1,0:T(8,128)S(1)}, f32[32,256]{1,0:T(8,128)S(1)}, u32[]{:S(2)}, u32[]{:S(2)}) collective-permute-start(f32[32,256]{1,0:T(8,128)S(1)} %get-tuple-element.12.refs_0_), channel_id=1, source_target_pairs={{0,1},{1,2},{2,3},{3,0},{4,5},{5,6},{6,7},{7,4},{8,9},{9,10},{10,1... | collective-permute-start | bytes 98312 | tf_op jit(solution)/shard_map/ppermute | solution.py:396
  161.4 5.4 %collective-permute-start.26 = (f32[32,256]{1,0:T(8,128)S(1)}, f32[32,256]{1,0:T(8,128)S(1)}, u32[]{:S(2)}, u32[]{:S(2)}) collective-permute-start(f32[32,256]{1,0:T(8,128)S(1)} %get-tuple-element.12.refs_0_), channel_id=1, source_target_pairs={{0,2},{1,3},{2,0},{3,1},{4,6},{5,7},{6,4},{7,5},{8,10},{9,11},{10,... | collective-permute-start | bytes 98312 | tf_op jit(solution)/shard_map/ppermute | solution.py:396
  163.7 3.9 %collective-permute-start.27 = (f32[32,256]{1,0:T(8,128)S(1)}, f32[32,256]{1,0:T(8,128)S(1)}, u32[]{:S(2)}, u32[]{:S(2)}) collective-permute-start(f32[32,256]{1,0:T(8,128)S(1)} %get-tuple-element.12.refs_0_), channel_id=1, source_target_pairs={{0,3},{1,0},{2,1},{3,2},{4,7},{5,4},{6,5},{7,6},{8,11},{9,8},{10,9... | collective-permute-start | bytes 98312 | tf_op jit(solution)/shard_map/ppermute | solution.py:396
  (21 other events, 431.1 us)
